TPU v7x, 256 devices: a whole 4x4x8 slice. The times are simulated.
256 devices in a mesh: rep: 128 (over x_hi, z, y, core), grp: 2 (over x_lo).
Axes of the slice: x: 4 (x_hi: 2, x_lo: 2; x = x_hi * 2 + x_lo), y: 4, z: 8, core: 2. Of those that a mesh axis runs over, the one named last changes fastest.
Arguments:
- local_params: bfloat16 [128, 2, 256, 8192], P('rep', 'grp'), may hold values from -130 to 130
- snapshot: bfloat16 [2, 256, 8192], P('grp'), may hold values from -4 to 4
- master: float32 [2, 256, 8192], P('grp', 'rep'), may hold values from -6 to 6
- momentum: float32 [2, 256, 8192], P('grp', 'rep'), may hold values from -4 to 4
Outputs:
- new_master: float32 [2, 256, 8192], P('grp', 'rep')
- new_momentum: float32 [2, 256, 8192], P('grp', 'rep')
- new_params: bfloat16 [2, 256, 8192], P('grp')
All inputs are finite; a program needn't handle non-finite values.
Results may differ from a plain program's by a relative error of at most 0.001.
Values may be sent and summed in bfloat16 or wider, within the bound.
No kernel may reach another device: no remote copies, remote signals or barrier semaphores. Data moves between devices by JAX's collectives and lax.ppermute only.
A program may use at most 128 MiB of HBM per device.

v0:
```python
import jax
import jax.numpy as jnp
from jax import lax
from jax.experimental import pallas as pl
from jax.experimental.pallas import tpu as pltpu
from jax.sharding import Mesh
from jax.sharding import PartitionSpec as P


REP = ("xh", "z", "y", "c")
ALL = ("xh", "z", "y", "c", "g")

nesterov_mu = 0.9
outer_rate = 0.7
clip_limit = 0.15
epsilon = 1e-06

SCALE = 16.0
WIDTH = 1024
MIB = 1024 * 1024
VMEM = pl.BlockSpec(memory_space=pltpu.VMEM)
SMEM = pl.BlockSpec(memory_space=pltpu.SMEM)
HBM = pl.BlockSpec(memory_space=pltpu.HBM)


def shift(axis, by):
    n = lax.axis_size(axis)
    return [(i, (i + by) % n) for i in range(n)]


def row_of(j, h, z, q, sign):
    ny, nz, nx = (lax.axis_size(a) for a in ("y", "z", "xh"))
    yd = (lax.axis_index("y") + sign * j) % ny
    xd = (lax.axis_index("xh") + h) % nx
    return ((xd * nz + z) * ny + yd) * 4 + q


def pick_kernel(core, local, out, sem):
    half = out.shape[1]
    begin = pl.multiple_of((1 - core[0]) * half, half)
    copy = pltpu.make_async_copy(local.at[:, pl.ds(begin, half)], out, sem)
    copy.start()
    copy.wait()


def pick(core, local):
    rows, cols = local.shape
    return pl.pallas_call(
        pick_kernel,
        in_specs=[SMEM, HBM],
        out_specs=VMEM,
        out_shape=jax.ShapeDtypeStruct((rows, cols // 2), local.dtype),
        scratch_shapes=[pltpu.SemaphoreType.DMA],
        compiler_params=pltpu.CompilerParams(vmem_limit_bytes=61 * MIB),
        name="pick",
    )(core, local)


def change_kernel(core, one, own, start, out, held, sems):
    _, half = out.shape
    copies = []
    for k in range(half // WIDTH):
        begin = pl.multiple_of(core[0] * half + k * WIDTH, WIDTH)
        for i, x in enumerate((own, start)):
            to = held.at[i, :, pl.ds(k * WIDTH, WIDTH)]
            copies.append(pltpu.make_async_copy(x.at[:, pl.ds(begin, WIDTH)], to, sems.at[i, k]))
    for copy in copies:
        copy.start()
    for k in range(half // WIDTH):
        copies[2 * k].wait()
        copies[2 * k + 1].wait()
        here = slice(k * WIDTH, (k + 1) * WIDTH)
        placed = [jnp.dot(one[...], held[i, :, here], preferred_element_type=jnp.float32) for i in range(2)]
        out[:, here] = 2.0 * placed[1] - placed[0]


def change(core, one, own, start):
    rows, cols = own.shape
    half = cols // 2
    return pl.pallas_call(
        change_kernel,
        in_specs=[SMEM, VMEM, HBM, HBM],
        out_specs=VMEM,
        out_shape=jax.ShapeDtypeStruct((rows, half), jnp.float32),
        scratch_shapes=[
            pltpu.VMEM((2, rows, half), own.dtype),
            pltpu.SemaphoreType.DMA((2, half // WIDTH)),
        ],
        compiler_params=pltpu.CompilerParams(vmem_limit_bytes=52 * MIB),
        name="change",
    )(core, one, own, start)


def to_blocks_kernel(one, own, other, *outs):
    *by_y, near, far = outs
    half, per = other.shape[1], by_y[0].shape[0]
    edge = by_y[0].shape[1]
    for at in range(0, half, WIDTH):
        here = slice(at, at + WIDTH)
        s = own[:, here] - jnp.dot(one[...], other[:, here], preferred_element_type=jnp.float32)
        for j in range(len(by_y)):
            block = s[j * per : (j + 1) * per]
            if at < edge:
                by_y[j][:, here] = block
            else:
                to = slice(j * per // 2, (j + 1) * per // 2), slice(at - edge, at - edge + WIDTH)
                near[to] = block[: per // 2]
                far[to] = block[per // 2 :]


def to_blocks(one, own, other, n):
    rows, half = other.shape
    shapes = [(rows // n, half // 2)] * n + [(rows // 2, half // 2)] * 2
    return pl.pallas_call(
        to_blocks_kernel,
        in_specs=[VMEM, VMEM, VMEM],
        out_specs=[VMEM] * len(shapes),
        out_shape=[jax.ShapeDtypeStruct(s, jnp.float32) for s in shapes],
        compiler_params=pltpu.CompilerParams(vmem_limit_bytes=6 * MIB),
        name="to_blocks",
    )(one, own, other)


def from_blocks_kernel(core, first, second, *refs):
    *ins, out = refs
    n = len(ins) // 2
    parts = ins[0].shape[1] // WIDTH
    side, k = pl.program_id(0), pl.program_id(1)

    def place(one, blocks, part):
        x = jnp.concatenate([b[:, part * WIDTH : (part + 1) * WIDTH] for b in blocks], axis=0)
        out[...] = jnp.dot(one[...], x, preferred_element_type=jnp.float32).astype(out.dtype)

    for s in range(2):
        mine = ins[s * n : (s + 1) * n]
        for part in range(parts):

            @pl.when((side == s) & (k == part))
            def _():
                place(first, mine[:-2], part)

            @pl.when((side == s) & (k == parts + part))
            def _():
                place(second, mine[-2:], part)


def from_blocks(core, first, second, mine, theirs):
    rows, width = first.shape[0], 4 * mine[0].shape[1]
    steps = width // 2 // WIDTH
    whole = pl.BlockSpec(memory_space=pltpu.VMEM)
    return pl.pallas_call(
        from_blocks_kernel,
        grid_spec=pltpu.PrefetchScalarGridSpec(
            num_scalar_prefetch=1,
            grid=(2, steps),
            in_specs=[whole] * (2 + len(mine) + len(theirs)),
            out_specs=pl.BlockSpec((rows, WIDTH), lambda s, k, core: (0, (core[0] + s) % 2 * steps + k)),
        ),
        out_shape=jax.ShapeDtypeStruct((rows, width), mine[0].dtype),
        compiler_params=pltpu.CompilerParams(vmem_limit_bytes=10 * MIB),
        name="from_blocks",
    )(core, first, second, *mine, *theirs)


def step(local_params, snapshot, master, momentum):
    replicas, ny, nz, nx = (lax.axis_size(a) for a in (REP, "y", "z", "xh"))
    core = lax.axis_index("c")
    core1 = core.astype(jnp.int32)[None]
    local, start = local_params[0, 0], snapshot[0]
    rows, cols = local.shape
    half = cols // 2
    edge = half // 2
    far_y = (2, 1, 3)
    wire = jnp.float16

    def send(x, axis, by):
        return lax.ppermute(x, axis, shift(axis, by))

    def wide(x):
        return x.astype(jnp.float32)

    other = send(pick(core1, local), "c", 1)
    o = jnp.arange(rows)
    q, z, h, j = o % 4, o // 4 % nz, o // (4 * nz) % nx, o // (4 * nz * nx)
    to = row_of(j, h, z, q, 1)[:, None] == o[None]
    z = (lax.axis_index("z") - z) % nz
    back_y = o[:, None] == row_of(j, h, z, q, -1)[None]
    j, h = o // (4 * nz) % ny, o // (4 * nz * ny)
    back_x = o[:, None] == row_of(j, h, z, q, -1)[None]

    to = jnp.where(to, SCALE, 0.0).astype(jnp.bfloat16)
    *by_y, near, far = to_blocks(to, change(core1, to, local, start), other, ny)
    far = far.astype(wire)
    by_y = [by_y[0]] + [x.astype(wire) for x in by_y[1:]]
    first, second = by_y[0], near
    second = second + wide(send(far, "xh", 1))
    for j in far_y:
        first = first + wide(send(by_y[j], "y", j))

    old, _ = lax.optimization_barrier(((master, momentum), (far, by_y[1:])))
    base = old[0][0] - outer_rate * nesterov_mu**2 * old[1][0]
    mine, theirs = (lax.dynamic_slice(base, (0, s * half), (2, half)) for s in (core, 1 - core))
    theirs = send(theirs, "c", 1)
    base = jnp.concatenate([jnp.where(core == 0, mine, theirs), jnp.where(core == 0, theirs, mine)], axis=0)
    base = lax.all_to_all(jnp.broadcast_to(base[None], (nz, 4, half)), "z", 0, 0, tiled=True)

    per = rows // (nx * ny)
    pieces = [second[j * per : (j + 1) * per] for j in range(ny)]
    second = pieces[0]
    far = send(first[per:].astype(wire), "xh", 1)
    for j in far_y:
        second = second + wide(send(pieces[j].astype(wire), "y", j))
    first = first[:per] + wide(far)

    total = jnp.concatenate([first, second], axis=1).astype(wire).reshape(nz, 4, half)
    base, total = lax.optimization_barrier((base, total))
    total = wide(lax.all_to_all(total, "z", 0, 0, tiled=True)).sum(axis=0)
    grad = total * (1.0 / (SCALE * replicas))
    grads = {k: send(grad, "z", k) for k in (4, 3, 5, 2, 6, 1, 7)}
    grads[0] = grad

    members = lax.axis_size(ALL)
    parts = lax.all_to_all(jnp.full((members, 1, 128), jnp.sum(grad * grad)), ALL, 0, 0, tiled=True)
    squares = jnp.sum(parts[:, 0, 0])
    elements = rows * cols * lax.axis_size("g")
    grad_rms = jnp.sqrt(squares / elements + epsilon)
    clip = jnp.minimum(1.0, clip_limit / grad_rms)

    mine = []
    for k in range(nz):
        there = lax.dynamic_index_in_dim(base, lax.rem(lax.axis_index("z") + (nz - k), nz), 0, keepdims=False)
        mine.append((there - outer_rate * (1.0 + nesterov_mu) * (clip * grads[k])).astype(jnp.bfloat16))
    mine = jnp.concatenate(mine, axis=0)
    first, second = mine[:, :edge], mine[:, edge:]
    arrived = {j: send(second, "y", j) for j in far_y}
    second = jnp.concatenate([second] + [arrived[j] for j in range(1, ny)], axis=0)
    first = jnp.concatenate([first, send(first, "xh", 1)], axis=0)
    arrived = {j: send(first, "y", j) for j in far_y}
    mine = [first] + [arrived[j] for j in range(1, ny)] + [second, send(second, "xh", 1)]
    theirs = [send(x, "c", 1) for x in mine]
    new_params = from_blocks(core1, back_y.astype(jnp.bfloat16), back_x.astype(jnp.bfloat16), mine, theirs)

    other = send(lax.dynamic_slice(grad, (2 * (1 - core), 0), (2, half)), "c", 1)
    own = lax.dynamic_slice(grad, (2 * core, 0), (2, half))
    own = [jnp.where(core == 0, own, other), jnp.where(core == 0, other, own)]
    clipped = clip * jnp.concatenate(own, axis=1)[None]
    new_momentum = nesterov_mu * momentum + clipped
    new_master = master - outer_rate * (clipped + nesterov_mu * new_momentum)
    return (new_master, new_momentum, new_params[None])


def solution(mesh):
    finer = Mesh(mesh.devices.reshape(2, 8, 4, 2, mesh.shape["grp"]), ALL)
    in_specs = (
        P(REP, "g", None, None),
        P("g", None, None),
        P("g", REP, None),
        P("g", REP, None),
    )
    out_specs = (P("g", REP, None), P("g", REP, None), P("g", None, None))
    return jax.shard_map(step, mesh=finer, in_specs=in_specs, out_specs=out_specs, check_vma=False)
```

profile of v0, /device:TPU:1, one launch (start us, length us, event | category | flops | bytes accessed | tf_op | source)
XLA Modules:
  0.0 135.5 jit_solution(10839054250051513216)
XLA Ops:
  0.6 3.0 %pick.1 = bf16[256,4096]{1,0:T(8,128)(2,1)} custom-call(s32[1]{0:T(128)} %bitcast.core, bf16[256,8192]{1,0:T(8,128)(2,1)} %bitcast.45), custom_call_target="tpu_custom_call" | custom-call | tf_op jit(solution)/shard_map/pick/pallas_call | solution.py:48
  3.6 3.3 %collective-permute-start = (bf16[256,4096]{1,0:T(8,128)(2,1)}, bf16[256,4096]{1,0:T(8,128)(2,1)S(1)}, u32[]{:S(2)}, u32[]{:S(2)}) collective-permute-start(bf16[256,4096]{1,0:T(8,128)(2,1)} %pick.1), channel_id=1, source_target_pairs={{0,2},{2,0},{1,3},{3,1},{4,6},{6,4},{5,7},{7,5},{8,10},{10,8},{9,1... | collective-permute-start | bytes 6291464 | tf_op jit(solution)/shard_map/ppermute | solution.py:177
  7.0 5.1 %change.1.own = f32[256,4096]{1,0:T(8,128)} custom-call(s32[1]{0:T(128)} %bitcast.core, bf16[256,256]{1,0:T(8,128)(2,1)S(1)} %select_convert_fusion.one, bf16[256,8192]{1,0:T(8,128)(2,1)} %bitcast.46, bf16[256,8192]{1,0:T(8,128)(2,1)} %bitcast.47), custom_call_target="tpu_custom_call" | custom-call | tf_op jit(solution)/shard_map/change/pallas_call | solution.py:80
  12.1 2.2 %copy-done = f32[256,4096]{1,0:T(8,128)S(1)} copy-done((f32[256,4096]{1,0:T(8,128)S(1)}, f32[256,4096]{1,0:T(8,128)}, u32[]{:S(2)}) %copy-start) | copy-done | bytes 4194328
  15.0 0.8 copy-done.1
  16.2 1.3 collective-permute-start.2
  17.9 2.3 %collective-permute-start.4 = (f16[64,2048]{1,0:T(8,128)(2,1)S(1)}, f16[64,2048]{1,0:T(8,128)(2,1)}, u32[]{:S(2)}, u32[]{:S(2)}) collective-permute-start(f16[64,2048]{1,0:T(8,128)(2,1)S(1)} %convert_element_type.82), channel_id=1, source_target_pairs={{0,12},{4,0},{8,4},{12,8},{1,13},{5,1},{9,5},{13,9},{2,14},{6,2},{... | collective-permute-start | bytes 786440 | tf_op jit(solution)/shard_map/ppermute | solution.py:177
  20.2 2.7 %collective-permute-start.6 = (f16[128,2048]{1,0:T(8,128)(2,1)S(1)}, f16[128,2048]{1,0:T(8,128)(2,1)}, u32[]{:S(2)}, u32[]{:S(2)}) collective-permute-start(f16[128,2048]{1,0:T(8,128)(2,1)S(1)} %convert_element_type.79), channel_id=1, source_target_pairs={{0,128},{128,0},{1,129},{129,1},{2,130},{130,2},{3,131},{131,3},{4... | collective-permute-start | bytes 1572872 | tf_op jit(solution)/shard_map/ppermute | solution.py:177
  23.0 0.9 broadcast_in_dim.33
  23.9 8.2 %all-to-all-start = ((f32[8,4,4096]{2,1,0:T(4,128)}), f32[8,4,4096]{2,1,0:T(4,128)S(1)}, u32[]{:S(2)}, u32[]{:S(2)}) async-start(f32[8,4,4096]{2,1,0:T(4,128)} %broadcast_in_dim.33), calls=%async_computation | async-start | bytes 1048576 | tf_op jit(solution)/shard_map/all_to_all | solution.py:205
  32.1 1.2 convert_add_fusion.1
  34.1 1.2 fusion.30
  35.4 1.5 %collective-permute-start.7 = (f16[32,2048]{1,0:T(8,128)(2,1)S(1)}, f16[32,2048]{1,0:T(8,128)(2,1)S(1)}, u32[]{:S(2)}, u32[]{:S(2)}) collective-permute-start(f16[32,2048]{1,0:T(8,128)(2,1)S(1)} %get-tuple-element.35), channel_id=1, source_target_pairs={{0,8},{4,12},{8,0},{12,4},{1,9},{5,13},{9,1},{13,5},{2,10},{6,14},... | collective-permute-start | bytes 393224 | tf_op jit(solution)/shard_map/ppermute | solution.py:177
  36.9 1.9 %collective-permute-start.8 = (f16[32,2048]{1,0:T(8,128)(2,1)S(1)}, f16[32,2048]{1,0:T(8,128)(2,1)S(1)}, u32[]{:S(2)}, u32[]{:S(2)}) collective-permute-start(f16[32,2048]{1,0:T(8,128)(2,1)S(1)} %get-tuple-element.37), channel_id=1, source_target_pairs={{0,4},{4,8},{8,12},{12,0},{1,5},{5,9},{9,13},{13,1},{2,6},{6,10},{... | collective-permute-start | bytes 393224 | tf_op jit(solution)/shard_map/ppermute | solution.py:177
  39.7 1.5 %collective-permute-done.7 = f16[32,2048]{1,0:T(8,128)(2,1)S(1)} collective-permute-done((f16[32,2048]{1,0:T(8,128)(2,1)S(1)}, f16[32,2048]{1,0:T(8,128)(2,1)S(1)}, u32[]{:S(2)}, u32[]{:S(2)}) %collective-permute-start.7) | collective-permute-done | bytes 131104 | tf_op jit(solution)/shard_map/ppermute | solution.py:177
  41.1 1.8 %collective-permute-done.8 = f16[32,2048]{1,0:T(8,128)(2,1)S(1)} collective-permute-done((f16[32,2048]{1,0:T(8,128)(2,1)S(1)}, f16[32,2048]{1,0:T(8,128)(2,1)S(1)}, u32[]{:S(2)}, u32[]{:S(2)}) %collective-permute-start.8) | collective-permute-done | bytes 131104 | tf_op jit(solution)/shard_map/ppermute | solution.py:177
  42.9 1.6 %collective-permute-done.9 = f16[32,2048]{1,0:T(8,128)(2,1)S(1)} collective-permute-done((f16[32,2048]{1,0:T(8,128)(2,1)S(1)}, f16[32,2048]{1,0:T(8,128)(2,1)S(1)}, u32[]{:S(2)}, u32[]{:S(2)}) %collective-permute-start.9) | collective-permute-done | bytes 131104 | tf_op jit(solution)/shard_map/ppermute | solution.py:177
  44.6 0.9 pad_maximum_fusion.1
  45.5 2.6 %all-to-all-done = f32[8,4,4096]{2,1,0:T(4,128)S(1)} async-done(((f32[8,4,4096]{2,1,0:T(4,128)}), f32[8,4,4096]{2,1,0:T(4,128)S(1)}, u32[]{:S(2)}, u32[]{:S(2)}) %all-to-all-start) | async-done | bytes 524320 | tf_op jit(solution)/shard_map/all_to_all | solution.py:205
  48.1 5.6 %all-to-all-start.1 = ((f16[8,4,4096]{2,1,0:T(4,128)(2,1)}), f16[8,4,4096]{2,1,0:T(4,128)(2,1)S(1)}, u32[]{:S(2)}, u32[]{:S(2)}) async-start(f16[8,4,4096]{2,1,0:T(4,128)(2,1)} %pad_maximum_fusion.1), calls=%async_computation.1 | async-start | bytes 524288 | tf_op jit(solution)/shard_map/all_to_all | solution.py:217
  53.7 9.2 %all-to-all-done.1 = f16[8,4,4096]{2,1,0:T(4,128)(2,1)S(1)} async-done(((f16[8,4,4096]{2,1,0:T(4,128)(2,1)}), f16[8,4,4096]{2,1,0:T(4,128)(2,1)S(1)}, u32[]{:S(2)}, u32[]{:S(2)}) %all-to-all-start.1) | async-done | bytes 262176 | tf_op jit(solution)/shard_map/all_to_all | solution.py:217
  63.7 1.4 %broadcast_in_dim.34 = f32[256,1,128]{2,1,0:T(1,128)} broadcast(f32[]{:T(128)} %get-tuple-element.44), dimensions={} | broadcast | bytes 131076 | tf_op jit(solution)/shard_map/broadcast_in_dim | solution.py:223
  65.0 8.6 %all-to-all-start.2 = ((f32[256,1,128]{2,1,0:T(1,128)}), f32[256,1,128]{2,1,0:T(1,128)S(1)}, u32[]{:S(2)}, u32[]{:S(2)}) async-start(f32[256,1,128]{2,1,0:T(1,128)} %broadcast_in_dim.34), calls=%async_computation.2 | async-start | bytes 262144 | tf_op jit(solution)/shard_map/all_to_all | solution.py:223
  73.7 1.8 %collective-permute-start.11 = (f32[4,4096]{1,0:T(4,128)S(1)}, f32[4,4096]{1,0:T(4,128)S(1)}, u32[]{:S(2)}, u32[]{:S(2)}) collective-permute-start(f32[4,4096]{1,0:T(4,128)S(1)} %get-tuple-element.45), channel_id=1, source_target_pairs={{0,16},{16,32},{32,48},{48,64},{64,80},{80,96},{96,112},{112,0},{1... | collective-permute-start | bytes 196616 | tf_op jit(solution)/shard_map/ppermute | solution.py:177
  75.5 2.6 %collective-permute-start.12 = (f32[4,4096]{1,0:T(4,128)S(1)}, f32[4,4096]{1,0:T(4,128)S(1)}, u32[]{:S(2)}, u32[]{:S(2)}) collective-permute-start(f32[4,4096]{1,0:T(4,128)S(1)} %get-tuple-element.45), channel_id=1, source_target_pairs={{0,32},{16,48},{32,64},{48,80},{64,96},{80,112},{96,0},{112,16},{1... | collective-permute-start | bytes 196616 | tf_op jit(solution)/shard_map/ppermute | solution.py:177
  78.2 3.3 %collective-permute-start.13 = (f32[4,4096]{1,0:T(4,128)S(1)}, f32[4,4096]{1,0:T(4,128)S(1)}, u32[]{:S(2)}, u32[]{:S(2)}) collective-permute-start(f32[4,4096]{1,0:T(4,128)S(1)} %get-tuple-element.45), channel_id=1, source_target_pairs={{0,48},{16,64},{32,80},{48,96},{64,112},{80,0},{96,16},{112,32},{1... | collective-permute-start | bytes 196616 | tf_op jit(solution)/shard_map/ppermute | solution.py:177
  81.5 1.0 collective-permute-start.14
  82.5 3.7 %collective-permute-start.15 = (f32[4,4096]{1,0:T(4,128)S(1)}, f32[4,4096]{1,0:T(4,128)S(1)}, u32[]{:S(2)}, u32[]{:S(2)}) collective-permute-start(f32[4,4096]{1,0:T(4,128)S(1)} %get-tuple-element.45), channel_id=1, source_target_pairs={{0,80},{16,96},{32,112},{48,0},{64,16},{80,32},{96,48},{112,64},{1... | collective-permute-start | bytes 196616 | tf_op jit(solution)/shard_map/ppermute | solution.py:177
  86.3 2.8 %collective-permute-start.16 = (f32[4,4096]{1,0:T(4,128)S(1)}, f32[4,4096]{1,0:T(4,128)S(1)}, u32[]{:S(2)}, u32[]{:S(2)}) collective-permute-start(f32[4,4096]{1,0:T(4,128)S(1)} %get-tuple-element.45), channel_id=1, source_target_pairs={{0,96},{16,112},{32,0},{48,16},{64,32},{80,48},{96,64},{112,80},{1... | collective-permute-start | bytes 196616 | tf_op jit(solution)/shard_map/ppermute | solution.py:177
  89.0 0.9 collective-permute-start.17
  89.9 0.9 slice_reduce_fusion
  91.5 0.9 collective-permute-done.15
  92.4 3.9 %collective-permute-done.16 = f32[4,4096]{1,0:T(4,128)S(1)} collective-permute-done((f32[4,4096]{1,0:T(4,128)S(1)}, f32[4,4096]{1,0:T(4,128)S(1)}, u32[]{:S(2)}, u32[]{:S(2)}) %collective-permute-start.16) | collective-permute-done | bytes 65568 | tf_op jit(solution)/shard_map/ppermute | solution.py:177
  96.7 2.8 %collective-permute-start.18 = (bf16[32,2048]{1,0:T(8,128)(2,1)S(1)}, bf16[32,2048]{1,0:T(8,128)(2,1)S(1)}, u32[]{:S(2)}, u32[]{:S(2)}) collective-permute-start(bf16[32,2048]{1,0:T(8,128)(2,1)S(1)} %get-tuple-element.39), channel_id=1, source_target_pairs={{0,128},{128,0},{1,129},{129,1},{2,130},{130,2},{3,131},{131,3},{4... | collective-permute-start | bytes 393224 | tf_op jit(solution)/shard_map/ppermute | solution.py:177
  99.5 1.9 %collective-permute-start.10 = (f32[2,4096]{1,0:T(2,128)S(1)}, f32[2,4096]{1,0:T(2,128)S(1)}, u32[]{:S(2)}, u32[]{:S(2)}) collective-permute-start(f32[2,4096]{1,0:T(2,128)S(1)} %constant_dynamic-slice_fusion), channel_id=1, source_target_pairs={{0,2},{2,0},{1,3},{3,1},{4,6},{6,4},{5,7},{7,5},{8,10},{10,8},{9,1... | collective-permute-start | bytes 98312 | tf_op jit(solution)/shard_map/ppermute | solution.py:177
  101.4 1.2 collective-permute-start.22
  102.7 2.5 %collective-permute-start.23 = (bf16[32,2048]{1,0:T(8,128)(2,1)S(1)}, bf16[32,2048]{1,0:T(8,128)(2,1)S(1)}, u32[]{:S(2)}, u32[]{:S(2)}) collective-permute-start(bf16[32,2048]{1,0:T(8,128)(2,1)S(1)} %get-tuple-element.38), channel_id=1, source_target_pairs={{0,8},{4,12},{8,0},{12,4},{1,9},{5,13},{9,1},{13,5},{2,10},{6,14},... | collective-permute-start | bytes 393224 | tf_op jit(solution)/shard_map/ppermute | solution.py:177
  105.2 1.1 collective-permute-start.24
  106.8 0.8 collective-permute-done.22
  107.6 1.6 %collective-permute-start.20 = (bf16[64,2048]{1,0:T(8,128)(2,1)S(1)}, bf16[64,2048]{1,0:T(8,128)(2,1)S(1)}, u32[]{:S(2)}, u32[]{:S(2)}) collective-permute-start(bf16[64,2048]{1,0:T(8,128)(2,1)S(1)} %pad_maximum_fusion.2.refs_0_), channel_id=1, source_target_pairs={{0,8},{4,12},{8,0},{12,4},{1,9},{5,13},{9,1},{13,5},{2,10},{6,14},... | collective-permute-start | bytes 786440 | tf_op jit(solution)/shard_map/ppermute | solution.py:177
  109.2 2.3 %collective-permute-done.23 = bf16[32,2048]{1,0:T(8,128)(2,1)S(1)} collective-permute-done((bf16[32,2048]{1,0:T(8,128)(2,1)S(1)}, bf16[32,2048]{1,0:T(8,128)(2,1)S(1)}, u32[]{:S(2)}, u32[]{:S(2)}) %collective-permute-start.23) | collective-permute-done | bytes 131104 | tf_op jit(solution)/shard_map/ppermute | solution.py:177
  111.5 1.6 %collective-permute-start.26 = (bf16[64,2048]{1,0:T(8,128)(2,1)S(1)}, bf16[64,2048]{1,0:T(8,128)(2,1)S(1)}, u32[]{:S(2)}, u32[]{:S(2)}) collective-permute-start(bf16[64,2048]{1,0:T(8,128)(2,1)S(1)} %pad_maximum_fusion.2.refs_0_), channel_id=1, source_target_pairs={{0,2},{2,0},{1,3},{3,1},{4,6},{6,4},{5,7},{7,5},{8,10},{10,8},{9,1... | collective-permute-start | bytes 786440 | tf_op jit(solution)/shard_map/ppermute | solution.py:177
  113.5 4.5 %collective-permute-done.19.refs_1_ = bf16[64,2048]{1,0:T(8,128)(2,1)S(1)} collective-permute-done((bf16[64,2048]{1,0:T(8,128)(2,1)S(1)}, bf16[64,2048]{1,0:T(8,128)(2,1)S(1)}, u32[]{:S(2)}, u32[]{:S(2)}) %collective-permute-start.19) | collective-permute-done | bytes 262176 | tf_op jit(solution)/shard_map/ppermute | solution.py:177
  118.6 4.1 %collective-permute-done.20.refs_2_ = bf16[64,2048]{1,0:T(8,128)(2,1)S(1)} collective-permute-done((bf16[64,2048]{1,0:T(8,128)(2,1)S(1)}, bf16[64,2048]{1,0:T(8,128)(2,1)S(1)}, u32[]{:S(2)}, u32[]{:S(2)}) %collective-permute-start.20) | collective-permute-done | bytes 262176 | tf_op jit(solution)/shard_map/ppermute | solution.py:177
  122.8 0.9 collective-permute-start.27
  124.2 4.0 %collective-permute-done.25.refs_5_ = bf16[128,2048]{1,0:T(8,128)(2,1)S(1)} collective-permute-done((bf16[128,2048]{1,0:T(8,128)(2,1)S(1)}, bf16[128,2048]{1,0:T(8,128)(2,1)S(1)}, u32[]{:S(2)}, u32[]{:S(2)}) %collective-permute-start.25) | collective-permute-done | bytes 524320 | tf_op jit(solution)/shard_map/ppermute | solution.py:177
  128.2 0.9 collective-permute-start.31
  130.6 4.9 %from_blocks.1 = bf16[256,8192]{1,0:T(8,128)(2,1)} custom-call(s32[1]{0:T(128)} %bitcast.core, bf16[256,256]{1,0:T(8,128)(2,1)S(1)} %fusion.4.first, bf16[256,256]{1,0:T(8,128)(2,1)S(1)} %fusion.5.second, bf16[64,2048]{1,0:T(8,128)(2,1)S(1)} %pad_maximum_fusion.2.refs_0_, bf16[64,2048]{1,0:T(8,128)(2,1)S(1)} %collective-permute-done.19.refs_1_, ...), custom_call_target="tpu_custom_call" | custom-call | tf_op jit(solution)/shard_map/from_blocks/pallas_call | solution.py:151
  (71 shorter events, 8.2 us)
Async XLA Ops:
  3.6 8.5 %collective-permute-start = (bf16[256,4096]{1,0:T(8,128)(2,1)}, bf16[256,4096]{1,0:T(8,128)(2,1)S(1)}, u32[]{:S(2)}, u32[]{:S(2)}) collective-permute-start(bf16[256,4096]{1,0:T(8,128)(2,1)} %pick.1), channel_id=1, source_target_pairs={{0,2},{2,0},{1,3},{3,1},{4,6},{6,4},{5,7},{7,5},{8,10},{10,8},{9,1... | collective-permute-start | bytes 6291464 | tf_op jit(solution)/shard_map/ppermute | solution.py:177
  12.1 2.2 %copy-start = (f32[256,4096]{1,0:T(8,128)S(1)}, f32[256,4096]{1,0:T(8,128)}, u32[]{:S(2)}) copy-start(f32[256,4096]{1,0:T(8,128)} %change.1.own) | copy-start | bytes 12582916
  14.3 1.7 %copy-start.3 = (f32[1,2,8192]{2,1,0:T(2,128)S(1)}, f32[1,2,8192]{2,1,0:T(2,128)}, u32[]{:S(2)}) copy-start(f32[1,2,8192]{2,1,0:T(2,128)} %param.6) | copy-start | bytes 196612
  14.3 1.7 %copy-start.4 = (f32[1,2,8192]{2,1,0:T(2,128)S(1)}, f32[1,2,8192]{2,1,0:T(2,128)}, u32[]{:S(2)}) copy-start(f32[1,2,8192]{2,1,0:T(2,128)} %param.7) | copy-start | bytes 196612
  15.0 0.8 copy-start.1
  15.8 16.3 %copy-start.2 = (f32[64,2048]{1,0:T(8,128)S(1)}, f32[64,2048]{1,0:T(8,128)}, u32[]{:S(2)}) copy-start(f32[64,2048]{1,0:T(8,128)} %copy-done.1) | copy-start | bytes 1572868
  16.1 6.8 %collective-permute-start.1 = (f32[2,4096]{1,0:T(2,128)S(1)}, f32[2,4096]{1,0:T(2,128)S(1)}, u32[]{:S(2)}, u32[]{:S(2)}) collective-permute-start(f32[2,4096]{1,0:T(2,128)S(1)} %dynamic-slice_bitcast_fusion), channel_id=1, source_target_pairs={{0,2},{2,0},{1,3},{3,1},{4,6},{6,4},{5,7},{7,5},{8,10},{10,8},{9,1... | collective-permute-start | bytes 98312 | tf_op jit(solution)/shard_map/ppermute | solution.py:177
  16.2 15.9 %collective-permute-start.2 = (f16[64,2048]{1,0:T(8,128)(2,1)S(1)}, f16[64,2048]{1,0:T(8,128)(2,1)}, u32[]{:S(2)}, u32[]{:S(2)}) collective-permute-start(f16[64,2048]{1,0:T(8,128)(2,1)S(1)} %convert_element_type.81), channel_id=1, source_target_pairs={{0,8},{4,12},{8,0},{12,4},{1,9},{5,13},{9,1},{13,5},{2,10},{6,14},... | collective-permute-start | bytes 786440 | tf_op jit(solution)/shard_map/ppermute | solution.py:177
  17.5 14.6 %collective-permute-start.3 = (f16[64,2048]{1,0:T(8,128)(2,1)S(1)}, f16[64,2048]{1,0:T(8,128)(2,1)}, u32[]{:S(2)}, u32[]{:S(2)}) collective-permute-start(f16[64,2048]{1,0:T(8,128)(2,1)S(1)} %convert_element_type.80), channel_id=1, source_target_pairs={{0,4},{4,8},{8,12},{12,0},{1,5},{5,9},{9,13},{13,1},{2,6},{6,10},{... | collective-permute-start | bytes 786440 | tf_op jit(solution)/shard_map/ppermute | solution.py:177
  17.9 14.2 %collective-permute-start.4 = (f16[64,2048]{1,0:T(8,128)(2,1)S(1)}, f16[64,2048]{1,0:T(8,128)(2,1)}, u32[]{:S(2)}, u32[]{:S(2)}) collective-permute-start(f16[64,2048]{1,0:T(8,128)(2,1)S(1)} %convert_element_type.82), channel_id=1, source_target_pairs={{0,12},{4,0},{8,4},{12,8},{1,13},{5,1},{9,5},{13,9},{2,14},{6,2},{... | collective-permute-start | bytes 786440 | tf_op jit(solution)/shard_map/ppermute | solution.py:177
  20.2 14.0 %collective-permute-start.6 = (f16[128,2048]{1,0:T(8,128)(2,1)S(1)}, f16[128,2048]{1,0:T(8,128)(2,1)}, u32[]{:S(2)}, u32[]{:S(2)}) collective-permute-start(f16[128,2048]{1,0:T(8,128)(2,1)S(1)} %convert_element_type.79), channel_id=1, source_target_pairs={{0,128},{128,0},{1,129},{129,1},{2,130},{130,2},{3,131},{131,3},{4... | collective-permute-start | bytes 1572872 | tf_op jit(solution)/shard_map/ppermute | solution.py:177
  23.9 24.2 %all-to-all-start = ((f32[8,4,4096]{2,1,0:T(4,128)}), f32[8,4,4096]{2,1,0:T(4,128)S(1)}, u32[]{:S(2)}, u32[]{:S(2)}) async-start(f32[8,4,4096]{2,1,0:T(4,128)} %broadcast_in_dim.33), calls=%async_computation | async-start | bytes 1048576 | tf_op jit(solution)/shard_map/all_to_all | solution.py:205
  33.3 6.2 %collective-permute-start.5 = (f16[32,2048]{1,0:T(8,128)(2,1)S(1)}, f16[32,2048]{1,0:T(8,128)(2,1)S(1)}, u32[]{:S(2)}, u32[]{:S(2)}) collective-permute-start(f16[32,2048]{1,0:T(8,128)(2,1)S(1)} %slice_convert_fusion), channel_id=1, source_target_pairs={{0,128},{128,0},{1,129},{129,1},{2,130},{130,2},{3,131},{131,3},{4... | collective-permute-start | bytes 393224 | tf_op jit(solution)/shard_map/ppermute | solution.py:177
  35.4 5.7 %collective-permute-start.7 = (f16[32,2048]{1,0:T(8,128)(2,1)S(1)}, f16[32,2048]{1,0:T(8,128)(2,1)S(1)}, u32[]{:S(2)}, u32[]{:S(2)}) collective-permute-start(f16[32,2048]{1,0:T(8,128)(2,1)S(1)} %get-tuple-element.35), channel_id=1, source_target_pairs={{0,8},{4,12},{8,0},{12,4},{1,9},{5,13},{9,1},{13,5},{2,10},{6,14},... | collective-permute-start | bytes 393224 | tf_op jit(solution)/shard_map/ppermute | solution.py:177
  36.9 6.0 %collective-permute-start.8 = (f16[32,2048]{1,0:T(8,128)(2,1)S(1)}, f16[32,2048]{1,0:T(8,128)(2,1)S(1)}, u32[]{:S(2)}, u32[]{:S(2)}) collective-permute-start(f16[32,2048]{1,0:T(8,128)(2,1)S(1)} %get-tuple-element.37), channel_id=1, source_target_pairs={{0,4},{4,8},{8,12},{12,0},{1,5},{5,9},{9,13},{13,1},{2,6},{6,10},{... | collective-permute-start | bytes 393224 | tf_op jit(solution)/shard_map/ppermute | solution.py:177
  38.8 5.6 %collective-permute-start.9 = (f16[32,2048]{1,0:T(8,128)(2,1)S(1)}, f16[32,2048]{1,0:T(8,128)(2,1)S(1)}, u32[]{:S(2)}, u32[]{:S(2)}) collective-permute-start(f16[32,2048]{1,0:T(8,128)(2,1)S(1)} %get-tuple-element.36), channel_id=1, source_target_pairs={{0,12},{4,0},{8,4},{12,8},{1,13},{5,1},{9,5},{13,9},{2,14},{6,2},{... | collective-permute-start | bytes 393224 | tf_op jit(solution)/shard_map/ppermute | solution.py:177
  48.1 14.9 %all-to-all-start.1 = ((f16[8,4,4096]{2,1,0:T(4,128)(2,1)}), f16[8,4,4096]{2,1,0:T(4,128)(2,1)S(1)}, u32[]{:S(2)}, u32[]{:S(2)}) async-start(f16[8,4,4096]{2,1,0:T(4,128)(2,1)} %pad_maximum_fusion.1), calls=%async_computation.1 | async-start | bytes 524288 | tf_op jit(solution)/shard_map/all_to_all | solution.py:217
  65.0 24.9 %all-to-all-start.2 = ((f32[256,1,128]{2,1,0:T(1,128)}), f32[256,1,128]{2,1,0:T(1,128)S(1)}, u32[]{:S(2)}, u32[]{:S(2)}) async-start(f32[256,1,128]{2,1,0:T(1,128)} %broadcast_in_dim.34), calls=%async_computation.2 | async-start | bytes 262144 | tf_op jit(solution)/shard_map/all_to_all | solution.py:223
  73.7 12.6 %collective-permute-start.11 = (f32[4,4096]{1,0:T(4,128)S(1)}, f32[4,4096]{1,0:T(4,128)S(1)}, u32[]{:S(2)}, u32[]{:S(2)}) collective-permute-start(f32[4,4096]{1,0:T(4,128)S(1)} %get-tuple-element.45), channel_id=1, source_target_pairs={{0,16},{16,32},{32,48},{48,64},{64,80},{80,96},{96,112},{112,0},{1... | collective-permute-start | bytes 196616 | tf_op jit(solution)/shard_map/ppermute | solution.py:177
  75.5 13.5 %collective-permute-start.12 = (f32[4,4096]{1,0:T(4,128)S(1)}, f32[4,4096]{1,0:T(4,128)S(1)}, u32[]{:S(2)}, u32[]{:S(2)}) collective-permute-start(f32[4,4096]{1,0:T(4,128)S(1)} %get-tuple-element.45), channel_id=1, source_target_pairs={{0,32},{16,48},{32,64},{48,80},{64,96},{80,112},{96,0},{112,16},{1... | collective-permute-start | bytes 196616 | tf_op jit(solution)/shard_map/ppermute | solution.py:177
  78.2 13.3 %collective-permute-start.13 = (f32[4,4096]{1,0:T(4,128)S(1)}, f32[4,4096]{1,0:T(4,128)S(1)}, u32[]{:S(2)}, u32[]{:S(2)}) collective-permute-start(f32[4,4096]{1,0:T(4,128)S(1)} %get-tuple-element.45), channel_id=1, source_target_pairs={{0,48},{16,64},{32,80},{48,96},{64,112},{80,0},{96,16},{112,32},{1... | collective-permute-start | bytes 196616 | tf_op jit(solution)/shard_map/ppermute | solution.py:177
  81.5 10.0 %collective-permute-start.14 = (f32[4,4096]{1,0:T(4,128)S(1)}, f32[4,4096]{1,0:T(4,128)S(1)}, u32[]{:S(2)}, u32[]{:S(2)}) collective-permute-start(f32[4,4096]{1,0:T(4,128)S(1)} %get-tuple-element.45), channel_id=1, source_target_pairs={{0,64},{16,80},{32,96},{48,112},{64,0},{80,16},{96,32},{112,48},{1... | collective-permute-start | bytes 196616 | tf_op jit(solution)/shard_map/ppermute | solution.py:177
  82.5 9.9 %collective-permute-start.15 = (f32[4,4096]{1,0:T(4,128)S(1)}, f32[4,4096]{1,0:T(4,128)S(1)}, u32[]{:S(2)}, u32[]{:S(2)}) collective-permute-start(f32[4,4096]{1,0:T(4,128)S(1)} %get-tuple-element.45), channel_id=1, source_target_pairs={{0,80},{16,96},{32,112},{48,0},{64,16},{80,32},{96,48},{112,64},{1... | collective-permute-start | bytes 196616 | tf_op jit(solution)/shard_map/ppermute | solution.py:177
  86.3 10.0 %collective-permute-start.16 = (f32[4,4096]{1,0:T(4,128)S(1)}, f32[4,4096]{1,0:T(4,128)S(1)}, u32[]{:S(2)}, u32[]{:S(2)}) collective-permute-start(f32[4,4096]{1,0:T(4,128)S(1)} %get-tuple-element.45), channel_id=1, source_target_pairs={{0,96},{16,112},{32,0},{48,16},{64,32},{80,48},{96,64},{112,80},{1... | collective-permute-start | bytes 196616 | tf_op jit(solution)/shard_map/ppermute | solution.py:177
  89.0 7.3 %collective-permute-start.17 = (f32[4,4096]{1,0:T(4,128)S(1)}, f32[4,4096]{1,0:T(4,128)S(1)}, u32[]{:S(2)}, u32[]{:S(2)}) collective-permute-start(f32[4,4096]{1,0:T(4,128)S(1)} %get-tuple-element.45), channel_id=1, source_target_pairs={{0,112},{16,0},{32,16},{48,32},{64,48},{80,64},{96,80},{112,96},{1... | collective-permute-start | bytes 196616 | tf_op jit(solution)/shard_map/ppermute | solution.py:177
  96.7 9.6 %collective-permute-start.18 = (bf16[32,2048]{1,0:T(8,128)(2,1)S(1)}, bf16[32,2048]{1,0:T(8,128)(2,1)S(1)}, u32[]{:S(2)}, u32[]{:S(2)}) collective-permute-start(bf16[32,2048]{1,0:T(8,128)(2,1)S(1)} %get-tuple-element.39), channel_id=1, source_target_pairs={{0,128},{128,0},{1,129},{129,1},{2,130},{130,2},{3,131},{131,3},{4... | collective-permute-start | bytes 393224 | tf_op jit(solution)/shard_map/ppermute | solution.py:177
  99.5 13.6 %collective-permute-start.10 = (f32[2,4096]{1,0:T(2,128)S(1)}, f32[2,4096]{1,0:T(2,128)S(1)}, u32[]{:S(2)}, u32[]{:S(2)}) collective-permute-start(f32[2,4096]{1,0:T(2,128)S(1)} %constant_dynamic-slice_fusion), channel_id=1, source_target_pairs={{0,2},{2,0},{1,3},{3,1},{4,6},{6,4},{5,7},{7,5},{8,10},{10,8},{9,1... | collective-permute-start | bytes 98312 | tf_op jit(solution)/shard_map/ppermute | solution.py:177
  101.4 6.2 %collective-permute-start.22 = (bf16[32,2048]{1,0:T(8,128)(2,1)S(1)}, bf16[32,2048]{1,0:T(8,128)(2,1)S(1)}, u32[]{:S(2)}, u32[]{:S(2)}) collective-permute-start(bf16[32,2048]{1,0:T(8,128)(2,1)S(1)} %get-tuple-element.38), channel_id=1, source_target_pairs={{0,4},{4,8},{8,12},{12,0},{1,5},{5,9},{9,13},{13,1},{2,6},{6,10},{... | collective-permute-start | bytes 393224 | tf_op jit(solution)/shard_map/ppermute | solution.py:177
  102.7 8.8 %collective-permute-start.23 = (bf16[32,2048]{1,0:T(8,128)(2,1)S(1)}, bf16[32,2048]{1,0:T(8,128)(2,1)S(1)}, u32[]{:S(2)}, u32[]{:S(2)}) collective-permute-start(bf16[32,2048]{1,0:T(8,128)(2,1)S(1)} %get-tuple-element.38), channel_id=1, source_target_pairs={{0,8},{4,12},{8,0},{12,4},{1,9},{5,13},{9,1},{13,5},{2,10},{6,14},... | collective-permute-start | bytes 393224 | tf_op jit(solution)/shard_map/ppermute | solution.py:177
  105.2 6.3 %collective-permute-start.24 = (bf16[32,2048]{1,0:T(8,128)(2,1)S(1)}, bf16[32,2048]{1,0:T(8,128)(2,1)S(1)}, u32[]{:S(2)}, u32[]{:S(2)}) collective-permute-start(bf16[32,2048]{1,0:T(8,128)(2,1)S(1)} %get-tuple-element.38), channel_id=1, source_target_pairs={{0,12},{4,0},{8,4},{12,8},{1,13},{5,1},{9,5},{13,9},{2,14},{6,2},{... | collective-permute-start | bytes 393224 | tf_op jit(solution)/shard_map/ppermute | solution.py:177
  106.4 11.7 %collective-permute-start.19 = (bf16[64,2048]{1,0:T(8,128)(2,1)S(1)}, bf16[64,2048]{1,0:T(8,128)(2,1)S(1)}, u32[]{:S(2)}, u32[]{:S(2)}) collective-permute-start(bf16[64,2048]{1,0:T(8,128)(2,1)S(1)} %pad_maximum_fusion.2.refs_0_), channel_id=1, source_target_pairs={{0,4},{4,8},{8,12},{12,0},{1,5},{5,9},{9,13},{13,1},{2,6},{6,10},{... | collective-permute-start | bytes 786440 | tf_op jit(solution)/shard_map/ppermute | solution.py:177
  107.6 15.1 %collective-permute-start.20 = (bf16[64,2048]{1,0:T(8,128)(2,1)S(1)}, bf16[64,2048]{1,0:T(8,128)(2,1)S(1)}, u32[]{:S(2)}, u32[]{:S(2)}) collective-permute-start(bf16[64,2048]{1,0:T(8,128)(2,1)S(1)} %pad_maximum_fusion.2.refs_0_), channel_id=1, source_target_pairs={{0,8},{4,12},{8,0},{12,4},{1,9},{5,13},{9,1},{13,5},{2,10},{6,14},... | collective-permute-start | bytes 786440 | tf_op jit(solution)/shard_map/ppermute | solution.py:177
  111.5 12.2 %collective-permute-start.21 = (bf16[64,2048]{1,0:T(8,128)(2,1)S(1)}, bf16[64,2048]{1,0:T(8,128)(2,1)S(1)}, u32[]{:S(2)}, u32[]{:S(2)}) collective-permute-start(bf16[64,2048]{1,0:T(8,128)(2,1)S(1)} %pad_maximum_fusion.2.refs_0_), channel_id=1, source_target_pairs={{0,12},{4,0},{8,4},{12,8},{1,13},{5,1},{9,5},{13,9},{2,14},{6,2},{... | collective-permute-start | bytes 786440 | tf_op jit(solution)/shard_map/ppermute | solution.py:177
  111.5 12.2 %collective-permute-start.26 = (bf16[64,2048]{1,0:T(8,128)(2,1)S(1)}, bf16[64,2048]{1,0:T(8,128)(2,1)S(1)}, u32[]{:S(2)}, u32[]{:S(2)}) collective-permute-start(bf16[64,2048]{1,0:T(8,128)(2,1)S(1)} %pad_maximum_fusion.2.refs_0_), channel_id=1, source_target_pairs={{0,2},{2,0},{1,3},{3,1},{4,6},{6,4},{5,7},{7,5},{8,10},{10,8},{9,1... | collective-permute-start | bytes 786440 | tf_op jit(solution)/shard_map/ppermute | solution.py:177
  113.2 15.1 %collective-permute-start.25 = (bf16[128,2048]{1,0:T(8,128)(2,1)S(1)}, bf16[128,2048]{1,0:T(8,128)(2,1)S(1)}, u32[]{:S(2)}, u32[]{:S(2)}) collective-permute-start(bf16[128,2048]{1,0:T(8,128)(2,1)S(1)} %pad_maximum_fusion.refs_4_), channel_id=1, source_target_pairs={{0,128},{128,0},{1,129},{129,1},{2,130},{130,2},{3,131},{131,3},{4... | collective-permute-start | bytes 1572872 | tf_op jit(solution)/shard_map/ppermute | solution.py:177
  118.0 11.8 %collective-permute-start.30 = (bf16[128,2048]{1,0:T(8,128)(2,1)S(1)}, bf16[128,2048]{1,0:T(8,128)(2,1)S(1)}, u32[]{:S(2)}, u32[]{:S(2)}) collective-permute-start(bf16[128,2048]{1,0:T(8,128)(2,1)S(1)} %pad_maximum_fusion.refs_4_), channel_id=1, source_target_pairs={{0,2},{2,0},{1,3},{3,1},{4,6},{6,4},{5,7},{7,5},{8,10},{10,8},{9,1... | collective-permute-start | bytes 1572872 | tf_op jit(solution)/shard_map/ppermute | solution.py:177
  122.8 7.1 %collective-permute-start.27 = (bf16[64,2048]{1,0:T(8,128)(2,1)S(1)}, bf16[64,2048]{1,0:T(8,128)(2,1)S(1)}, u32[]{:S(2)}, u32[]{:S(2)}) collective-permute-start(bf16[64,2048]{1,0:T(8,128)(2,1)S(1)} %collective-permute-done.19.refs_1_), channel_id=1, source_target_pairs={{0,2},{2,0},{1,3},{3,1},{4,6},{6,4},{5,7},{7,5},{8,10},{10,8},{9,1... | collective-permute-start | bytes 786440 | tf_op jit(solution)/shard_map/ppermute | solution.py:177
  123.7 6.2 %collective-permute-start.28 = (bf16[64,2048]{1,0:T(8,128)(2,1)S(1)}, bf16[64,2048]{1,0:T(8,128)(2,1)S(1)}, u32[]{:S(2)}, u32[]{:S(2)}) collective-permute-start(bf16[64,2048]{1,0:T(8,128)(2,1)S(1)} %collective-permute-done.20.refs_2_), channel_id=1, source_target_pairs={{0,2},{2,0},{1,3},{3,1},{4,6},{6,4},{5,7},{7,5},{8,10},{10,8},{9,1... | collective-permute-start | bytes 786440 | tf_op jit(solution)/shard_map/ppermute | solution.py:177
  123.7 6.2 %collective-permute-start.29 = (bf16[64,2048]{1,0:T(8,128)(2,1)S(1)}, bf16[64,2048]{1,0:T(8,128)(2,1)S(1)}, u32[]{:S(2)}, u32[]{:S(2)}) collective-permute-start(bf16[64,2048]{1,0:T(8,128)(2,1)S(1)} %collective-permute-done.21.refs_3_), channel_id=1, source_target_pairs={{0,2},{2,0},{1,3},{3,1},{4,6},{6,4},{5,7},{7,5},{8,10},{10,8},{9,1... | collective-permute-start | bytes 786440 | tf_op jit(solution)/shard_map/ppermute | solution.py:177
  128.2 2.4 %collective-permute-start.31 = (bf16[128,2048]{1,0:T(8,128)(2,1)S(1)}, bf16[128,2048]{1,0:T(8,128)(2,1)S(1)}, u32[]{:S(2)}, u32[]{:S(2)}) collective-permute-start(bf16[128,2048]{1,0:T(8,128)(2,1)S(1)} %collective-permute-done.25.refs_5_), channel_id=1, source_target_pairs={{0,2},{2,0},{1,3},{3,1},{4,6},{6,4},{5,7},{7,5},{8,10},{10,8},{9,1... | collective-permute-start | bytes 1572872 | tf_op jit(solution)/shard_map/ppermute | solution.py:177
where the time goes:
time: 136 us
  starting transfers between devices  70.1 us (52%)
  waiting for transfers between devices  37.9 us (28%)
  Pallas kernels  13.6 us (10%)
  other arithmetic  6.53 us (5%)
  local copies, waits for them, and re-layouts  5.66 us (4%)
  between operations  1.7 us (1%)
    ppermute x32, starting transfers between devices, send(): return lax.ppermute(x, axis, shift(axis, by))  47.7 us
    ppermute x32, waiting for transfers between devices, send(): return lax.ppermute(x, axis, shift(axis, by))  26.1 us
    all_to_all x1, waiting for transfers between devices, step(): total = wide(lax.all_to_all(total, 'z', 0, 0, tiled=True)).sum(axis=0)  9.25 us
    all_to_all x1, starting transfers between devices, step(): lax.all_to_all(jnp.full((members, 1, 128), jnp.sum(grad * grad)), ALL, 0,...  8.6 us
    all_to_all x1, starting transfers between devices, step(): lax.all_to_all(jnp.broadcast_to(base[None], (nz, 4, half)), 'z', 0, 0, ti...  8.19 us
    all_to_all x1, starting transfers between devices, step(): total = wide(lax.all_to_all(total, 'z', 0, 0, tiled=True)).sum(axis=0)  5.59 us
    pallas_call x1, Pallas kernels, change(): pl.pallas_call(change_kernel, in_specs=[SMEM, VMEM, HBM, HBM], out_specs=...  5.06 us
    pallas_call x1, Pallas kernels, from_blocks(): pl.pallas_call(from_blocks_kernel, grid_spec=pltpu.PrefetchScalarGridSpec...  4.88 us
  transfers between devices with their start and end apart: 35, of which 13 were waited for; matrix products, arithmetic and copies ran while one was open for 5% of the time, Pallas kernels for 4%

commit v1 on v0

--- a/solution.py
+++ b/solution.py
@@ -51,7 +51,7 @@
         out_specs=VMEM,
         out_shape=jax.ShapeDtypeStruct((rows, cols // 2), local.dtype),
         scratch_shapes=[pltpu.SemaphoreType.DMA],
-        compiler_params=pltpu.CompilerParams(vmem_limit_bytes=61 * MIB),
+        compiler_params=pltpu.CompilerParams(vmem_limit_bytes=59 * MIB),
         name="pick",
     )(core, local)
 
@@ -86,7 +86,7 @@
             pltpu.VMEM((2, rows, half), own.dtype),
             pltpu.SemaphoreType.DMA((2, half // WIDTH)),
         ],
-        compiler_params=pltpu.CompilerParams(vmem_limit_bytes=52 * MIB),
+        compiler_params=pltpu.CompilerParams(vmem_limit_bytes=49 * MIB),
         name="change",
     )(core, one, own, start)
 
@@ -121,45 +121,41 @@
     )(one, own, other)
 
 
-def from_blocks_kernel(core, first, second, *refs):
-    *ins, out = refs
-    n = len(ins) // 2
-    parts = ins[0].shape[1] // WIDTH
+def from_blocks_kernel(core, one, *refs):
+    out = refs[-1]
+    n = (len(refs) - 1) // 2
+    ins = refs[: 2 * n]
     side, k = pl.program_id(0), pl.program_id(1)
-
-    def place(one, blocks, part):
-        x = jnp.concatenate([b[:, part * WIDTH : (part + 1) * WIDTH] for b in blocks], axis=0)
-        out[...] = jnp.dot(one[...], x, preferred_element_type=jnp.float32).astype(out.dtype)
-
     for s in range(2):
-        mine = ins[s * n : (s + 1) * n]
-        for part in range(parts):
+        for part in range(ins[0].shape[1] // WIDTH):
 
             @pl.when((side == s) & (k == part))
             def _():
-                place(first, mine[:-2], part)
-
-            @pl.when((side == s) & (k == parts + part))
-            def _():
-                place(second, mine[-2:], part)
-
-
-def from_blocks(core, first, second, mine, theirs):
-    rows, width = first.shape[0], 4 * mine[0].shape[1]
-    steps = width // 2 // WIDTH
-    whole = pl.BlockSpec(memory_space=pltpu.VMEM)
+                blocks = [b[:, part * WIDTH : (part + 1) * WIDTH] for b in ins[s * n : (s + 1) * n]]
+                x = jnp.concatenate(blocks, axis=0)
+                out[...] = jnp.dot(one[...], x, preferred_element_type=jnp.float32).astype(out.dtype)
+
+
+def from_blocks(core, one, mine, theirs, quarter, out=None):
+    rows, width = one.shape[0], 4 * mine[0].shape[1]
+    steps = mine[0].shape[1] // WIDTH
+    blocks = [*mine, *theirs]
+    rest = [] if out is None else [out]
     return pl.pallas_call(
         from_blocks_kernel,
         grid_spec=pltpu.PrefetchScalarGridSpec(
             num_scalar_prefetch=1,
             grid=(2, steps),
-            in_specs=[whole] * (2 + len(mine) + len(theirs)),
-            out_specs=pl.BlockSpec((rows, WIDTH), lambda s, k, core: (0, (core[0] + s) % 2 * steps + k)),
+            in_specs=[VMEM] * (1 + len(blocks)) + [HBM] * len(rest),
+            out_specs=pl.BlockSpec(
+                (rows, WIDTH), lambda s, k, core: (0, ((core[0] + s) % 2 * 2 + quarter) * steps + k)
+            ),
         ),
         out_shape=jax.ShapeDtypeStruct((rows, width), mine[0].dtype),
+        input_output_aliases={2 + len(blocks): 0} if rest else {},
         compiler_params=pltpu.CompilerParams(vmem_limit_bytes=10 * MIB),
         name="from_blocks",
-    )(core, first, second, *mine, *theirs)
+    )(core, one, *blocks, *rest)
 
 
 def step(local_params, snapshot, master, momentum):
@@ -176,10 +172,12 @@
     def send(x, axis, by):
         return lax.ppermute(x, axis, shift(axis, by))
 
+    def part(x, row, col):
+        return lax.dynamic_slice(x, (row, col), (2, half), allow_negative_indices=False)
+
     def wide(x):
         return x.astype(jnp.float32)
 
-    other = send(pick(core1, local), "c", 1)
     o = jnp.arange(rows)
     q, z, h, j = o % 4, o // 4 % nz, o // (4 * nz) % nx, o // (4 * nz * nx)
     to = row_of(j, h, z, q, 1)[:, None] == o[None]
@@ -189,20 +187,22 @@
     back_x = o[:, None] == row_of(j, h, z, q, -1)[None]
 
     to = jnp.where(to, SCALE, 0.0).astype(jnp.bfloat16)
+    at = (core * half, (1 - core) * half, 2 * core, 2 * (1 - core))
+    local, start, to, at, core1 = lax.optimization_barrier((local, start, to, at, core1))
+    other = send(pick(core1, local), "c", 1)
     *by_y, near, far = to_blocks(to, change(core1, to, local, start), other, ny)
-    far = far.astype(wire)
-    by_y = [by_y[0]] + [x.astype(wire) for x in by_y[1:]]
-    first, second = by_y[0], near
+    far, near = far.astype(wire), near.astype(wire)
+    by_y = [x.astype(wire) for x in by_y]
+    first, second = wide(by_y[0]), wide(near)
     second = second + wide(send(far, "xh", 1))
     for j in far_y:
         first = first + wide(send(by_y[j], "y", j))
 
     old, _ = lax.optimization_barrier(((master, momentum), (far, by_y[1:])))
     base = old[0][0] - outer_rate * nesterov_mu**2 * old[1][0]
-    mine, theirs = (lax.dynamic_slice(base, (0, s * half), (2, half)) for s in (core, 1 - core))
+    mine, theirs = part(base, 0, at[0]), part(base, 0, at[1])
     theirs = send(theirs, "c", 1)
     base = jnp.concatenate([jnp.where(core == 0, mine, theirs), jnp.where(core == 0, theirs, mine)], axis=0)
-    base = lax.all_to_all(jnp.broadcast_to(base[None], (nz, 4, half)), "z", 0, 0, tiled=True)
 
     per = rows // (nx * ny)
     pieces = [second[j * per : (j + 1) * per] for j in range(ny)]
@@ -216,8 +216,10 @@
     base, total = lax.optimization_barrier((base, total))
     total = wide(lax.all_to_all(total, "z", 0, 0, tiled=True)).sum(axis=0)
     grad = total * (1.0 / (SCALE * replicas))
-    grads = {k: send(grad, "z", k) for k in (4, 3, 5, 2, 6, 1, 7)}
-    grads[0] = grad
+    grad = lax.optimization_barrier(grad)
+    pair = lax.optimization_barrier(jnp.concatenate([base, grad], axis=1))
+    pairs = {k: send(pair, "z", k) for k in (4, 3, 5, 2, 6, 1, 7)}
+    pairs[0] = pair
 
     members = lax.axis_size(ALL)
     parts = lax.all_to_all(jnp.full((members, 1, 128), jnp.sum(grad * grad)), ALL, 0, 0, tiled=True)
@@ -226,22 +228,24 @@
     grad_rms = jnp.sqrt(squares / elements + epsilon)
     clip = jnp.minimum(1.0, clip_limit / grad_rms)
 
-    mine = []
-    for k in range(nz):
-        there = lax.dynamic_index_in_dim(base, lax.rem(lax.axis_index("z") + (nz - k), nz), 0, keepdims=False)
-        mine.append((there - outer_rate * (1.0 + nesterov_mu) * (clip * grads[k])).astype(jnp.bfloat16))
+    pairs = [pairs[k] for k in range(nz)]
+    mine = [x[:, :half] - outer_rate * (1.0 + nesterov_mu) * (clip * x[:, half:]) for x in pairs]
+    mine = [x.astype(jnp.bfloat16) for x in mine]
     mine = jnp.concatenate(mine, axis=0)
     first, second = mine[:, :edge], mine[:, edge:]
     arrived = {j: send(second, "y", j) for j in far_y}
     second = jnp.concatenate([second] + [arrived[j] for j in range(1, ny)], axis=0)
     first = jnp.concatenate([first, send(first, "xh", 1)], axis=0)
     arrived = {j: send(first, "y", j) for j in far_y}
-    mine = [first] + [arrived[j] for j in range(1, ny)] + [second, send(second, "xh", 1)]
+    mine = [first] + [arrived[j] for j in range(1, ny)]
     theirs = [send(x, "c", 1) for x in mine]
-    new_params = from_blocks(core1, back_y.astype(jnp.bfloat16), back_x.astype(jnp.bfloat16), mine, theirs)
-
-    other = send(lax.dynamic_slice(grad, (2 * (1 - core), 0), (2, half)), "c", 1)
-    own = lax.dynamic_slice(grad, (2 * core, 0), (2, half))
+    new_params = from_blocks(core1, back_y.astype(jnp.bfloat16), mine, theirs, 0)
+    mine = [second, send(second, "xh", 1)]
+    theirs = [send(x, "c", 1) for x in mine]
+    new_params = from_blocks(core1, back_x.astype(jnp.bfloat16), mine, theirs, 1, new_params)
+
+    other = send(part(grad, at[3], 0), "c", 1)
+    own = part(grad, at[2], 0)
     own = [jnp.where(core == 0, own, other), jnp.where(core == 0, other, own)]
     clipped = clip * jnp.concatenate(own, axis=1)[None]
     new_momentum = nesterov_mu * momentum + clipped

time: 136 us -> 143 us (1.051)
  waiting for transfers between devices: 37.9 us -> 59.1 us
  starting transfers between devices: 70.1 us -> 61.8 us
  local copies, waits for them, and re-layouts: 5.66 us -> 2.51 us
  Pallas kernels: 13.6 us -> 11.9 us
    ppermute x32, waiting for transfers between devices: 26.1 us -> 48.1 us  [send(): return lax.ppermute(x, axis, shift(axis, by))]
    all_to_all x1 -> x0, starting transfers between devices: 8.19 us -> none  [step(): lax.all_to_all(jnp.broadcast_to(base[None], (nz, 4, half)), 'z', 0, 0, ti...]
    ppermute x32, starting transfers between devices: 47.7 us -> 44.9 us  [send(): return lax.ppermute(x, axis, shift(axis, by))]
    all_to_all x1 -> x0, waiting for transfers between devices: 2.6 us -> none  [step(): lax.all_to_all(jnp.broadcast_to(base[None], (nz, 4, half)), 'z', 0, 0, ti...]
    all_to_all x1, starting transfers between devices: 5.59 us -> 8.19 us  [step(): total = wide(lax.all_to_all(total, 'z', 0, 0, tiled=True)).sum(axis=0)]
    unnamed x10 -> x6, local copies, waits for them, and re-layouts: 2.98 us -> 0.62 us
    pallas_call x1, Pallas kernels: 5.06 us -> 3.05 us  [change(): pl.pallas_call(change_kernel, in_specs=[SMEM, VMEM, HBM, HBM], out_specs=...]
    all_to_all x1, waiting for transfers between devices: 0.01 us -> 1.92 us  [step(): lax.all_to_all(jnp.full((members, 1, 128), jnp.sum(grad * grad)), ALL, 0,...]
  transfers between devices with their start and end apart: 35 -> 34, of which waited for: 13 -> 19; matrix products, arithmetic and copies ran while one was open for 5% -> 3% of each run, Pallas kernels for 4% -> 4%
where the time goes in v1:
time: 143 us
  starting transfers between devices  61.8 us (43%)
  waiting for transfers between devices  59.1 us (41%)
  Pallas kernels  11.9 us (8%)
  other arithmetic  5.59 us (4%)
  local copies, waits for them, and re-layouts  2.51 us (2%)
  between operations  1.67 us (1%)
    ppermute x32, waiting for transfers between devices, send(): return lax.ppermute(x, axis, shift(axis, by))  48.1 us
    ppermute x32, starting transfers between devices, send(): return lax.ppermute(x, axis, shift(axis, by))  44.9 us
    all_to_all x1, waiting for transfers between devices, step(): total = wide(lax.all_to_all(total, 'z', 0, 0, tiled=True)).sum(axis=0)  9.18 us
    all_to_all x1, starting transfers between devices, step(): lax.all_to_all(jnp.full((members, 1, 128), jnp.sum(grad * grad)), ALL, 0,...  8.64 us
    all_to_all x1, starting transfers between devices, step(): total = wide(lax.all_to_all(total, 'z', 0, 0, tiled=True)).sum(axis=0)  8.19 us
    pallas_call x2, Pallas kernels, from_blocks(): pl.pallas_call(from_blocks_kernel, grid_spec=pltpu.PrefetchScalarGridSpec...  5.25 us
    pallas_call x1, Pallas kernels, change(): pl.pallas_call(change_kernel, in_specs=[SMEM, VMEM, HBM, HBM], out_specs=...  3.05 us
    pallas_call x1, Pallas kernels, pick(): pl.pallas_call(pick_kernel, in_specs=[SMEM, HBM], out_specs=VMEM, out_sha...  2.92 us
  transfers between devices with their start and end apart: 34, of which 19 were waited for; matrix products, arithmetic and copies ran while one was open for 3% of the time, Pallas kernels for 4%

profile of v1, /device:TPU:1, one launch (start us, length us, event | category | flops | bytes accessed | tf_op | source)
XLA Modules:
  0.0 142.6 jit_solution(3041645583844567956)
XLA Ops:
  0.8 2.9 %pick.1 = bf16[256,4096]{1,0:T(8,128)(2,1)} custom-call(s32[1]{0:T(128)} %bitcast.2.core, bf16[256,8192]{1,0:T(8,128)(2,1)} %bitcast.13), custom_call_target="tpu_custom_call" | custom-call | tf_op jit(solution)/shard_map/pick/pallas_call | solution.py:48
  3.7 3.3 %collective-permute-start = (bf16[256,4096]{1,0:T(8,128)(2,1)}, bf16[256,4096]{1,0:T(8,128)(2,1)S(1)}, u32[]{:S(2)}, u32[]{:S(2)}) collective-permute-start(bf16[256,4096]{1,0:T(8,128)(2,1)} %pick.1), channel_id=1, source_target_pairs={{0,2},{2,0},{1,3},{3,1},{4,6},{6,4},{5,7},{7,5},{8,10},{10,8},{9,1... | collective-permute-start | bytes 6291464 | tf_op jit(solution)/shard_map/ppermute | solution.py:173
  7.0 3.0 %change.1.own = f32[256,4096]{1,0:T(8,128)S(1)} custom-call(s32[1]{0:T(128)} %bitcast.2.core, bf16[256,256]{1,0:T(8,128)(2,1)S(1)} %select_convert_fusion.one, bf16[256,8192]{1,0:T(8,128)(2,1)} %bitcast.14, bf16[256,8192]{1,0:T(8,128)(2,1)} %bitcast.16), custom_call_target="tpu_custom_call" | custom-call | tf_op jit(solution)/shard_map/change/pallas_call | solution.py:80
  10.1 0.9 collective-permute-done.other
  13.1 1.3 collective-permute-start.2
  14.8 2.3 %collective-permute-start.4 = (f16[64,2048]{1,0:T(8,128)(2,1)S(1)}, f16[64,2048]{1,0:T(8,128)(2,1)S(1)}, u32[]{:S(2)}, u32[]{:S(2)}) collective-permute-start(f16[64,2048]{1,0:T(8,128)(2,1)S(1)} %convert_element_type.94), channel_id=1, source_target_pairs={{0,12},{4,0},{8,4},{12,8},{1,13},{5,1},{9,5},{13,9},{2,14},{6,2},{... | collective-permute-start | bytes 786440 | tf_op jit(solution)/shard_map/ppermute | solution.py:173
  17.1 2.7 %collective-permute-start.6 = (f16[128,2048]{1,0:T(8,128)(2,1)S(1)}, f16[128,2048]{1,0:T(8,128)(2,1)S(1)}, u32[]{:S(2)}, u32[]{:S(2)}) collective-permute-start(f16[128,2048]{1,0:T(8,128)(2,1)S(1)} %convert_element_type.91), channel_id=1, source_target_pairs={{0,128},{128,0},{1,129},{129,1},{2,130},{130,2},{3,131},{131,3},{4... | collective-permute-start | bytes 1572872 | tf_op jit(solution)/shard_map/ppermute | solution.py:173
  20.0 2.5 %collective-permute-done.2 = f16[64,2048]{1,0:T(8,128)(2,1)S(1)} collective-permute-done((f16[64,2048]{1,0:T(8,128)(2,1)S(1)}, f16[64,2048]{1,0:T(8,128)(2,1)S(1)}, u32[]{:S(2)}, u32[]{:S(2)}) %collective-permute-start.2) | collective-permute-done | bytes 262176 | tf_op jit(solution)/shard_map/ppermute | solution.py:173
  22.5 6.1 %collective-permute-done.3 = f16[64,2048]{1,0:T(8,128)(2,1)S(1)} collective-permute-done((f16[64,2048]{1,0:T(8,128)(2,1)S(1)}, f16[64,2048]{1,0:T(8,128)(2,1)S(1)}, u32[]{:S(2)}, u32[]{:S(2)}) %collective-permute-start.3) | collective-permute-done | bytes 262176 | tf_op jit(solution)/shard_map/ppermute | solution.py:173
  28.6 1.2 convert_add_fusion.1
  29.8 1.1 collective-permute-start.5
  31.4 1.5 %collective-permute-start.7 = (f16[32,2048]{1,0:T(8,128)(2,1)S(1)}, f16[32,2048]{1,0:T(8,128)(2,1)S(1)}, u32[]{:S(2)}, u32[]{:S(2)}) collective-permute-start(f16[32,2048]{1,0:T(8,128)(2,1)S(1)} %get-tuple-element.43), channel_id=1, source_target_pairs={{0,8},{4,12},{8,0},{12,4},{1,9},{5,13},{9,1},{13,5},{2,10},{6,14},... | collective-permute-start | bytes 393224 | tf_op jit(solution)/shard_map/ppermute | solution.py:173
  32.9 1.7 %collective-permute-start.8 = (f16[32,2048]{1,0:T(8,128)(2,1)S(1)}, f16[32,2048]{1,0:T(8,128)(2,1)S(1)}, u32[]{:S(2)}, u32[]{:S(2)}) collective-permute-start(f16[32,2048]{1,0:T(8,128)(2,1)S(1)} %get-tuple-element.45), channel_id=1, source_target_pairs={{0,4},{4,8},{8,12},{12,0},{1,5},{5,9},{9,13},{13,1},{2,6},{6,10},{... | collective-permute-start | bytes 393224 | tf_op jit(solution)/shard_map/ppermute | solution.py:173
  34.6 1.0 collective-permute-start.9
  36.1 0.8 collective-permute-done.7
  36.9 2.3 %collective-permute-done.8 = f16[32,2048]{1,0:T(8,128)(2,1)S(1)} collective-permute-done((f16[32,2048]{1,0:T(8,128)(2,1)S(1)}, f16[32,2048]{1,0:T(8,128)(2,1)S(1)}, u32[]{:S(2)}, u32[]{:S(2)}) %collective-permute-start.8) | collective-permute-done | bytes 131104 | tf_op jit(solution)/shard_map/ppermute | solution.py:173
  39.2 1.0 collective-permute-done.9
  40.3 0.9 pad_maximum_fusion.1
  41.2 8.2 %all-to-all-start = ((f16[8,4,4096]{2,1,0:T(4,128)(2,1)}), f16[8,4,4096]{2,1,0:T(4,128)(2,1)S(1)}, u32[]{:S(2)}, u32[]{:S(2)}) async-start(f16[8,4,4096]{2,1,0:T(4,128)(2,1)} %pad_maximum_fusion.1), calls=%async_computation | async-start | bytes 524288 | tf_op jit(solution)/shard_map/all_to_all | solution.py:217
  49.5 9.2 %all-to-all-done = f16[8,4,4096]{2,1,0:T(4,128)(2,1)S(1)} async-done(((f16[8,4,4096]{2,1,0:T(4,128)(2,1)}), f16[8,4,4096]{2,1,0:T(4,128)(2,1)S(1)}, u32[]{:S(2)}, u32[]{:S(2)}) %all-to-all-start) | async-done | bytes 262176 | tf_op jit(solution)/shard_map/all_to_all | solution.py:217
  59.4 1.4 broadcast_in_dim.27
  60.8 8.6 %all-to-all-start.1 = ((f32[256,1,128]{2,1,0:T(1,128)}), f32[256,1,128]{2,1,0:T(1,128)S(1)}, u32[]{:S(2)}, u32[]{:S(2)}) async-start(f32[256,1,128]{2,1,0:T(1,128)} %broadcast_in_dim.27), calls=%async_computation.1 | async-start | bytes 262144 | tf_op jit(solution)/shard_map/all_to_all | solution.py:225
  69.5 4.6 %collective-permute-start.17 = (f32[4,8192]{1,0:T(4,128)S(1)}, f32[4,8192]{1,0:T(4,128)S(1)}, u32[]{:S(2)}, u32[]{:S(2)}) collective-permute-start(f32[4,8192]{1,0:T(4,128)S(1)} %pad_maximum_fusion.3), channel_id=1, source_target_pairs={{0,112},{16,0},{32,16},{48,32},{64,48},{80,64},{96,80},{112,96},{1... | collective-permute-start | bytes 393224 | tf_op jit(solution)/shard_map/ppermute | solution.py:173
  74.1 1.5 %collective-permute-start.16 = (f32[4,8192]{1,0:T(4,128)S(1)}, f32[4,8192]{1,0:T(4,128)S(1)}, u32[]{:S(2)}, u32[]{:S(2)}) collective-permute-start(f32[4,8192]{1,0:T(4,128)S(1)} %pad_maximum_fusion.3), channel_id=1, source_target_pairs={{0,96},{16,112},{32,0},{48,16},{64,32},{80,48},{96,64},{112,80},{1... | collective-permute-start | bytes 393224 | tf_op jit(solution)/shard_map/ppermute | solution.py:173
  76.3 4.1 %collective-permute-start.14 = (f32[4,8192]{1,0:T(4,128)S(1)}, f32[4,8192]{1,0:T(4,128)S(1)}, u32[]{:S(2)}, u32[]{:S(2)}) collective-permute-start(f32[4,8192]{1,0:T(4,128)S(1)} %pad_maximum_fusion.3), channel_id=1, source_target_pairs={{0,64},{16,80},{32,96},{48,112},{64,0},{80,16},{96,32},{112,48},{1... | collective-permute-start | bytes 393224 | tf_op jit(solution)/shard_map/ppermute | solution.py:173
  80.4 1.9 %all-to-all-done.1 = f32[256,1,128]{2,1,0:T(1,128)S(1)} async-done(((f32[256,1,128]{2,1,0:T(1,128)}), f32[256,1,128]{2,1,0:T(1,128)S(1)}, u32[]{:S(2)}, u32[]{:S(2)}) %all-to-all-start.1) | async-done | bytes 131104 | tf_op jit(solution)/shard_map/all_to_all | solution.py:225
  82.3 0.9 slice_reduce_fusion
  83.9 1.1 collective-permute-start.12
  85.1 1.1 collective-permute-start.11
  86.1 4.2 %collective-permute-done.15 = f32[4,8192]{1,0:T(4,128)S(1)} collective-permute-done((f32[4,8192]{1,0:T(4,128)S(1)}, f32[4,8192]{1,0:T(4,128)S(1)}, u32[]{:S(2)}, u32[]{:S(2)}) %collective-permute-start.15) | collective-permute-done | bytes 131104 | tf_op jit(solution)/shard_map/ppermute | solution.py:173
  90.4 5.7 %collective-permute-done.13 = f32[4,8192]{1,0:T(4,128)S(1)} collective-permute-done((f32[4,8192]{1,0:T(4,128)S(1)}, f32[4,8192]{1,0:T(4,128)S(1)}, u32[]{:S(2)}, u32[]{:S(2)}) %collective-permute-start.13) | collective-permute-done | bytes 131104 | tf_op jit(solution)/shard_map/ppermute | solution.py:173
  96.2 2.7 %collective-permute-done.12 = f32[4,8192]{1,0:T(4,128)S(1)} collective-permute-done((f32[4,8192]{1,0:T(4,128)S(1)}, f32[4,8192]{1,0:T(4,128)S(1)}, u32[]{:S(2)}, u32[]{:S(2)}) %collective-permute-start.12) | collective-permute-done | bytes 131104 | tf_op jit(solution)/shard_map/ppermute | solution.py:173
  98.9 5.4 %collective-permute-done.11 = f32[4,8192]{1,0:T(4,128)S(1)} collective-permute-done((f32[4,8192]{1,0:T(4,128)S(1)}, f32[4,8192]{1,0:T(4,128)S(1)}, u32[]{:S(2)}, u32[]{:S(2)}) %collective-permute-start.11) | collective-permute-done | bytes 131104 | tf_op jit(solution)/shard_map/ppermute | solution.py:173
  104.6 2.9 %collective-permute-start.24 = (bf16[32,2048]{1,0:T(8,128)(2,1)S(1)}, bf16[32,2048]{1,0:T(8,128)(2,1)S(1)}, u32[]{:S(2)}, u32[]{:S(2)}) collective-permute-start(bf16[32,2048]{1,0:T(8,128)(2,1)S(1)} %get-tuple-element.46), channel_id=1, source_target_pairs={{0,128},{128,0},{1,129},{129,1},{2,130},{130,2},{3,131},{131,3},{4... | collective-permute-start | bytes 393224 | tf_op jit(solution)/shard_map/ppermute | solution.py:173
  107.5 1.5 %collective-permute-start.10 = (f32[2,4096]{1,0:T(2,128)S(1)}, f32[2,4096]{1,0:T(2,128)S(1)}, u32[]{:S(2)}, u32[]{:S(2)}) collective-permute-start(f32[2,4096]{1,0:T(2,128)S(1)} %constant_dynamic-slice_fusion), channel_id=1, source_target_pairs={{0,2},{2,0},{1,3},{3,1},{4,6},{6,4},{5,7},{7,5},{8,10},{10,8},{9,1... | collective-permute-start | bytes 98312 | tf_op jit(solution)/shard_map/ppermute | solution.py:173
  108.9 1.2 collective-permute-start.18
  110.2 2.5 %collective-permute-start.19 = (bf16[32,2048]{1,0:T(8,128)(2,1)S(1)}, bf16[32,2048]{1,0:T(8,128)(2,1)S(1)}, u32[]{:S(2)}, u32[]{:S(2)}) collective-permute-start(bf16[32,2048]{1,0:T(8,128)(2,1)S(1)} %get-tuple-element.47), channel_id=1, source_target_pairs={{0,8},{4,12},{8,0},{12,4},{1,9},{5,13},{9,1},{13,5},{2,10},{6,14},... | collective-permute-start | bytes 393224 | tf_op jit(solution)/shard_map/ppermute | solution.py:173
  112.7 1.1 collective-permute-start.20
  115.1 1.6 %collective-permute-start.26 = (bf16[64,2048]{1,0:T(8,128)(2,1)S(1)}, bf16[64,2048]{1,0:T(8,128)(2,1)S(1)}, u32[]{:S(2)}, u32[]{:S(2)}) collective-permute-start(bf16[64,2048]{1,0:T(8,128)(2,1)S(1)} %pad_maximum_fusion.2.refs_0_), channel_id=1, source_target_pairs={{0,8},{4,12},{8,0},{12,4},{1,9},{5,13},{9,1},{13,5},{2,10},{6,14},... | collective-permute-start | bytes 786440 | tf_op jit(solution)/shard_map/ppermute | solution.py:173
  116.7 2.3 %collective-permute-done.19 = bf16[32,2048]{1,0:T(8,128)(2,1)S(1)} collective-permute-done((bf16[32,2048]{1,0:T(8,128)(2,1)S(1)}, bf16[32,2048]{1,0:T(8,128)(2,1)S(1)}, u32[]{:S(2)}, u32[]{:S(2)}) %collective-permute-start.19) | collective-permute-done | bytes 131104 | tf_op jit(solution)/shard_map/ppermute | solution.py:173
  119.0 1.6 %collective-permute-start.28 = (bf16[64,2048]{1,0:T(8,128)(2,1)S(1)}, bf16[64,2048]{1,0:T(8,128)(2,1)S(1)}, u32[]{:S(2)}, u32[]{:S(2)}) collective-permute-start(bf16[64,2048]{1,0:T(8,128)(2,1)S(1)} %pad_maximum_fusion.2.refs_0_), channel_id=1, source_target_pairs={{0,2},{2,0},{1,3},{3,1},{4,6},{6,4},{5,7},{7,5},{8,10},{10,8},{9,1... | collective-permute-start | bytes 786440 | tf_op jit(solution)/shard_map/ppermute | solution.py:173
  121.0 4.5 %collective-permute-done.25.refs_1_ = bf16[64,2048]{1,0:T(8,128)(2,1)S(1)} collective-permute-done((bf16[64,2048]{1,0:T(8,128)(2,1)S(1)}, bf16[64,2048]{1,0:T(8,128)(2,1)S(1)}, u32[]{:S(2)}, u32[]{:S(2)}) %collective-permute-start.25) | collective-permute-done | bytes 262176 | tf_op jit(solution)/shard_map/ppermute | solution.py:173
  126.1 4.1 %collective-permute-done.26.refs_2_ = bf16[64,2048]{1,0:T(8,128)(2,1)S(1)} collective-permute-done((bf16[64,2048]{1,0:T(8,128)(2,1)S(1)}, bf16[64,2048]{1,0:T(8,128)(2,1)S(1)}, u32[]{:S(2)}, u32[]{:S(2)}) %collective-permute-start.26) | collective-permute-done | bytes 262176 | tf_op jit(solution)/shard_map/ppermute | solution.py:173
  130.2 0.9 collective-permute-start.29
  131.7 4.0 %collective-permute-done.21.refs_1_ = bf16[128,2048]{1,0:T(8,128)(2,1)S(1)} collective-permute-done((bf16[128,2048]{1,0:T(8,128)(2,1)S(1)}, bf16[128,2048]{1,0:T(8,128)(2,1)S(1)}, u32[]{:S(2)}, u32[]{:S(2)}) %collective-permute-start.21) | collective-permute-done | bytes 524320 | tf_op jit(solution)/shard_map/ppermute | solution.py:173
  135.7 0.9 collective-permute-start.23
  137.4 2.6 %from_blocks.2.refs_4_ = bf16[256,8192]{1,0:T(8,128)(2,1)} custom-call(s32[1]{0:T(128)} %bitcast.2.core, bf16[256,256]{1,0:T(8,128)(2,1)S(1)} %fusion.5.one, bf16[64,2048]{1,0:T(8,128)(2,1)S(1)} %pad_maximum_fusion.2.refs_0_, bf16[64,2048]{1,0:T(8,128)(2,1)S(1)} %collective-permute-done.25.refs_1_, bf16[64,2048]{1,0:T(8,128)(2,1)S(1)} %collective-permute-done.26.refs_2_, ...), custom_call_target="tpu_custom_call" | custom-call | tf_op jit(solution)/shard_map/from_blocks/pallas_call | solution.py:144
  140.0 2.6 %from_blocks.3 = bf16[256,8192]{1,0:T(8,128)(2,1)} custom-call(s32[1]{0:T(128)} %bitcast.2.core, bf16[256,256]{1,0:T(8,128)(2,1)S(1)} %fusion.4.one, bf16[128,2048]{1,0:T(8,128)(2,1)S(1)} %pad_maximum_fusion.refs_0_, bf16[128,2048]{1,0:T(8,128)(2,1)S(1)} %collective-permute-done.21.refs_1_, ...), custom_call_target="tpu_custom_call", output_to_operand_aliasing={{}: (6, {})} | custom-call | tf_op jit(solution)/shard_map/from_blocks/pallas_call | solution.py:144
  (75 shorter events, 9.4 us)
Async XLA Ops:
  3.7 7.3 %collective-permute-start = (bf16[256,4096]{1,0:T(8,128)(2,1)}, bf16[256,4096]{1,0:T(8,128)(2,1)S(1)}, u32[]{:S(2)}, u32[]{:S(2)}) collective-permute-start(bf16[256,4096]{1,0:T(8,128)(2,1)} %pick.1), channel_id=1, source_target_pairs={{0,2},{2,0},{1,3},{3,1},{4,6},{6,4},{5,7},{7,5},{8,10},{10,8},{9,1... | collective-permute-start | bytes 6291464 | tf_op jit(solution)/shard_map/ppermute | solution.py:173
  10.0 2.5 %copy-start.1 = (f32[1,2,8192]{2,1,0:T(2,128)S(1)}, f32[1,2,8192]{2,1,0:T(2,128)}, u32[]{:S(2)}) copy-start(f32[1,2,8192]{2,1,0:T(2,128)} %param.6) | copy-start | bytes 196612
  10.1 2.5 %copy-start.2 = (f32[1,2,8192]{2,1,0:T(2,128)S(1)}, f32[1,2,8192]{2,1,0:T(2,128)}, u32[]{:S(2)}) copy-start(f32[1,2,8192]{2,1,0:T(2,128)} %param.7) | copy-start | bytes 196612
  11.7 0.8 copy-start
  12.7 7.2 %collective-permute-start.1 = (f32[2,4096]{1,0:T(2,128)S(1)}, f32[2,4096]{1,0:T(2,128)S(1)}, u32[]{:S(2)}, u32[]{:S(2)}) collective-permute-start(f32[2,4096]{1,0:T(2,128)S(1)} %dynamic-slice_bitcast_fusion), channel_id=1, source_target_pairs={{0,2},{2,0},{1,3},{3,1},{4,6},{6,4},{5,7},{7,5},{8,10},{10,8},{9,1... | collective-permute-start | bytes 98312 | tf_op jit(solution)/shard_map/ppermute | solution.py:173
  13.1 9.4 %collective-permute-start.2 = (f16[64,2048]{1,0:T(8,128)(2,1)S(1)}, f16[64,2048]{1,0:T(8,128)(2,1)S(1)}, u32[]{:S(2)}, u32[]{:S(2)}) collective-permute-start(f16[64,2048]{1,0:T(8,128)(2,1)S(1)} %convert_element_type.93), channel_id=1, source_target_pairs={{0,8},{4,12},{8,0},{12,4},{1,9},{5,13},{9,1},{13,5},{2,10},{6,14},... | collective-permute-start | bytes 786440 | tf_op jit(solution)/shard_map/ppermute | solution.py:173
  14.4 14.2 %collective-permute-start.3 = (f16[64,2048]{1,0:T(8,128)(2,1)S(1)}, f16[64,2048]{1,0:T(8,128)(2,1)S(1)}, u32[]{:S(2)}, u32[]{:S(2)}) collective-permute-start(f16[64,2048]{1,0:T(8,128)(2,1)S(1)} %convert_element_type.92), channel_id=1, source_target_pairs={{0,4},{4,8},{8,12},{12,0},{1,5},{5,9},{9,13},{13,1},{2,6},{6,10},{... | collective-permute-start | bytes 786440 | tf_op jit(solution)/shard_map/ppermute | solution.py:173
  14.8 13.8 %collective-permute-start.4 = (f16[64,2048]{1,0:T(8,128)(2,1)S(1)}, f16[64,2048]{1,0:T(8,128)(2,1)S(1)}, u32[]{:S(2)}, u32[]{:S(2)}) collective-permute-start(f16[64,2048]{1,0:T(8,128)(2,1)S(1)} %convert_element_type.94), channel_id=1, source_target_pairs={{0,12},{4,0},{8,4},{12,8},{1,13},{5,1},{9,5},{13,9},{2,14},{6,2},{... | collective-permute-start | bytes 786440 | tf_op jit(solution)/shard_map/ppermute | solution.py:173
  17.1 14.0 %collective-permute-start.6 = (f16[128,2048]{1,0:T(8,128)(2,1)S(1)}, f16[128,2048]{1,0:T(8,128)(2,1)S(1)}, u32[]{:S(2)}, u32[]{:S(2)}) collective-permute-start(f16[128,2048]{1,0:T(8,128)(2,1)S(1)} %convert_element_type.91), channel_id=1, source_target_pairs={{0,128},{128,0},{1,129},{129,1},{2,130},{130,2},{3,131},{131,3},{4... | collective-permute-start | bytes 1572872 | tf_op jit(solution)/shard_map/ppermute | solution.py:173
  29.8 6.2 %collective-permute-start.5 = (f16[32,2048]{1,0:T(8,128)(2,1)S(1)}, f16[32,2048]{1,0:T(8,128)(2,1)S(1)}, u32[]{:S(2)}, u32[]{:S(2)}) collective-permute-start(f16[32,2048]{1,0:T(8,128)(2,1)S(1)} %slice_convert_fusion), channel_id=1, source_target_pairs={{0,128},{128,0},{1,129},{129,1},{2,130},{130,2},{3,131},{131,3},{4... | collective-permute-start | bytes 393224 | tf_op jit(solution)/shard_map/ppermute | solution.py:173
  31.4 5.5 %collective-permute-start.7 = (f16[32,2048]{1,0:T(8,128)(2,1)S(1)}, f16[32,2048]{1,0:T(8,128)(2,1)S(1)}, u32[]{:S(2)}, u32[]{:S(2)}) collective-permute-start(f16[32,2048]{1,0:T(8,128)(2,1)S(1)} %get-tuple-element.43), channel_id=1, source_target_pairs={{0,8},{4,12},{8,0},{12,4},{1,9},{5,13},{9,1},{13,5},{2,10},{6,14},... | collective-permute-start | bytes 393224 | tf_op jit(solution)/shard_map/ppermute | solution.py:173
  32.9 6.3 %collective-permute-start.8 = (f16[32,2048]{1,0:T(8,128)(2,1)S(1)}, f16[32,2048]{1,0:T(8,128)(2,1)S(1)}, u32[]{:S(2)}, u32[]{:S(2)}) collective-permute-start(f16[32,2048]{1,0:T(8,128)(2,1)S(1)} %get-tuple-element.45), channel_id=1, source_target_pairs={{0,4},{4,8},{8,12},{12,0},{1,5},{5,9},{9,13},{13,1},{2,6},{6,10},{... | collective-permute-start | bytes 393224 | tf_op jit(solution)/shard_map/ppermute | solution.py:173
  34.6 5.6 %collective-permute-start.9 = (f16[32,2048]{1,0:T(8,128)(2,1)S(1)}, f16[32,2048]{1,0:T(8,128)(2,1)S(1)}, u32[]{:S(2)}, u32[]{:S(2)}) collective-permute-start(f16[32,2048]{1,0:T(8,128)(2,1)S(1)} %get-tuple-element.44), channel_id=1, source_target_pairs={{0,12},{4,0},{8,4},{12,8},{1,13},{5,1},{9,5},{13,9},{2,14},{6,2},{... | collective-permute-start | bytes 393224 | tf_op jit(solution)/shard_map/ppermute | solution.py:173
  41.2 17.5 %all-to-all-start = ((f16[8,4,4096]{2,1,0:T(4,128)(2,1)}), f16[8,4,4096]{2,1,0:T(4,128)(2,1)S(1)}, u32[]{:S(2)}, u32[]{:S(2)}) async-start(f16[8,4,4096]{2,1,0:T(4,128)(2,1)} %pad_maximum_fusion.1), calls=%async_computation | async-start | bytes 524288 | tf_op jit(solution)/shard_map/all_to_all | solution.py:217
  60.8 21.5 %all-to-all-start.1 = ((f32[256,1,128]{2,1,0:T(1,128)}), f32[256,1,128]{2,1,0:T(1,128)S(1)}, u32[]{:S(2)}, u32[]{:S(2)}) async-start(f32[256,1,128]{2,1,0:T(1,128)} %broadcast_in_dim.27), calls=%async_computation.1 | async-start | bytes 262144 | tf_op jit(solution)/shard_map/all_to_all | solution.py:225
  69.5 14.4 %collective-permute-start.17 = (f32[4,8192]{1,0:T(4,128)S(1)}, f32[4,8192]{1,0:T(4,128)S(1)}, u32[]{:S(2)}, u32[]{:S(2)}) collective-permute-start(f32[4,8192]{1,0:T(4,128)S(1)} %pad_maximum_fusion.3), channel_id=1, source_target_pairs={{0,112},{16,0},{32,16},{48,32},{64,48},{80,64},{96,80},{112,96},{1... | collective-permute-start | bytes 393224 | tf_op jit(solution)/shard_map/ppermute | solution.py:173
  74.1 10.9 %collective-permute-start.16 = (f32[4,8192]{1,0:T(4,128)S(1)}, f32[4,8192]{1,0:T(4,128)S(1)}, u32[]{:S(2)}, u32[]{:S(2)}) collective-permute-start(f32[4,8192]{1,0:T(4,128)S(1)} %pad_maximum_fusion.3), channel_id=1, source_target_pairs={{0,96},{16,112},{32,0},{48,16},{64,32},{80,48},{96,64},{112,80},{1... | collective-permute-start | bytes 393224 | tf_op jit(solution)/shard_map/ppermute | solution.py:173
  75.7 14.7 %collective-permute-start.15 = (f32[4,8192]{1,0:T(4,128)S(1)}, f32[4,8192]{1,0:T(4,128)S(1)}, u32[]{:S(2)}, u32[]{:S(2)}) collective-permute-start(f32[4,8192]{1,0:T(4,128)S(1)} %pad_maximum_fusion.3), channel_id=1, source_target_pairs={{0,80},{16,96},{32,112},{48,0},{64,16},{80,32},{96,48},{112,64},{1... | collective-permute-start | bytes 393224 | tf_op jit(solution)/shard_map/ppermute | solution.py:173
  76.3 14.1 %collective-permute-start.14 = (f32[4,8192]{1,0:T(4,128)S(1)}, f32[4,8192]{1,0:T(4,128)S(1)}, u32[]{:S(2)}, u32[]{:S(2)}) collective-permute-start(f32[4,8192]{1,0:T(4,128)S(1)} %pad_maximum_fusion.3), channel_id=1, source_target_pairs={{0,64},{16,80},{32,96},{48,112},{64,0},{80,16},{96,32},{112,48},{1... | collective-permute-start | bytes 393224 | tf_op jit(solution)/shard_map/ppermute | solution.py:173
  80.4 15.8 %collective-permute-start.13 = (f32[4,8192]{1,0:T(4,128)S(1)}, f32[4,8192]{1,0:T(4,128)S(1)}, u32[]{:S(2)}, u32[]{:S(2)}) collective-permute-start(f32[4,8192]{1,0:T(4,128)S(1)} %pad_maximum_fusion.3), channel_id=1, source_target_pairs={{0,48},{16,64},{32,80},{48,96},{64,112},{80,0},{96,16},{112,32},{1... | collective-permute-start | bytes 393224 | tf_op jit(solution)/shard_map/ppermute | solution.py:173
  83.9 15.0 %collective-permute-start.12 = (f32[4,8192]{1,0:T(4,128)S(1)}, f32[4,8192]{1,0:T(4,128)S(1)}, u32[]{:S(2)}, u32[]{:S(2)}) collective-permute-start(f32[4,8192]{1,0:T(4,128)S(1)} %pad_maximum_fusion.3), channel_id=1, source_target_pairs={{0,32},{16,48},{32,64},{48,80},{64,96},{80,112},{96,0},{112,16},{1... | collective-permute-start | bytes 393224 | tf_op jit(solution)/shard_map/ppermute | solution.py:173
  85.1 19.3 %collective-permute-start.11 = (f32[4,8192]{1,0:T(4,128)S(1)}, f32[4,8192]{1,0:T(4,128)S(1)}, u32[]{:S(2)}, u32[]{:S(2)}) collective-permute-start(f32[4,8192]{1,0:T(4,128)S(1)} %pad_maximum_fusion.3), channel_id=1, source_target_pairs={{0,16},{16,32},{32,48},{48,64},{64,80},{80,96},{96,112},{112,0},{1... | collective-permute-start | bytes 393224 | tf_op jit(solution)/shard_map/ppermute | solution.py:173
  104.6 9.2 %collective-permute-start.24 = (bf16[32,2048]{1,0:T(8,128)(2,1)S(1)}, bf16[32,2048]{1,0:T(8,128)(2,1)S(1)}, u32[]{:S(2)}, u32[]{:S(2)}) collective-permute-start(bf16[32,2048]{1,0:T(8,128)(2,1)S(1)} %get-tuple-element.46), channel_id=1, source_target_pairs={{0,128},{128,0},{1,129},{129,1},{2,130},{130,2},{3,131},{131,3},{4... | collective-permute-start | bytes 393224 | tf_op jit(solution)/shard_map/ppermute | solution.py:173
  107.5 13.2 %collective-permute-start.10 = (f32[2,4096]{1,0:T(2,128)S(1)}, f32[2,4096]{1,0:T(2,128)S(1)}, u32[]{:S(2)}, u32[]{:S(2)}) collective-permute-start(f32[2,4096]{1,0:T(2,128)S(1)} %constant_dynamic-slice_fusion), channel_id=1, source_target_pairs={{0,2},{2,0},{1,3},{3,1},{4,6},{6,4},{5,7},{7,5},{8,10},{10,8},{9,1... | collective-permute-start | bytes 98312 | tf_op jit(solution)/shard_map/ppermute | solution.py:173
  108.9 6.2 %collective-permute-start.18 = (bf16[32,2048]{1,0:T(8,128)(2,1)S(1)}, bf16[32,2048]{1,0:T(8,128)(2,1)S(1)}, u32[]{:S(2)}, u32[]{:S(2)}) collective-permute-start(bf16[32,2048]{1,0:T(8,128)(2,1)S(1)} %get-tuple-element.47), channel_id=1, source_target_pairs={{0,4},{4,8},{8,12},{12,0},{1,5},{5,9},{9,13},{13,1},{2,6},{6,10},{... | collective-permute-start | bytes 393224 | tf_op jit(solution)/shard_map/ppermute | solution.py:173
  110.2 8.8 %collective-permute-start.19 = (bf16[32,2048]{1,0:T(8,128)(2,1)S(1)}, bf16[32,2048]{1,0:T(8,128)(2,1)S(1)}, u32[]{:S(2)}, u32[]{:S(2)}) collective-permute-start(bf16[32,2048]{1,0:T(8,128)(2,1)S(1)} %get-tuple-element.47), channel_id=1, source_target_pairs={{0,8},{4,12},{8,0},{12,4},{1,9},{5,13},{9,1},{13,5},{2,10},{6,14},... | collective-permute-start | bytes 393224 | tf_op jit(solution)/shard_map/ppermute | solution.py:173
  112.7 6.3 %collective-permute-start.20 = (bf16[32,2048]{1,0:T(8,128)(2,1)S(1)}, bf16[32,2048]{1,0:T(8,128)(2,1)S(1)}, u32[]{:S(2)}, u32[]{:S(2)}) collective-permute-start(bf16[32,2048]{1,0:T(8,128)(2,1)S(1)} %get-tuple-element.47), channel_id=1, source_target_pairs={{0,12},{4,0},{8,4},{12,8},{1,13},{5,1},{9,5},{13,9},{2,14},{6,2},{... | collective-permute-start | bytes 393224 | tf_op jit(solution)/shard_map/ppermute | solution.py:173
  113.8 11.7 %collective-permute-start.25 = (bf16[64,2048]{1,0:T(8,128)(2,1)S(1)}, bf16[64,2048]{1,0:T(8,128)(2,1)S(1)}, u32[]{:S(2)}, u32[]{:S(2)}) collective-permute-start(bf16[64,2048]{1,0:T(8,128)(2,1)S(1)} %pad_maximum_fusion.2.refs_0_), channel_id=1, source_target_pairs={{0,4},{4,8},{8,12},{12,0},{1,5},{5,9},{9,13},{13,1},{2,6},{6,10},{... | collective-permute-start | bytes 786440 | tf_op jit(solution)/shard_map/ppermute | solution.py:173
  115.1 15.1 %collective-permute-start.26 = (bf16[64,2048]{1,0:T(8,128)(2,1)S(1)}, bf16[64,2048]{1,0:T(8,128)(2,1)S(1)}, u32[]{:S(2)}, u32[]{:S(2)}) collective-permute-start(bf16[64,2048]{1,0:T(8,128)(2,1)S(1)} %pad_maximum_fusion.2.refs_0_), channel_id=1, source_target_pairs={{0,8},{4,12},{8,0},{12,4},{1,9},{5,13},{9,1},{13,5},{2,10},{6,14},... | collective-permute-start | bytes 786440 | tf_op jit(solution)/shard_map/ppermute | solution.py:173
  119.0 12.2 %collective-permute-start.27 = (bf16[64,2048]{1,0:T(8,128)(2,1)S(1)}, bf16[64,2048]{1,0:T(8,128)(2,1)S(1)}, u32[]{:S(2)}, u32[]{:S(2)}) collective-permute-start(bf16[64,2048]{1,0:T(8,128)(2,1)S(1)} %pad_maximum_fusion.2.refs_0_), channel_id=1, source_target_pairs={{0,12},{4,0},{8,4},{12,8},{1,13},{5,1},{9,5},{13,9},{2,14},{6,2},{... | collective-permute-start | bytes 786440 | tf_op jit(solution)/shard_map/ppermute | solution.py:173
  119.0 12.2 %collective-permute-start.28 = (bf16[64,2048]{1,0:T(8,128)(2,1)S(1)}, bf16[64,2048]{1,0:T(8,128)(2,1)S(1)}, u32[]{:S(2)}, u32[]{:S(2)}) collective-permute-start(bf16[64,2048]{1,0:T(8,128)(2,1)S(1)} %pad_maximum_fusion.2.refs_0_), channel_id=1, source_target_pairs={{0,2},{2,0},{1,3},{3,1},{4,6},{6,4},{5,7},{7,5},{8,10},{10,8},{9,1... | collective-permute-start | bytes 786440 | tf_op jit(solution)/shard_map/ppermute | solution.py:173
  120.7 15.1 %collective-permute-start.21 = (bf16[128,2048]{1,0:T(8,128)(2,1)S(1)}, bf16[128,2048]{1,0:T(8,128)(2,1)S(1)}, u32[]{:S(2)}, u32[]{:S(2)}) collective-permute-start(bf16[128,2048]{1,0:T(8,128)(2,1)S(1)} %pad_maximum_fusion.refs_0_), channel_id=1, source_target_pairs={{0,128},{128,0},{1,129},{129,1},{2,130},{130,2},{3,131},{131,3},{4... | collective-permute-start | bytes 1572872 | tf_op jit(solution)/shard_map/ppermute | solution.py:173
  125.5 14.5 %collective-permute-start.22 = (bf16[128,2048]{1,0:T(8,128)(2,1)S(1)}, bf16[128,2048]{1,0:T(8,128)(2,1)S(1)}, u32[]{:S(2)}, u32[]{:S(2)}) collective-permute-start(bf16[128,2048]{1,0:T(8,128)(2,1)S(1)} %pad_maximum_fusion.refs_0_), channel_id=1, source_target_pairs={{0,2},{2,0},{1,3},{3,1},{4,6},{6,4},{5,7},{7,5},{8,10},{10,8},{9,1... | collective-permute-start | bytes 1572872 | tf_op jit(solution)/shard_map/ppermute | solution.py:173
  130.2 7.1 %collective-permute-start.29 = (bf16[64,2048]{1,0:T(8,128)(2,1)S(1)}, bf16[64,2048]{1,0:T(8,128)(2,1)S(1)}, u32[]{:S(2)}, u32[]{:S(2)}) collective-permute-start(bf16[64,2048]{1,0:T(8,128)(2,1)S(1)} %collective-permute-done.25.refs_1_), channel_id=1, source_target_pairs={{0,2},{2,0},{1,3},{3,1},{4,6},{6,4},{5,7},{7,5},{8,10},{10,8},{9,1... | collective-permute-start | bytes 786440 | tf_op jit(solution)/shard_map/ppermute | solution.py:173
  131.2 6.2 %collective-permute-start.30 = (bf16[64,2048]{1,0:T(8,128)(2,1)S(1)}, bf16[64,2048]{1,0:T(8,128)(2,1)S(1)}, u32[]{:S(2)}, u32[]{:S(2)}) collective-permute-start(bf16[64,2048]{1,0:T(8,128)(2,1)S(1)} %collective-permute-done.26.refs_2_), channel_id=1, source_target_pairs={{0,2},{2,0},{1,3},{3,1},{4,6},{6,4},{5,7},{7,5},{8,10},{10,8},{9,1... | collective-permute-start | bytes 786440 | tf_op jit(solution)/shard_map/ppermute | solution.py:173
  131.2 6.1 %collective-permute-start.31 = (bf16[64,2048]{1,0:T(8,128)(2,1)S(1)}, bf16[64,2048]{1,0:T(8,128)(2,1)S(1)}, u32[]{:S(2)}, u32[]{:S(2)}) collective-permute-start(bf16[64,2048]{1,0:T(8,128)(2,1)S(1)} %collective-permute-done.27.refs_3_), channel_id=1, source_target_pairs={{0,2},{2,0},{1,3},{3,1},{4,6},{6,4},{5,7},{7,5},{8,10},{10,8},{9,1... | collective-permute-start | bytes 786440 | tf_op jit(solution)/shard_map/ppermute | solution.py:173
  135.7 4.3 %collective-permute-start.23 = (bf16[128,2048]{1,0:T(8,128)(2,1)S(1)}, bf16[128,2048]{1,0:T(8,128)(2,1)S(1)}, u32[]{:S(2)}, u32[]{:S(2)}) collective-permute-start(bf16[128,2048]{1,0:T(8,128)(2,1)S(1)} %collective-permute-done.21.refs_1_), channel_id=1, source_target_pairs={{0,2},{2,0},{1,3},{3,1},{4,6},{6,4},{5,7},{7,5},{8,10},{10,8},{9,1... | collective-permute-start | bytes 1572872 | tf_op jit(solution)/shard_map/ppermute | solution.py:173

commit v2 on v1

--- a/solution.py
+++ b/solution.py
@@ -180,7 +180,7 @@
 
     o = jnp.arange(rows)
     q, z, h, j = o % 4, o // 4 % nz, o // (4 * nz) % nx, o // (4 * nz * nx)
-    to = row_of(j, h, z, q, 1)[:, None] == o[None]
+    to = row_of(j, h, (lax.axis_index("z") + z) % nz, q, 1)[:, None] == o[None]
     z = (lax.axis_index("z") - z) % nz
     back_y = o[:, None] == row_of(j, h, z, q, -1)[None]
     j, h = o // (4 * nz) % ny, o // (4 * nz * ny)
@@ -203,6 +203,7 @@
     mine, theirs = part(base, 0, at[0]), part(base, 0, at[1])
     theirs = send(theirs, "c", 1)
     base = jnp.concatenate([jnp.where(core == 0, mine, theirs), jnp.where(core == 0, theirs, mine)], axis=0)
+    base = lax.all_to_all(jnp.broadcast_to(base[None], (nz, 4, half)), "z", 0, 0, tiled=True)
 
     per = rows // (nx * ny)
     pieces = [second[j * per : (j + 1) * per] for j in range(ny)]
@@ -212,14 +213,16 @@
         second = second + wide(send(pieces[j].astype(wire), "y", j))
     first = first[:per] + wide(far)
 
-    total = jnp.concatenate([first, second], axis=1).astype(wire).reshape(nz, 4, half)
-    base, total = lax.optimization_barrier((base, total))
-    total = wide(lax.all_to_all(total, "z", 0, 0, tiled=True)).sum(axis=0)
+    far_z = (4, 3, 5, 2, 6, 1, 7)
+    total = jnp.concatenate([first, second], axis=1).reshape(nz, 4, half)
+    pieces = [total[k] for k in range(nz)]
+    total = pieces[0]
+    for k in far_z:
+        total = total + wide(send(pieces[k].astype(wire), "z", k))
     grad = total * (1.0 / (SCALE * replicas))
-    grad = lax.optimization_barrier(grad)
-    pair = lax.optimization_barrier(jnp.concatenate([base, grad], axis=1))
-    pairs = {k: send(pair, "z", k) for k in (4, 3, 5, 2, 6, 1, 7)}
-    pairs[0] = pair
+    grad, base = lax.optimization_barrier((grad, base))
+    grads = {k: send(grad, "z", k) for k in far_z}
+    grads[0] = grad
 
     members = lax.axis_size(ALL)
     parts = lax.all_to_all(jnp.full((members, 1, 128), jnp.sum(grad * grad)), ALL, 0, 0, tiled=True)
@@ -228,9 +231,11 @@
     grad_rms = jnp.sqrt(squares / elements + epsilon)
     clip = jnp.minimum(1.0, clip_limit / grad_rms)
 
-    pairs = [pairs[k] for k in range(nz)]
-    mine = [x[:, :half] - outer_rate * (1.0 + nesterov_mu) * (clip * x[:, half:]) for x in pairs]
-    mine = [x.astype(jnp.bfloat16) for x in mine]
+    mine = []
+    for k in range(nz):
+        there = lax.rem(lax.axis_index("z") + (nz - k), nz)
+        there = lax.dynamic_index_in_dim(base, there, 0, keepdims=False, allow_negative_indices=False)
+        mine.append((there - outer_rate * (1.0 + nesterov_mu) * (clip * grads[k])).astype(jnp.bfloat16))
     mine = jnp.concatenate(mine, axis=0)
     first, second = mine[:, :edge], mine[:, edge:]
     arrived = {j: send(second, "y", j) for j in far_y}

time: 143 us -> 147 us (1.028)
  starting transfers between devices: 61.8 us -> 85.5 us
  waiting for transfers between devices: 59.1 us -> 41.2 us
  other arithmetic: 5.59 us -> 3.57 us
    ppermute x32 -> x39, starting transfers between devices: 44.9 us -> 64.2 us  [send(): return lax.ppermute(x, axis, shift(axis, by))]
    all_to_all x1, waiting for transfers between devices: 9.18 us -> 0.01 us  [step(): lax.all_to_all(jnp.broadcast_to(base[None], (nz, 4, half)), 'z', 0, 0, ti...]
    ppermute x32 -> x39, waiting for transfers between devices: 48.1 us -> 41.2 us  [send(): return lax.ppermute(x, axis, shift(axis, by))]
    all_to_all x1, starting transfers between devices: 8.64 us -> 15.1 us  [step(): lax.all_to_all(jnp.full((members, 1, 128), jnp.sum(grad * grad)), ALL, 0,...]
    all_to_all x1, starting transfers between devices: 8.19 us -> 6.11 us  [step(): lax.all_to_all(jnp.broadcast_to(base[None], (nz, 4, half)), 'z', 0, 0, ti...]
    all_to_all x1, waiting for transfers between devices: 1.92 us -> 0.01 us  [step(): lax.all_to_all(jnp.full((members, 1, 128), jnp.sum(grad * grad)), ALL, 0,...]
  transfers between devices with their start and end apart: 34 -> 41, of which waited for: 19 -> 16; matrix products, arithmetic and copies ran while one was open for 3% -> 2% of each run, Pallas kernels for 4% -> 4%
where the time goes in v2:
time: 147 us
  starting transfers between devices  85.5 us (58%)
  waiting for transfers between devices  41.2 us (28%)
  Pallas kernels  11.9 us (8%)
  other arithmetic  3.57 us (2%)
  local copies, waits for them, and re-layouts  2.76 us (2%)
  between operations  1.66 us (1%)
    ppermute x39, starting transfers between devices, send(): return lax.ppermute(x, axis, shift(axis, by))  64.2 us
    ppermute x39, waiting for transfers between devices, send(): return lax.ppermute(x, axis, shift(axis, by))  41.2 us
    all_to_all x1, starting transfers between devices, step(): lax.all_to_all(jnp.full((members, 1, 128), jnp.sum(grad * grad)), ALL, 0,...  15.1 us
    all_to_all x1, starting transfers between devices, step(): lax.all_to_all(jnp.broadcast_to(base[None], (nz, 4, half)), 'z', 0, 0, ti...  6.11 us
    pallas_call x2, Pallas kernels, from_blocks(): pl.pallas_call(from_blocks_kernel, grid_spec=pltpu.PrefetchScalarGridSpec...  5.25 us
    pallas_call x1, Pallas kernels, change(): pl.pallas_call(change_kernel, in_specs=[SMEM, VMEM, HBM, HBM], out_specs=...  3.05 us
  transfers between devices with their start and end apart: 41, of which 16 were waited for; matrix products, arithmetic and copies ran while one was open for 2% of the time, Pallas kernels for 4%

profile of v2, /device:TPU:1, one launch (start us, length us, event | category | flops | bytes accessed | tf_op | source)
XLA Modules:
  0.0 146.6 jit_solution(1493572728685488710)
XLA Ops:
  0.8 2.9 %pick.1 = bf16[256,4096]{1,0:T(8,128)(2,1)} custom-call(s32[1]{0:T(128)} %bitcast.2.core, bf16[256,8192]{1,0:T(8,128)(2,1)} %bitcast.45), custom_call_target="tpu_custom_call" | custom-call | tf_op jit(solution)/shard_map/pick/pallas_call | solution.py:48
  3.7 3.3 %collective-permute-start = (bf16[256,4096]{1,0:T(8,128)(2,1)}, bf16[256,4096]{1,0:T(8,128)(2,1)S(1)}, u32[]{:S(2)}, u32[]{:S(2)}) collective-permute-start(bf16[256,4096]{1,0:T(8,128)(2,1)} %pick.1), channel_id=1, source_target_pairs={{0,2},{2,0},{1,3},{3,1},{4,6},{6,4},{5,7},{7,5},{8,10},{10,8},{9,1... | collective-permute-start | bytes 6291464 | tf_op jit(solution)/shard_map/ppermute | solution.py:173
  7.0 3.0 %change.1.own = f32[256,4096]{1,0:T(8,128)S(1)} custom-call(s32[1]{0:T(128)} %bitcast.2.core, bf16[256,256]{1,0:T(8,128)(2,1)S(1)} %select_convert_fusion.one, bf16[256,8192]{1,0:T(8,128)(2,1)} %bitcast.46, bf16[256,8192]{1,0:T(8,128)(2,1)} %bitcast.48), custom_call_target="tpu_custom_call" | custom-call | tf_op jit(solution)/shard_map/change/pallas_call | solution.py:80
  10.1 0.9 collective-permute-done.other
  12.6 1.3 collective-permute-start.1
  14.2 2.3 %collective-permute-start.3 = (f16[64,2048]{1,0:T(8,128)(2,1)S(1)}, f16[64,2048]{1,0:T(8,128)(2,1)S(1)}, u32[]{:S(2)}, u32[]{:S(2)}) collective-permute-start(f16[64,2048]{1,0:T(8,128)(2,1)S(1)} %convert_element_type.120), channel_id=1, source_target_pairs={{0,12},{4,0},{8,4},{12,8},{1,13},{5,1},{9,5},{13,9},{2,14},{6,2},{... | collective-permute-start | bytes 786440 | tf_op jit(solution)/shard_map/ppermute | solution.py:173
  16.5 2.7 %collective-permute-start.5 = (f16[128,2048]{1,0:T(8,128)(2,1)S(1)}, f16[128,2048]{1,0:T(8,128)(2,1)S(1)}, u32[]{:S(2)}, u32[]{:S(2)}) collective-permute-start(f16[128,2048]{1,0:T(8,128)(2,1)S(1)} %convert_element_type.125), channel_id=1, source_target_pairs={{0,128},{128,0},{1,129},{129,1},{2,130},{130,2},{3,131},{131,3},{4... | collective-permute-start | bytes 1572872 | tf_op jit(solution)/shard_map/ppermute | solution.py:173
  19.4 2.5 %collective-permute-done.1 = f16[64,2048]{1,0:T(8,128)(2,1)S(1)} collective-permute-done((f16[64,2048]{1,0:T(8,128)(2,1)S(1)}, f16[64,2048]{1,0:T(8,128)(2,1)S(1)}, u32[]{:S(2)}, u32[]{:S(2)}) %collective-permute-start.1) | collective-permute-done | bytes 262176 | tf_op jit(solution)/shard_map/ppermute | solution.py:173
  21.9 6.1 %collective-permute-done.2 = f16[64,2048]{1,0:T(8,128)(2,1)S(1)} collective-permute-done((f16[64,2048]{1,0:T(8,128)(2,1)S(1)}, f16[64,2048]{1,0:T(8,128)(2,1)S(1)}, u32[]{:S(2)}, u32[]{:S(2)}) %collective-permute-start.2) | collective-permute-done | bytes 262176 | tf_op jit(solution)/shard_map/ppermute | solution.py:173
  28.2 1.1 collective-permute-start.4
  29.3 1.3 collective-permute-done.5
  31.4 1.5 %collective-permute-start.7 = (f16[32,2048]{1,0:T(8,128)(2,1)S(1)}, f16[32,2048]{1,0:T(8,128)(2,1)S(1)}, u32[]{:S(2)}, u32[]{:S(2)}) collective-permute-start(f16[32,2048]{1,0:T(8,128)(2,1)S(1)} %get-tuple-element.53), channel_id=1, source_target_pairs={{0,4},{4,8},{8,12},{12,0},{1,5},{5,9},{9,13},{13,1},{2,6},{6,10},{... | collective-permute-start | bytes 393224 | tf_op jit(solution)/shard_map/ppermute | solution.py:173
  32.9 1.2 collective-permute-start.8
  34.4 1.9 %collective-permute-done.6 = f16[32,2048]{1,0:T(8,128)(2,1)S(1)} collective-permute-done((f16[32,2048]{1,0:T(8,128)(2,1)S(1)}, f16[32,2048]{1,0:T(8,128)(2,1)S(1)}, u32[]{:S(2)}, u32[]{:S(2)}) %collective-permute-start.6) | collective-permute-done | bytes 131104 | tf_op jit(solution)/shard_map/ppermute | solution.py:173
  36.3 3.1 %collective-permute-done.7 = f16[32,2048]{1,0:T(8,128)(2,1)S(1)} collective-permute-done((f16[32,2048]{1,0:T(8,128)(2,1)S(1)}, f16[32,2048]{1,0:T(8,128)(2,1)S(1)}, u32[]{:S(2)}, u32[]{:S(2)}) %collective-permute-start.7) | collective-permute-done | bytes 131104 | tf_op jit(solution)/shard_map/ppermute | solution.py:173
  39.7 3.1 %collective-permute-start.10 = (f16[4,4096]{1,0:T(4,128)(2,1)S(1)}, f16[4,4096]{1,0:T(4,128)(2,1)S(1)}, u32[]{:S(2)}, u32[]{:S(2)}) collective-permute-start(f16[4,4096]{1,0:T(4,128)(2,1)S(1)} %get-tuple-element.62), channel_id=1, source_target_pairs={{0,48},{16,64},{32,80},{48,96},{64,112},{80,0},{96,16},{112,32},{1... | collective-permute-start | bytes 98312 | tf_op jit(solution)/shard_map/ppermute | solution.py:173
  42.7 2.2 %collective-permute-start.11 = (f16[4,4096]{1,0:T(4,128)(2,1)S(1)}, f16[4,4096]{1,0:T(4,128)(2,1)S(1)}, u32[]{:S(2)}, u32[]{:S(2)}) collective-permute-start(f16[4,4096]{1,0:T(4,128)(2,1)S(1)} %get-tuple-element.61), channel_id=1, source_target_pairs={{0,80},{16,96},{32,112},{48,0},{64,16},{80,32},{96,48},{112,64},{1... | collective-permute-start | bytes 98312 | tf_op jit(solution)/shard_map/ppermute | solution.py:173
  45.8 6.1 %all-to-all-start = ((f32[8,4,4096]{2,1,0:T(4,128)}), f32[8,4,4096]{2,1,0:T(4,128)S(1)}, u32[]{:S(2)}, u32[]{:S(2)}) async-start(f32[8,4,4096]{2,1,0:T(4,128)} %broadcast_in_dim.33), calls=%async_computation | async-start | bytes 1048576 | tf_op jit(solution)/shard_map/all_to_all | solution.py:206
  52.0 2.4 %collective-permute-start.12 = (f16[4,4096]{1,0:T(4,128)(2,1)S(1)}, f16[4,4096]{1,0:T(4,128)(2,1)S(1)}, u32[]{:S(2)}, u32[]{:S(2)}) collective-permute-start(f16[4,4096]{1,0:T(4,128)(2,1)S(1)} %get-tuple-element.60), channel_id=1, source_target_pairs={{0,32},{16,48},{32,64},{48,80},{64,96},{80,112},{96,0},{112,16},{1... | collective-permute-start | bytes 98312 | tf_op jit(solution)/shard_map/ppermute | solution.py:173
  54.3 1.2 collective-permute-start.13
  55.5 1.4 collective-permute-start.14
  57.0 1.2 collective-permute-start.15
  58.2 5.4 %collective-permute-start.9 = (f16[4,4096]{1,0:T(4,128)(2,1)S(1)}, f16[4,4096]{1,0:T(4,128)(2,1)S(1)}, u32[]{:S(2)}, u32[]{:S(2)}) collective-permute-start(f16[4,4096]{1,0:T(4,128)(2,1)S(1)} %get-tuple-element.56), channel_id=1, source_target_pairs={{0,64},{16,80},{32,96},{48,112},{64,0},{80,16},{96,32},{112,48},{1... | collective-permute-start | bytes 98312 | tf_op jit(solution)/shard_map/ppermute | solution.py:173
  64.4 3.8 %collective-permute-done.9 = f16[4,4096]{1,0:T(4,128)(2,1)S(1)} collective-permute-done((f16[4,4096]{1,0:T(4,128)(2,1)S(1)}, f16[4,4096]{1,0:T(4,128)(2,1)S(1)}, u32[]{:S(2)}, u32[]{:S(2)}) %collective-permute-start.9) | collective-permute-done | bytes 32800 | tf_op jit(solution)/shard_map/ppermute | solution.py:173
  68.9 1.4 broadcast_in_dim.34
  70.3 15.1 %all-to-all-start.1 = ((f32[256,1,128]{2,1,0:T(1,128)}), f32[256,1,128]{2,1,0:T(1,128)S(1)}, u32[]{:S(2)}, u32[]{:S(2)}) async-start(f32[256,1,128]{2,1,0:T(1,128)} %broadcast_in_dim.34), calls=%async_computation.1 | async-start | bytes 262144 | tf_op jit(solution)/shard_map/all_to_all | solution.py:228
  85.5 1.6 %collective-permute-start.18 = (f32[4,4096]{1,0:T(4,128)S(1)}, f32[4,4096]{1,0:T(4,128)S(1)}, u32[]{:S(2)}, u32[]{:S(2)}) collective-permute-start(f32[4,4096]{1,0:T(4,128)S(1)} %fusion.21), channel_id=1, source_target_pairs={{0,16},{16,32},{32,48},{48,64},{64,80},{80,96},{96,112},{112,0},{1... | collective-permute-start | bytes 196616 | tf_op jit(solution)/shard_map/ppermute | solution.py:173
  87.0 2.6 %collective-permute-start.19 = (f32[4,4096]{1,0:T(4,128)S(1)}, f32[4,4096]{1,0:T(4,128)S(1)}, u32[]{:S(2)}, u32[]{:S(2)}) collective-permute-start(f32[4,4096]{1,0:T(4,128)S(1)} %fusion.21), channel_id=1, source_target_pairs={{0,32},{16,48},{32,64},{48,80},{64,96},{80,112},{96,0},{112,16},{1... | collective-permute-start | bytes 196616 | tf_op jit(solution)/shard_map/ppermute | solution.py:173
  89.7 3.3 %collective-permute-start.20 = (f32[4,4096]{1,0:T(4,128)S(1)}, f32[4,4096]{1,0:T(4,128)S(1)}, u32[]{:S(2)}, u32[]{:S(2)}) collective-permute-start(f32[4,4096]{1,0:T(4,128)S(1)} %fusion.21), channel_id=1, source_target_pairs={{0,48},{16,64},{32,80},{48,96},{64,112},{80,0},{96,16},{112,32},{1... | collective-permute-start | bytes 196616 | tf_op jit(solution)/shard_map/ppermute | solution.py:173
  93.0 1.0 collective-permute-start.21
  94.0 3.7 %collective-permute-start.22 = (f32[4,4096]{1,0:T(4,128)S(1)}, f32[4,4096]{1,0:T(4,128)S(1)}, u32[]{:S(2)}, u32[]{:S(2)}) collective-permute-start(f32[4,4096]{1,0:T(4,128)S(1)} %fusion.21), channel_id=1, source_target_pairs={{0,80},{16,96},{32,112},{48,0},{64,16},{80,32},{96,48},{112,64},{1... | collective-permute-start | bytes 196616 | tf_op jit(solution)/shard_map/ppermute | solution.py:173
  97.7 2.8 %collective-permute-start.23 = (f32[4,4096]{1,0:T(4,128)S(1)}, f32[4,4096]{1,0:T(4,128)S(1)}, u32[]{:S(2)}, u32[]{:S(2)}) collective-permute-start(f32[4,4096]{1,0:T(4,128)S(1)} %fusion.21), channel_id=1, source_target_pairs={{0,96},{16,112},{32,0},{48,16},{64,32},{80,48},{96,64},{112,80},{1... | collective-permute-start | bytes 196616 | tf_op jit(solution)/shard_map/ppermute | solution.py:173
  100.5 0.9 collective-permute-start.24
  103.9 3.9 %collective-permute-done.23 = f32[4,4096]{1,0:T(4,128)S(1)} collective-permute-done((f32[4,4096]{1,0:T(4,128)S(1)}, f32[4,4096]{1,0:T(4,128)S(1)}, u32[]{:S(2)}, u32[]{:S(2)}) %collective-permute-start.23) | collective-permute-done | bytes 65568 | tf_op jit(solution)/shard_map/ppermute | solution.py:173
  108.2 2.8 %collective-permute-start.31 = (bf16[32,2048]{1,0:T(8,128)(2,1)S(1)}, bf16[32,2048]{1,0:T(8,128)(2,1)S(1)}, u32[]{:S(2)}, u32[]{:S(2)}) collective-permute-start(bf16[32,2048]{1,0:T(8,128)(2,1)S(1)} %get-tuple-element.54), channel_id=1, source_target_pairs={{0,128},{128,0},{1,129},{129,1},{2,130},{130,2},{3,131},{131,3},{4... | collective-permute-start | bytes 393224 | tf_op jit(solution)/shard_map/ppermute | solution.py:173
  111.0 1.9 %collective-permute-start.17 = (f32[2,4096]{1,0:T(2,128)S(1)}, f32[2,4096]{1,0:T(2,128)S(1)}, u32[]{:S(2)}, u32[]{:S(2)}) collective-permute-start(f32[2,4096]{1,0:T(2,128)S(1)} %constant_dynamic-slice_fusion), channel_id=1, source_target_pairs={{0,2},{2,0},{1,3},{3,1},{4,6},{6,4},{5,7},{7,5},{8,10},{10,8},{9,1... | collective-permute-start | bytes 98312 | tf_op jit(solution)/shard_map/ppermute | solution.py:173
  112.9 1.2 collective-permute-start.25
  114.2 2.5 %collective-permute-start.26 = (bf16[32,2048]{1,0:T(8,128)(2,1)S(1)}, bf16[32,2048]{1,0:T(8,128)(2,1)S(1)}, u32[]{:S(2)}, u32[]{:S(2)}) collective-permute-start(bf16[32,2048]{1,0:T(8,128)(2,1)S(1)} %get-tuple-element.55), channel_id=1, source_target_pairs={{0,8},{4,12},{8,0},{12,4},{1,9},{5,13},{9,1},{13,5},{2,10},{6,14},... | collective-permute-start | bytes 393224 | tf_op jit(solution)/shard_map/ppermute | solution.py:173
  116.7 1.1 collective-permute-start.27
  119.1 1.6 %collective-permute-start.33 = (bf16[64,2048]{1,0:T(8,128)(2,1)S(1)}, bf16[64,2048]{1,0:T(8,128)(2,1)S(1)}, u32[]{:S(2)}, u32[]{:S(2)}) collective-permute-start(bf16[64,2048]{1,0:T(8,128)(2,1)S(1)} %pad_maximum_fusion.2.refs_0_), channel_id=1, source_target_pairs={{0,8},{4,12},{8,0},{12,4},{1,9},{5,13},{9,1},{13,5},{2,10},{6,14},... | collective-permute-start | bytes 786440 | tf_op jit(solution)/shard_map/ppermute | solution.py:173
  120.7 2.3 %collective-permute-done.26 = bf16[32,2048]{1,0:T(8,128)(2,1)S(1)} collective-permute-done((bf16[32,2048]{1,0:T(8,128)(2,1)S(1)}, bf16[32,2048]{1,0:T(8,128)(2,1)S(1)}, u32[]{:S(2)}, u32[]{:S(2)}) %collective-permute-start.26) | collective-permute-done | bytes 131104 | tf_op jit(solution)/shard_map/ppermute | solution.py:173
  123.0 1.6 %collective-permute-start.35 = (bf16[64,2048]{1,0:T(8,128)(2,1)S(1)}, bf16[64,2048]{1,0:T(8,128)(2,1)S(1)}, u32[]{:S(2)}, u32[]{:S(2)}) collective-permute-start(bf16[64,2048]{1,0:T(8,128)(2,1)S(1)} %pad_maximum_fusion.2.refs_0_), channel_id=1, source_target_pairs={{0,2},{2,0},{1,3},{3,1},{4,6},{6,4},{5,7},{7,5},{8,10},{10,8},{9,1... | collective-permute-start | bytes 786440 | tf_op jit(solution)/shard_map/ppermute | solution.py:173
  125.0 4.5 %collective-permute-done.32.refs_1_ = bf16[64,2048]{1,0:T(8,128)(2,1)S(1)} collective-permute-done((bf16[64,2048]{1,0:T(8,128)(2,1)S(1)}, bf16[64,2048]{1,0:T(8,128)(2,1)S(1)}, u32[]{:S(2)}, u32[]{:S(2)}) %collective-permute-start.32) | collective-permute-done | bytes 262176 | tf_op jit(solution)/shard_map/ppermute | solution.py:173
  130.1 4.1 %collective-permute-done.33.refs_2_ = bf16[64,2048]{1,0:T(8,128)(2,1)S(1)} collective-permute-done((bf16[64,2048]{1,0:T(8,128)(2,1)S(1)}, bf16[64,2048]{1,0:T(8,128)(2,1)S(1)}, u32[]{:S(2)}, u32[]{:S(2)}) %collective-permute-start.33) | collective-permute-done | bytes 262176 | tf_op jit(solution)/shard_map/ppermute | solution.py:173
  134.2 0.9 collective-permute-start.36
  135.7 4.0 %collective-permute-done.28.refs_1_ = bf16[128,2048]{1,0:T(8,128)(2,1)S(1)} collective-permute-done((bf16[128,2048]{1,0:T(8,128)(2,1)S(1)}, bf16[128,2048]{1,0:T(8,128)(2,1)S(1)}, u32[]{:S(2)}, u32[]{:S(2)}) %collective-permute-start.28) | collective-permute-done | bytes 524320 | tf_op jit(solution)/shard_map/ppermute | solution.py:173
  141.3 2.6 %from_blocks.2.refs_4_ = bf16[256,8192]{1,0:T(8,128)(2,1)} custom-call(s32[1]{0:T(128)} %bitcast.2.core, bf16[256,256]{1,0:T(8,128)(2,1)S(1)} %fusion.4.one, bf16[64,2048]{1,0:T(8,128)(2,1)S(1)} %pad_maximum_fusion.2.refs_0_, bf16[64,2048]{1,0:T(8,128)(2,1)S(1)} %collective-permute-done.32.refs_1_, bf16[64,2048]{1,0:T(8,128)(2,1)S(1)} %collective-permute-done.33.refs_2_, ...), custom_call_target="tpu_custom_call" | custom-call | tf_op jit(solution)/shard_map/from_blocks/pallas_call | solution.py:144
  144.0 2.6 %from_blocks.3 = bf16[256,8192]{1,0:T(8,128)(2,1)} custom-call(s32[1]{0:T(128)} %bitcast.2.core, bf16[256,256]{1,0:T(8,128)(2,1)S(1)} %fusion.3.one, bf16[128,2048]{1,0:T(8,128)(2,1)S(1)} %pad_maximum_fusion.1.refs_0_, bf16[128,2048]{1,0:T(8,128)(2,1)S(1)} %collective-permute-done.28.refs_1_, ...), custom_call_target="tpu_custom_call", output_to_operand_aliasing={{}: (6, {})} | custom-call | tf_op jit(solution)/shard_map/from_blocks/pallas_call | solution.py:144
  (78 shorter events, 12.7 us)
Async XLA Ops:
  3.7 7.3 %collective-permute-start = (bf16[256,4096]{1,0:T(8,128)(2,1)}, bf16[256,4096]{1,0:T(8,128)(2,1)S(1)}, u32[]{:S(2)}, u32[]{:S(2)}) collective-permute-start(bf16[256,4096]{1,0:T(8,128)(2,1)} %pick.1), channel_id=1, source_target_pairs={{0,2},{2,0},{1,3},{3,1},{4,6},{6,4},{5,7},{7,5},{8,10},{10,8},{9,1... | collective-permute-start | bytes 6291464 | tf_op jit(solution)/shard_map/ppermute | solution.py:173
  10.0 1.8 %copy-start = (f32[1,2,8192]{2,1,0:T(2,128)S(1)}, f32[1,2,8192]{2,1,0:T(2,128)}, u32[]{:S(2)}) copy-start(f32[1,2,8192]{2,1,0:T(2,128)} %param.6) | copy-start | bytes 196612
  10.1 1.8 %copy-start.1 = (f32[1,2,8192]{2,1,0:T(2,128)S(1)}, f32[1,2,8192]{2,1,0:T(2,128)}, u32[]{:S(2)}) copy-start(f32[1,2,8192]{2,1,0:T(2,128)} %param.7) | copy-start | bytes 196612
  12.1 7.2 %collective-permute-start.16 = (f32[2,4096]{1,0:T(2,128)S(1)}, f32[2,4096]{1,0:T(2,128)S(1)}, u32[]{:S(2)}, u32[]{:S(2)}) collective-permute-start(f32[2,4096]{1,0:T(2,128)S(1)} %dynamic-slice_bitcast_fusion), channel_id=1, source_target_pairs={{0,2},{2,0},{1,3},{3,1},{4,6},{6,4},{5,7},{7,5},{8,10},{10,8},{9,1... | collective-permute-start | bytes 98312 | tf_op jit(solution)/shard_map/ppermute | solution.py:173
  12.6 9.4 %collective-permute-start.1 = (f16[64,2048]{1,0:T(8,128)(2,1)S(1)}, f16[64,2048]{1,0:T(8,128)(2,1)S(1)}, u32[]{:S(2)}, u32[]{:S(2)}) collective-permute-start(f16[64,2048]{1,0:T(8,128)(2,1)S(1)} %convert_element_type.116), channel_id=1, source_target_pairs={{0,8},{4,12},{8,0},{12,4},{1,9},{5,13},{9,1},{13,5},{2,10},{6,14},... | collective-permute-start | bytes 786440 | tf_op jit(solution)/shard_map/ppermute | solution.py:173
  13.8 14.2 %collective-permute-start.2 = (f16[64,2048]{1,0:T(8,128)(2,1)S(1)}, f16[64,2048]{1,0:T(8,128)(2,1)S(1)}, u32[]{:S(2)}, u32[]{:S(2)}) collective-permute-start(f16[64,2048]{1,0:T(8,128)(2,1)S(1)} %convert_element_type.118), channel_id=1, source_target_pairs={{0,4},{4,8},{8,12},{12,0},{1,5},{5,9},{9,13},{13,1},{2,6},{6,10},{... | collective-permute-start | bytes 786440 | tf_op jit(solution)/shard_map/ppermute | solution.py:173
  14.2 13.8 %collective-permute-start.3 = (f16[64,2048]{1,0:T(8,128)(2,1)S(1)}, f16[64,2048]{1,0:T(8,128)(2,1)S(1)}, u32[]{:S(2)}, u32[]{:S(2)}) collective-permute-start(f16[64,2048]{1,0:T(8,128)(2,1)S(1)} %convert_element_type.120), channel_id=1, source_target_pairs={{0,12},{4,0},{8,4},{12,8},{1,13},{5,1},{9,5},{13,9},{2,14},{6,2},{... | collective-permute-start | bytes 786440 | tf_op jit(solution)/shard_map/ppermute | solution.py:173
  16.5 14.0 %collective-permute-start.5 = (f16[128,2048]{1,0:T(8,128)(2,1)S(1)}, f16[128,2048]{1,0:T(8,128)(2,1)S(1)}, u32[]{:S(2)}, u32[]{:S(2)}) collective-permute-start(f16[128,2048]{1,0:T(8,128)(2,1)S(1)} %convert_element_type.125), channel_id=1, source_target_pairs={{0,128},{128,0},{1,129},{129,1},{2,130},{130,2},{3,131},{131,3},{4... | collective-permute-start | bytes 1572872 | tf_op jit(solution)/shard_map/ppermute | solution.py:173
  28.2 6.2 %collective-permute-start.4 = (f16[32,2048]{1,0:T(8,128)(2,1)S(1)}, f16[32,2048]{1,0:T(8,128)(2,1)S(1)}, u32[]{:S(2)}, u32[]{:S(2)}) collective-permute-start(f16[32,2048]{1,0:T(8,128)(2,1)S(1)} %slice_convert_fusion), channel_id=1, source_target_pairs={{0,128},{128,0},{1,129},{129,1},{2,130},{130,2},{3,131},{131,3},{4... | collective-permute-start | bytes 393224 | tf_op jit(solution)/shard_map/ppermute | solution.py:173
  30.8 5.5 %collective-permute-start.6 = (f16[32,2048]{1,0:T(8,128)(2,1)S(1)}, f16[32,2048]{1,0:T(8,128)(2,1)S(1)}, u32[]{:S(2)}, u32[]{:S(2)}) collective-permute-start(f16[32,2048]{1,0:T(8,128)(2,1)S(1)} %get-tuple-element.51), channel_id=1, source_target_pairs={{0,8},{4,12},{8,0},{12,4},{1,9},{5,13},{9,1},{13,5},{2,10},{6,14},... | collective-permute-start | bytes 393224 | tf_op jit(solution)/shard_map/ppermute | solution.py:173
  31.4 8.0 %collective-permute-start.7 = (f16[32,2048]{1,0:T(8,128)(2,1)S(1)}, f16[32,2048]{1,0:T(8,128)(2,1)S(1)}, u32[]{:S(2)}, u32[]{:S(2)}) collective-permute-start(f16[32,2048]{1,0:T(8,128)(2,1)S(1)} %get-tuple-element.53), channel_id=1, source_target_pairs={{0,4},{4,8},{8,12},{12,0},{1,5},{5,9},{9,13},{13,1},{2,6},{6,10},{... | collective-permute-start | bytes 393224 | tf_op jit(solution)/shard_map/ppermute | solution.py:173
  32.9 6.5 %collective-permute-start.8 = (f16[32,2048]{1,0:T(8,128)(2,1)S(1)}, f16[32,2048]{1,0:T(8,128)(2,1)S(1)}, u32[]{:S(2)}, u32[]{:S(2)}) collective-permute-start(f16[32,2048]{1,0:T(8,128)(2,1)S(1)} %get-tuple-element.52), channel_id=1, source_target_pairs={{0,12},{4,0},{8,4},{12,8},{1,13},{5,1},{9,5},{13,9},{2,14},{6,2},{... | collective-permute-start | bytes 393224 | tf_op jit(solution)/shard_map/ppermute | solution.py:173
  39.7 17.3 %collective-permute-start.10 = (f16[4,4096]{1,0:T(4,128)(2,1)S(1)}, f16[4,4096]{1,0:T(4,128)(2,1)S(1)}, u32[]{:S(2)}, u32[]{:S(2)}) collective-permute-start(f16[4,4096]{1,0:T(4,128)(2,1)S(1)} %get-tuple-element.62), channel_id=1, source_target_pairs={{0,48},{16,64},{32,80},{48,96},{64,112},{80,0},{96,16},{112,32},{1... | collective-permute-start | bytes 98312 | tf_op jit(solution)/shard_map/ppermute | solution.py:173
  42.7 15.5 %collective-permute-start.11 = (f16[4,4096]{1,0:T(4,128)(2,1)S(1)}, f16[4,4096]{1,0:T(4,128)(2,1)S(1)}, u32[]{:S(2)}, u32[]{:S(2)}) collective-permute-start(f16[4,4096]{1,0:T(4,128)(2,1)S(1)} %get-tuple-element.61), channel_id=1, source_target_pairs={{0,80},{16,96},{32,112},{48,0},{64,16},{80,32},{96,48},{112,64},{1... | collective-permute-start | bytes 98312 | tf_op jit(solution)/shard_map/ppermute | solution.py:173
  45.8 22.5 %all-to-all-start = ((f32[8,4,4096]{2,1,0:T(4,128)}), f32[8,4,4096]{2,1,0:T(4,128)S(1)}, u32[]{:S(2)}, u32[]{:S(2)}) async-start(f32[8,4,4096]{2,1,0:T(4,128)} %broadcast_in_dim.33), calls=%async_computation | async-start | bytes 1048576 | tf_op jit(solution)/shard_map/all_to_all | solution.py:206
  52.0 12.4 %collective-permute-start.12 = (f16[4,4096]{1,0:T(4,128)(2,1)S(1)}, f16[4,4096]{1,0:T(4,128)(2,1)S(1)}, u32[]{:S(2)}, u32[]{:S(2)}) collective-permute-start(f16[4,4096]{1,0:T(4,128)(2,1)S(1)} %get-tuple-element.60), channel_id=1, source_target_pairs={{0,32},{16,48},{32,64},{48,80},{64,96},{80,112},{96,0},{112,16},{1... | collective-permute-start | bytes 98312 | tf_op jit(solution)/shard_map/ppermute | solution.py:173
  54.3 10.1 %collective-permute-start.13 = (f16[4,4096]{1,0:T(4,128)(2,1)S(1)}, f16[4,4096]{1,0:T(4,128)(2,1)S(1)}, u32[]{:S(2)}, u32[]{:S(2)}) collective-permute-start(f16[4,4096]{1,0:T(4,128)(2,1)S(1)} %get-tuple-element.59), channel_id=1, source_target_pairs={{0,96},{16,112},{32,0},{48,16},{64,32},{80,48},{96,64},{112,80},{1... | collective-permute-start | bytes 98312 | tf_op jit(solution)/shard_map/ppermute | solution.py:173
  55.5 8.8 %collective-permute-start.14 = (f16[4,4096]{1,0:T(4,128)(2,1)S(1)}, f16[4,4096]{1,0:T(4,128)(2,1)S(1)}, u32[]{:S(2)}, u32[]{:S(2)}) collective-permute-start(f16[4,4096]{1,0:T(4,128)(2,1)S(1)} %get-tuple-element.58), channel_id=1, source_target_pairs={{0,16},{16,32},{32,48},{48,64},{64,80},{80,96},{96,112},{112,0},{1... | collective-permute-start | bytes 98312 | tf_op jit(solution)/shard_map/ppermute | solution.py:173
  57.0 7.4 %collective-permute-start.15 = (f16[4,4096]{1,0:T(4,128)(2,1)S(1)}, f16[4,4096]{1,0:T(4,128)(2,1)S(1)}, u32[]{:S(2)}, u32[]{:S(2)}) collective-permute-start(f16[4,4096]{1,0:T(4,128)(2,1)S(1)} %get-tuple-element.57), channel_id=1, source_target_pairs={{0,112},{16,0},{32,16},{48,32},{64,48},{80,64},{96,80},{112,96},{1... | collective-permute-start | bytes 98312 | tf_op jit(solution)/shard_map/ppermute | solution.py:173
  58.2 10.0 %collective-permute-start.9 = (f16[4,4096]{1,0:T(4,128)(2,1)S(1)}, f16[4,4096]{1,0:T(4,128)(2,1)S(1)}, u32[]{:S(2)}, u32[]{:S(2)}) collective-permute-start(f16[4,4096]{1,0:T(4,128)(2,1)S(1)} %get-tuple-element.56), channel_id=1, source_target_pairs={{0,64},{16,80},{32,96},{48,112},{64,0},{80,16},{96,32},{112,48},{1... | collective-permute-start | bytes 98312 | tf_op jit(solution)/shard_map/ppermute | solution.py:173
  70.3 31.1 %all-to-all-start.1 = ((f32[256,1,128]{2,1,0:T(1,128)}), f32[256,1,128]{2,1,0:T(1,128)S(1)}, u32[]{:S(2)}, u32[]{:S(2)}) async-start(f32[256,1,128]{2,1,0:T(1,128)} %broadcast_in_dim.34), calls=%async_computation.1 | async-start | bytes 262144 | tf_op jit(solution)/shard_map/all_to_all | solution.py:228
  85.5 12.3 %collective-permute-start.18 = (f32[4,4096]{1,0:T(4,128)S(1)}, f32[4,4096]{1,0:T(4,128)S(1)}, u32[]{:S(2)}, u32[]{:S(2)}) collective-permute-start(f32[4,4096]{1,0:T(4,128)S(1)} %fusion.21), channel_id=1, source_target_pairs={{0,16},{16,32},{32,48},{48,64},{64,80},{80,96},{96,112},{112,0},{1... | collective-permute-start | bytes 196616 | tf_op jit(solution)/shard_map/ppermute | solution.py:173
  87.0 13.5 %collective-permute-start.19 = (f32[4,4096]{1,0:T(4,128)S(1)}, f32[4,4096]{1,0:T(4,128)S(1)}, u32[]{:S(2)}, u32[]{:S(2)}) collective-permute-start(f32[4,4096]{1,0:T(4,128)S(1)} %fusion.21), channel_id=1, source_target_pairs={{0,32},{16,48},{32,64},{48,80},{64,96},{80,112},{96,0},{112,16},{1... | collective-permute-start | bytes 196616 | tf_op jit(solution)/shard_map/ppermute | solution.py:173
  89.7 13.3 %collective-permute-start.20 = (f32[4,4096]{1,0:T(4,128)S(1)}, f32[4,4096]{1,0:T(4,128)S(1)}, u32[]{:S(2)}, u32[]{:S(2)}) collective-permute-start(f32[4,4096]{1,0:T(4,128)S(1)} %fusion.21), channel_id=1, source_target_pairs={{0,48},{16,64},{32,80},{48,96},{64,112},{80,0},{96,16},{112,32},{1... | collective-permute-start | bytes 196616 | tf_op jit(solution)/shard_map/ppermute | solution.py:173
  93.0 10.0 %collective-permute-start.21 = (f32[4,4096]{1,0:T(4,128)S(1)}, f32[4,4096]{1,0:T(4,128)S(1)}, u32[]{:S(2)}, u32[]{:S(2)}) collective-permute-start(f32[4,4096]{1,0:T(4,128)S(1)} %fusion.21), channel_id=1, source_target_pairs={{0,64},{16,80},{32,96},{48,112},{64,0},{80,16},{96,32},{112,48},{1... | collective-permute-start | bytes 196616 | tf_op jit(solution)/shard_map/ppermute | solution.py:173
  94.0 9.9 %collective-permute-start.22 = (f32[4,4096]{1,0:T(4,128)S(1)}, f32[4,4096]{1,0:T(4,128)S(1)}, u32[]{:S(2)}, u32[]{:S(2)}) collective-permute-start(f32[4,4096]{1,0:T(4,128)S(1)} %fusion.21), channel_id=1, source_target_pairs={{0,80},{16,96},{32,112},{48,0},{64,16},{80,32},{96,48},{112,64},{1... | collective-permute-start | bytes 196616 | tf_op jit(solution)/shard_map/ppermute | solution.py:173
  97.7 10.0 %collective-permute-start.23 = (f32[4,4096]{1,0:T(4,128)S(1)}, f32[4,4096]{1,0:T(4,128)S(1)}, u32[]{:S(2)}, u32[]{:S(2)}) collective-permute-start(f32[4,4096]{1,0:T(4,128)S(1)} %fusion.21), channel_id=1, source_target_pairs={{0,96},{16,112},{32,0},{48,16},{64,32},{80,48},{96,64},{112,80},{1... | collective-permute-start | bytes 196616 | tf_op jit(solution)/shard_map/ppermute | solution.py:173
  100.5 7.3 %collective-permute-start.24 = (f32[4,4096]{1,0:T(4,128)S(1)}, f32[4,4096]{1,0:T(4,128)S(1)}, u32[]{:S(2)}, u32[]{:S(2)}) collective-permute-start(f32[4,4096]{1,0:T(4,128)S(1)} %fusion.21), channel_id=1, source_target_pairs={{0,112},{16,0},{32,16},{48,32},{64,48},{80,64},{96,80},{112,96},{1... | collective-permute-start | bytes 196616 | tf_op jit(solution)/shard_map/ppermute | solution.py:173
  108.2 9.6 %collective-permute-start.31 = (bf16[32,2048]{1,0:T(8,128)(2,1)S(1)}, bf16[32,2048]{1,0:T(8,128)(2,1)S(1)}, u32[]{:S(2)}, u32[]{:S(2)}) collective-permute-start(bf16[32,2048]{1,0:T(8,128)(2,1)S(1)} %get-tuple-element.54), channel_id=1, source_target_pairs={{0,128},{128,0},{1,129},{129,1},{2,130},{130,2},{3,131},{131,3},{4... | collective-permute-start | bytes 393224 | tf_op jit(solution)/shard_map/ppermute | solution.py:173
  111.0 13.6 %collective-permute-start.17 = (f32[2,4096]{1,0:T(2,128)S(1)}, f32[2,4096]{1,0:T(2,128)S(1)}, u32[]{:S(2)}, u32[]{:S(2)}) collective-permute-start(f32[2,4096]{1,0:T(2,128)S(1)} %constant_dynamic-slice_fusion), channel_id=1, source_target_pairs={{0,2},{2,0},{1,3},{3,1},{4,6},{6,4},{5,7},{7,5},{8,10},{10,8},{9,1... | collective-permute-start | bytes 98312 | tf_op jit(solution)/shard_map/ppermute | solution.py:173
  112.9 6.2 %collective-permute-start.25 = (bf16[32,2048]{1,0:T(8,128)(2,1)S(1)}, bf16[32,2048]{1,0:T(8,128)(2,1)S(1)}, u32[]{:S(2)}, u32[]{:S(2)}) collective-permute-start(bf16[32,2048]{1,0:T(8,128)(2,1)S(1)} %get-tuple-element.55), channel_id=1, source_target_pairs={{0,4},{4,8},{8,12},{12,0},{1,5},{5,9},{9,13},{13,1},{2,6},{6,10},{... | collective-permute-start | bytes 393224 | tf_op jit(solution)/shard_map/ppermute | solution.py:173
  114.2 8.8 %collective-permute-start.26 = (bf16[32,2048]{1,0:T(8,128)(2,1)S(1)}, bf16[32,2048]{1,0:T(8,128)(2,1)S(1)}, u32[]{:S(2)}, u32[]{:S(2)}) collective-permute-start(bf16[32,2048]{1,0:T(8,128)(2,1)S(1)} %get-tuple-element.55), channel_id=1, source_target_pairs={{0,8},{4,12},{8,0},{12,4},{1,9},{5,13},{9,1},{13,5},{2,10},{6,14},... | collective-permute-start | bytes 393224 | tf_op jit(solution)/shard_map/ppermute | solution.py:173
  116.7 6.3 %collective-permute-start.27 = (bf16[32,2048]{1,0:T(8,128)(2,1)S(1)}, bf16[32,2048]{1,0:T(8,128)(2,1)S(1)}, u32[]{:S(2)}, u32[]{:S(2)}) collective-permute-start(bf16[32,2048]{1,0:T(8,128)(2,1)S(1)} %get-tuple-element.55), channel_id=1, source_target_pairs={{0,12},{4,0},{8,4},{12,8},{1,13},{5,1},{9,5},{13,9},{2,14},{6,2},{... | collective-permute-start | bytes 393224 | tf_op jit(solution)/shard_map/ppermute | solution.py:173
  117.8 11.7 %collective-permute-start.32 = (bf16[64,2048]{1,0:T(8,128)(2,1)S(1)}, bf16[64,2048]{1,0:T(8,128)(2,1)S(1)}, u32[]{:S(2)}, u32[]{:S(2)}) collective-permute-start(bf16[64,2048]{1,0:T(8,128)(2,1)S(1)} %pad_maximum_fusion.2.refs_0_), channel_id=1, source_target_pairs={{0,4},{4,8},{8,12},{12,0},{1,5},{5,9},{9,13},{13,1},{2,6},{6,10},{... | collective-permute-start | bytes 786440 | tf_op jit(solution)/shard_map/ppermute | solution.py:173
  119.1 15.1 %collective-permute-start.33 = (bf16[64,2048]{1,0:T(8,128)(2,1)S(1)}, bf16[64,2048]{1,0:T(8,128)(2,1)S(1)}, u32[]{:S(2)}, u32[]{:S(2)}) collective-permute-start(bf16[64,2048]{1,0:T(8,128)(2,1)S(1)} %pad_maximum_fusion.2.refs_0_), channel_id=1, source_target_pairs={{0,8},{4,12},{8,0},{12,4},{1,9},{5,13},{9,1},{13,5},{2,10},{6,14},... | collective-permute-start | bytes 786440 | tf_op jit(solution)/shard_map/ppermute | solution.py:173
  123.0 12.2 %collective-permute-start.34 = (bf16[64,2048]{1,0:T(8,128)(2,1)S(1)}, bf16[64,2048]{1,0:T(8,128)(2,1)S(1)}, u32[]{:S(2)}, u32[]{:S(2)}) collective-permute-start(bf16[64,2048]{1,0:T(8,128)(2,1)S(1)} %pad_maximum_fusion.2.refs_0_), channel_id=1, source_target_pairs={{0,12},{4,0},{8,4},{12,8},{1,13},{5,1},{9,5},{13,9},{2,14},{6,2},{... | collective-permute-start | bytes 786440 | tf_op jit(solution)/shard_map/ppermute | solution.py:173
  123.0 12.2 %collective-permute-start.35 = (bf16[64,2048]{1,0:T(8,128)(2,1)S(1)}, bf16[64,2048]{1,0:T(8,128)(2,1)S(1)}, u32[]{:S(2)}, u32[]{:S(2)}) collective-permute-start(bf16[64,2048]{1,0:T(8,128)(2,1)S(1)} %pad_maximum_fusion.2.refs_0_), channel_id=1, source_target_pairs={{0,2},{2,0},{1,3},{3,1},{4,6},{6,4},{5,7},{7,5},{8,10},{10,8},{9,1... | collective-permute-start | bytes 786440 | tf_op jit(solution)/shard_map/ppermute | solution.py:173
  124.6 15.1 %collective-permute-start.28 = (bf16[128,2048]{1,0:T(8,128)(2,1)S(1)}, bf16[128,2048]{1,0:T(8,128)(2,1)S(1)}, u32[]{:S(2)}, u32[]{:S(2)}) collective-permute-start(bf16[128,2048]{1,0:T(8,128)(2,1)S(1)} %pad_maximum_fusion.1.refs_0_), channel_id=1, source_target_pairs={{0,128},{128,0},{1,129},{129,1},{2,130},{130,2},{3,131},{131,3},{4... | collective-permute-start | bytes 1572872 | tf_op jit(solution)/shard_map/ppermute | solution.py:173
  129.5 14.5 %collective-permute-start.29 = (bf16[128,2048]{1,0:T(8,128)(2,1)S(1)}, bf16[128,2048]{1,0:T(8,128)(2,1)S(1)}, u32[]{:S(2)}, u32[]{:S(2)}) collective-permute-start(bf16[128,2048]{1,0:T(8,128)(2,1)S(1)} %pad_maximum_fusion.1.refs_0_), channel_id=1, source_target_pairs={{0,2},{2,0},{1,3},{3,1},{4,6},{6,4},{5,7},{7,5},{8,10},{10,8},{9,1... | collective-permute-start | bytes 1572872 | tf_op jit(solution)/shard_map/ppermute | solution.py:173
  134.2 7.1 %collective-permute-start.36 = (bf16[64,2048]{1,0:T(8,128)(2,1)S(1)}, bf16[64,2048]{1,0:T(8,128)(2,1)S(1)}, u32[]{:S(2)}, u32[]{:S(2)}) collective-permute-start(bf16[64,2048]{1,0:T(8,128)(2,1)S(1)} %collective-permute-done.32.refs_1_), channel_id=1, source_target_pairs={{0,2},{2,0},{1,3},{3,1},{4,6},{6,4},{5,7},{7,5},{8,10},{10,8},{9,1... | collective-permute-start | bytes 786440 | tf_op jit(solution)/shard_map/ppermute | solution.py:173
  135.2 6.2 %collective-permute-start.37 = (bf16[64,2048]{1,0:T(8,128)(2,1)S(1)}, bf16[64,2048]{1,0:T(8,128)(2,1)S(1)}, u32[]{:S(2)}, u32[]{:S(2)}) collective-permute-start(bf16[64,2048]{1,0:T(8,128)(2,1)S(1)} %collective-permute-done.33.refs_2_), channel_id=1, source_target_pairs={{0,2},{2,0},{1,3},{3,1},{4,6},{6,4},{5,7},{7,5},{8,10},{10,8},{9,1... | collective-permute-start | bytes 786440 | tf_op jit(solution)/shard_map/ppermute | solution.py:173
  135.2 6.1 %collective-permute-start.38 = (bf16[64,2048]{1,0:T(8,128)(2,1)S(1)}, bf16[64,2048]{1,0:T(8,128)(2,1)S(1)}, u32[]{:S(2)}, u32[]{:S(2)}) collective-permute-start(bf16[64,2048]{1,0:T(8,128)(2,1)S(1)} %collective-permute-done.34.refs_3_), channel_id=1, source_target_pairs={{0,2},{2,0},{1,3},{3,1},{4,6},{6,4},{5,7},{7,5},{8,10},{10,8},{9,1... | collective-permute-start | bytes 786440 | tf_op jit(solution)/shard_map/ppermute | solution.py:173
  139.7 4.3 %collective-permute-start.30 = (bf16[128,2048]{1,0:T(8,128)(2,1)S(1)}, bf16[128,2048]{1,0:T(8,128)(2,1)S(1)}, u32[]{:S(2)}, u32[]{:S(2)}) collective-permute-start(bf16[128,2048]{1,0:T(8,128)(2,1)S(1)} %collective-permute-done.28.refs_1_), channel_id=1, source_target_pairs={{0,2},{2,0},{1,3},{3,1},{4,6},{6,4},{5,7},{7,5},{8,10},{10,8},{9,1... | collective-permute-start | bytes 1572872 | tf_op jit(solution)/shard_map/ppermute | solution.py:173

commit v3 on v1

--- a/solution.py
+++ b/solution.py
@@ -92,30 +92,21 @@
 
 
 def to_blocks_kernel(one, own, other, *outs):
-    *by_y, near, far = outs
-    half, per = other.shape[1], by_y[0].shape[0]
-    edge = by_y[0].shape[1]
+    half, per = other.shape[1], outs[0].shape[0]
     for at in range(0, half, WIDTH):
         here = slice(at, at + WIDTH)
         s = own[:, here] - jnp.dot(one[...], other[:, here], preferred_element_type=jnp.float32)
-        for j in range(len(by_y)):
-            block = s[j * per : (j + 1) * per]
-            if at < edge:
-                by_y[j][:, here] = block
-            else:
-                to = slice(j * per // 2, (j + 1) * per // 2), slice(at - edge, at - edge + WIDTH)
-                near[to] = block[: per // 2]
-                far[to] = block[per // 2 :]
+        for i, out in enumerate(outs):
+            out[:, here] = s[i * per : (i + 1) * per]
 
 
 def to_blocks(one, own, other, n):
     rows, half = other.shape
-    shapes = [(rows // n, half // 2)] * n + [(rows // 2, half // 2)] * 2
     return pl.pallas_call(
         to_blocks_kernel,
         in_specs=[VMEM, VMEM, VMEM],
-        out_specs=[VMEM] * len(shapes),
-        out_shape=[jax.ShapeDtypeStruct(s, jnp.float32) for s in shapes],
+        out_specs=[VMEM] * n,
+        out_shape=[jax.ShapeDtypeStruct((rows // n, half), jnp.float32)] * n,
         compiler_params=pltpu.CompilerParams(vmem_limit_bytes=6 * MIB),
         name="to_blocks",
     )(one, own, other)
@@ -172,6 +163,10 @@
     def send(x, axis, by):
         return lax.ppermute(x, axis, shift(axis, by))
 
+    def send_xy(x, h, j):
+        moves = [(a, (a // ny + h) % nx * ny + (a + j) % ny) for a in range(nx * ny)]
+        return lax.ppermute(x, ("xh", "y"), moves)
+
     def part(x, row, col):
         return lax.dynamic_slice(x, (row, col), (2, half), allow_negative_indices=False)
 
@@ -179,48 +174,33 @@
         return x.astype(jnp.float32)
 
     o = jnp.arange(rows)
-    q, z, h, j = o % 4, o // 4 % nz, o // (4 * nz) % nx, o // (4 * nz * nx)
+    q, z, j, h = o % 4, o // 4 % nz, o // (4 * nz) % ny, o // (4 * nz * ny)
     to = row_of(j, h, z, q, 1)[:, None] == o[None]
-    z = (lax.axis_index("z") - z) % nz
+    back_x = o[:, None] == row_of(j, h, z, q, -1)[None]
+    j, h = o // (4 * nz * nx), o // (4 * nz) % nx
     back_y = o[:, None] == row_of(j, h, z, q, -1)[None]
-    j, h = o // (4 * nz) % ny, o // (4 * nz * ny)
-    back_x = o[:, None] == row_of(j, h, z, q, -1)[None]
 
     to = jnp.where(to, SCALE, 0.0).astype(jnp.bfloat16)
     at = (core * half, (1 - core) * half, 2 * core, 2 * (1 - core))
     local, start, to, at, core1 = lax.optimization_barrier((local, start, to, at, core1))
     other = send(pick(core1, local), "c", 1)
-    *by_y, near, far = to_blocks(to, change(core1, to, local, start), other, ny)
-    far, near = far.astype(wire), near.astype(wire)
-    by_y = [x.astype(wire) for x in by_y]
-    first, second = wide(by_y[0]), wide(near)
-    second = second + wide(send(far, "xh", 1))
-    for j in far_y:
-        first = first + wide(send(by_y[j], "y", j))
-
-    old, _ = lax.optimization_barrier(((master, momentum), (far, by_y[1:])))
+    blocks = to_blocks(to, change(core1, to, local, start), other, nx * ny)
+    away = [(h, j) for h in (1, 0) for j in (2, 1, 3, 0) if h or j]
+    sent = {(h, j): blocks[h * ny + j].astype(wire) for h, j in away}
+    total = blocks[0]
+    for h, j in away:
+        total = total + wide(send_xy(sent[h, j], h, j))
+
+    old, _ = lax.optimization_barrier(((master, momentum), list(sent.values())))
     base = old[0][0] - outer_rate * nesterov_mu**2 * old[1][0]
     mine, theirs = part(base, 0, at[0]), part(base, 0, at[1])
     theirs = send(theirs, "c", 1)
     base = jnp.concatenate([jnp.where(core == 0, mine, theirs), jnp.where(core == 0, theirs, mine)], axis=0)
 
-    per = rows // (nx * ny)
-    pieces = [second[j * per : (j + 1) * per] for j in range(ny)]
-    second = pieces[0]
-    far = send(first[per:].astype(wire), "xh", 1)
-    for j in far_y:
-        second = second + wide(send(pieces[j].astype(wire), "y", j))
-    first = first[:per] + wide(far)
-
-    total = jnp.concatenate([first, second], axis=1).astype(wire).reshape(nz, 4, half)
+    total = total.astype(wire).reshape(nz, 4, half)
     base, total = lax.optimization_barrier((base, total))
     total = wide(lax.all_to_all(total, "z", 0, 0, tiled=True)).sum(axis=0)
     grad = total * (1.0 / (SCALE * replicas))
-    grad = lax.optimization_barrier(grad)
-    pair = lax.optimization_barrier(jnp.concatenate([base, grad], axis=1))
-    pairs = {k: send(pair, "z", k) for k in (4, 3, 5, 2, 6, 1, 7)}
-    pairs[0] = pair
-
     members = lax.axis_size(ALL)
     parts = lax.all_to_all(jnp.full((members, 1, 128), jnp.sum(grad * grad)), ALL, 0, 0, tiled=True)
     squares = jnp.sum(parts[:, 0, 0])
@@ -228,10 +208,9 @@
     grad_rms = jnp.sqrt(squares / elements + epsilon)
     clip = jnp.minimum(1.0, clip_limit / grad_rms)
 
-    pairs = [pairs[k] for k in range(nz)]
-    mine = [x[:, :half] - outer_rate * (1.0 + nesterov_mu) * (clip * x[:, half:]) for x in pairs]
-    mine = [x.astype(jnp.bfloat16) for x in mine]
-    mine = jnp.concatenate(mine, axis=0)
+    mine = (base - outer_rate * (1.0 + nesterov_mu) * (clip * grad)).astype(jnp.bfloat16)
+    mine = lax.all_to_all(jnp.broadcast_to(mine[None], (nz, 4, half)), "z", 0, 0, tiled=True)
+    mine = mine.reshape(nz * 4, half)
     first, second = mine[:, :edge], mine[:, edge:]
     arrived = {j: send(second, "y", j) for j in far_y}
     second = jnp.concatenate([second] + [arrived[j] for j in range(1, ny)], axis=0)
@@ -240,8 +219,11 @@
     mine = [first] + [arrived[j] for j in range(1, ny)]
     theirs = [send(x, "c", 1) for x in mine]
     new_params = from_blocks(core1, back_y.astype(jnp.bfloat16), mine, theirs, 0)
-    mine = [second, send(second, "xh", 1)]
-    theirs = [send(x, "c", 1) for x in mine]
+    arrived = send(second, "xh", 1)
+    theirs = [send(second, "c", 1)]
+    arrived, new_params = lax.optimization_barrier((arrived, new_params))
+    mine = [second, arrived]
+    theirs.append(send(arrived, "c", 1))
     new_params = from_blocks(core1, back_x.astype(jnp.bfloat16), mine, theirs, 1, new_params)
 
     other = send(part(grad, at[3], 0), "c", 1)

time: 143 us -> 137 us (0.958)
  blocking collectives: 0 us -> 39.3 us
  starting transfers between devices: 61.8 us -> 39.3 us
  waiting for transfers between devices: 59.1 us -> 38.5 us
  other arithmetic: 5.59 us -> 3.37 us
    ppermute x32 -> x17, waiting for transfers between devices: 48.1 us -> 7.89 us  [send(): return lax.ppermute(x, axis, shift(axis, by))]
    all_to_all x0 -> x2, blocking collectives: none -> 39.3 us  [the longest x1 21.1 us: step(): lax.all_to_all(jnp.full((members, 1, 128), jnp.sum(grad * grad)), ALL, 0,...]
    ppermute x0 -> x7, waiting for transfers between devices: none -> 18.9 us  [send_xy(): return lax.ppermute(x, ('xh', 'y'), moves)]
    ppermute x32 -> x17, starting transfers between devices: 44.9 us -> 26 us  [send(): return lax.ppermute(x, axis, shift(axis, by))]
    all_to_all x2 -> x1, starting transfers between devices: 16.8 us -> 3.41 us  [step(): lax.all_to_all(jnp.broadcast_to(mine[None], (nz, 4, half)), 'z', 0, 0, ti...]
    ppermute x0 -> x7, starting transfers between devices: none -> 9.91 us  [send_xy(): return lax.ppermute(x, ('xh', 'y'), moves)]
    all_to_all x2 -> x1, waiting for transfers between devices: 11.1 us -> 11.7 us  [step(): lax.all_to_all(jnp.broadcast_to(mine[None], (nz, 4, half)), 'z', 0, 0, ti...]
  transfers between devices with their start and end apart: 34 -> 25, of which waited for: 19 -> 14; matrix products, arithmetic and copies ran while one was open for 3% -> 1% of each run, Pallas kernels for 4% -> 4%
where the time goes in v3:
time: 137 us; the launch traced here: 136 us
  starting transfers between devices  39.3 us (29%)
  blocking collectives  39.3 us (29%)
  waiting for transfers between devices  38.5 us (28%)
  Pallas kernels  11.8 us (9%)
  other arithmetic  3.37 us (2%)
  local copies, waits for them, and re-layouts  2.4 us (2%)
  between operations  1.59 us (1%)
    ppermute x17, starting transfers between devices, send(): return lax.ppermute(x, axis, shift(axis, by))  26 us
    all_to_all x1, blocking collectives, step(): lax.all_to_all(jnp.full((members, 1, 128), jnp.sum(grad * grad)), ALL, 0,...  21.1 us
    ppermute x7, waiting for transfers between devices, send_xy(): return lax.ppermute(x, ('xh', 'y'), moves)  18.9 us
    all_to_all x1, blocking collectives, step(): total = wide(lax.all_to_all(total, 'z', 0, 0, tiled=True)).sum(axis=0)  18.3 us
    all_to_all x1, waiting for transfers between devices, step(): lax.all_to_all(jnp.broadcast_to(mine[None], (nz, 4, half)), 'z', 0, 0, ti...  11.7 us
    ppermute x7, starting transfers between devices, send_xy(): return lax.ppermute(x, ('xh', 'y'), moves)  9.91 us
    ppermute x17, waiting for transfers between devices, send(): return lax.ppermute(x, axis, shift(axis, by))  7.89 us
    pallas_call x2, Pallas kernels, from_blocks(): pl.pallas_call(from_blocks_kernel, grid_spec=pltpu.PrefetchScalarGridSpec...  5.16 us
  transfers between devices with their start and end apart: 25, of which 14 were waited for; matrix products, arithmetic and copies ran while one was open for 1% of the time, Pallas kernels for 4%

profile of v3, /device:TPU:1, one launch (start us, length us, event | category | flops | bytes accessed | tf_op | source)
XLA Modules:
  0.0 136.4 jit_solution(10282497123216228072)
XLA Ops:
  0.8 2.9 %pick.1 = bf16[256,4096]{1,0:T(8,128)(2,1)} custom-call(s32[1]{0:T(128)} %bitcast.2.core, bf16[256,8192]{1,0:T(8,128)(2,1)} %bitcast.13), custom_call_target="tpu_custom_call" | custom-call | tf_op jit(solution)/shard_map/pick/pallas_call | solution.py:48
  3.7 3.3 %collective-permute-start = (bf16[256,4096]{1,0:T(8,128)(2,1)}, bf16[256,4096]{1,0:T(8,128)(2,1)S(1)}, u32[]{:S(2)}, u32[]{:S(2)}) collective-permute-start(bf16[256,4096]{1,0:T(8,128)(2,1)} %pick.1), channel_id=1, source_target_pairs={{0,2},{2,0},{1,3},{3,1},{4,6},{6,4},{5,7},{7,5},{8,10},{10,8},{9,1... | collective-permute-start | bytes 6291464 | tf_op jit(solution)/shard_map/ppermute | solution.py:164
  7.0 3.0 %change.1.own = f32[256,4096]{1,0:T(8,128)S(1)} custom-call(s32[1]{0:T(128)} %bitcast.2.core, bf16[256,256]{1,0:T(8,128)(2,1)S(1)} %select_convert_fusion.one, bf16[256,8192]{1,0:T(8,128)(2,1)} %bitcast.14, bf16[256,8192]{1,0:T(8,128)(2,1)} %bitcast.16), custom_call_target="tpu_custom_call" | custom-call | tf_op jit(solution)/shard_map/change/pallas_call | solution.py:80
  10.0 0.9 collective-permute-done.other
  11.0 0.7 to_blocks.1
  12.0 0.6 copy-done
  12.7 0.5 collective-permute-start.1
  13.2 3.7 %collective-permute-start.2 = (f16[32,4096]{1,0:T(8,128)(2,1)S(1)}, f16[32,4096]{1,0:T(8,128)(2,1)S(1)}, u32[]{:S(2)}, u32[]{:S(2)}) collective-permute-start(f16[32,4096]{1,0:T(8,128)(2,1)S(1)} %convert_element_type.61), channel_id=1, source_target_pairs={{0,136},{4,140},{8,128},{12,132},{128,8},{132,12},{136,0},{140,4},... | collective-permute-start | bytes 786440 | tf_op jit(solution)/shard_map/ppermute | solution.py:168
  16.9 0.3 collective-permute-start.3
  17.2 4.7 %collective-permute-start.4 = (f16[32,4096]{1,0:T(8,128)(2,1)S(1)}, f16[32,4096]{1,0:T(8,128)(2,1)S(1)}, u32[]{:S(2)}, u32[]{:S(2)}) collective-permute-start(f16[32,4096]{1,0:T(8,128)(2,1)S(1)} %convert_element_type.63), channel_id=1, source_target_pairs={{0,140},{4,128},{8,132},{12,136},{128,12},{132,0},{136,4},{140,8},... | collective-permute-start | bytes 786440 | tf_op jit(solution)/shard_map/ppermute | solution.py:168
  22.2 0.6 collective-permute-start.6
  22.8 2.2 %collective-permute-done.2 = f16[32,4096]{1,0:T(8,128)(2,1)S(1)} collective-permute-done((f16[32,4096]{1,0:T(8,128)(2,1)S(1)}, f16[32,4096]{1,0:T(8,128)(2,1)S(1)}, u32[]{:S(2)}, u32[]{:S(2)}) %collective-permute-start.2) | collective-permute-done | bytes 262176 | tf_op jit(solution)/shard_map/ppermute | solution.py:168
  25.0 5.3 %collective-permute-done.3 = f16[32,4096]{1,0:T(8,128)(2,1)S(1)} collective-permute-done((f16[32,4096]{1,0:T(8,128)(2,1)S(1)}, f16[32,4096]{1,0:T(8,128)(2,1)S(1)}, u32[]{:S(2)}, u32[]{:S(2)}) %collective-permute-start.3) | collective-permute-done | bytes 262176 | tf_op jit(solution)/shard_map/ppermute | solution.py:168
  30.4 0.4 collective-permute-start.8
  30.8 4.8 %collective-permute-done.4 = f16[32,4096]{1,0:T(8,128)(2,1)S(1)} collective-permute-done((f16[32,4096]{1,0:T(8,128)(2,1)S(1)}, f16[32,4096]{1,0:T(8,128)(2,1)S(1)}, u32[]{:S(2)}, u32[]{:S(2)}) %collective-permute-start.4) | collective-permute-done | bytes 262176 | tf_op jit(solution)/shard_map/ppermute | solution.py:168
  35.6 5.0 %collective-permute-done.5 = f16[32,4096]{1,0:T(8,128)(2,1)S(1)} collective-permute-done((f16[32,4096]{1,0:T(8,128)(2,1)S(1)}, f16[32,4096]{1,0:T(8,128)(2,1)S(1)}, u32[]{:S(2)}, u32[]{:S(2)}) %collective-permute-start.5) | collective-permute-done | bytes 262176 | tf_op jit(solution)/shard_map/ppermute | solution.py:168
  40.6 1.6 %collective-permute-done.7 = f16[32,4096]{1,0:T(8,128)(2,1)S(1)} collective-permute-done((f16[32,4096]{1,0:T(8,128)(2,1)S(1)}, f16[32,4096]{1,0:T(8,128)(2,1)S(1)}, u32[]{:S(2)}, u32[]{:S(2)}) %collective-permute-start.7) | collective-permute-done | bytes 262176 | tf_op jit(solution)/shard_map/ppermute | solution.py:168
  42.2 0.3 add_convert_fusion
  42.6 18.3 %all_to_all.15 = f16[8,4,4096]{2,1,0:T(4,128)(2,1)S(1)} all-to-all(f16[8,4,4096]{2,1,0:T(4,128)(2,1)S(1)} %reshape.278), channel_id=1, replica_groups=mesh['xh'=2,'z'=8,'y'=4,'c'=2,'g'=2] {'z'}, dimensions={0} | all-to-all | bytes 524288 | tf_op jit(solution)/shard_map/all_to_all | solution.py:202
  61.0 0.6 multiply_reduce_fusion
  61.6 0.7 broadcast_in_dim.33
  62.3 21.1 %all_to_all.16 = f32[256,1,128]{2,1,0:T(1,128)S(1)} all-to-all(f32[256,1,128]{2,1,0:T(1,128)S(1)} %broadcast_in_dim.33), channel_id=1, replica_groups=mesh['xh'=2,'z'=8,'y'=4,'c'=2,'g'=2] {'xh','z','y','c','g'}, dimensions={0} | all-to-all | bytes 262144 | tf_op jit(solution)/shard_map/all_to_all | solution.py:205
  83.4 0.9 slice_reduce_fusion
  85.0 0.8 broadcast_in_dim.34
  85.8 3.4 %all-to-all-start.2 = ((bf16[8,4,4096]{2,1,0:T(4,128)(2,1)}), bf16[8,4,4096]{2,1,0:T(4,128)(2,1)S(1)}, u32[]{:S(2)}, u32[]{:S(2)}) async-start(bf16[8,4,4096]{2,1,0:T(4,128)(2,1)} %broadcast_in_dim.34), calls=%async_computation.2 | async-start | bytes 524288 | tf_op jit(solution)/shard_map/all_to_all | solution.py:212
  89.3 11.7 %all-to-all-done.2 = bf16[8,4,4096]{2,1,0:T(4,128)(2,1)S(1)} async-done(((bf16[8,4,4096]{2,1,0:T(4,128)(2,1)}), bf16[8,4,4096]{2,1,0:T(4,128)(2,1)S(1)}, u32[]{:S(2)}, u32[]{:S(2)}) %all-to-all-start.2) | async-done | bytes 262176 | tf_op jit(solution)/shard_map/all_to_all | solution.py:212
  101.2 0.5 collective-permute-start.10
  101.7 3.3 %collective-permute-start.11 = (bf16[32,2048]{1,0:T(8,128)(2,1)S(1)}, bf16[32,2048]{1,0:T(8,128)(2,1)S(1)}, u32[]{:S(2)}, u32[]{:S(2)}) collective-permute-start(bf16[32,2048]{1,0:T(8,128)(2,1)S(1)} %get-tuple-element.50), channel_id=1, source_target_pairs={{0,8},{4,12},{8,0},{12,4},{1,9},{5,13},{9,1},{13,5},{2,10},{6,14},... | collective-permute-start | bytes 393224 | tf_op jit(solution)/shard_map/ppermute | solution.py:164
  104.9 1.2 collective-permute-start.12
  106.1 0.4 collective-permute-done.14
  106.5 0.3 collective-permute-start.15
  106.8 0.8 collective-permute-start.16
  107.6 1.7 %collective-permute-start.17 = (bf16[64,2048]{1,0:T(8,128)(2,1)S(1)}, bf16[64,2048]{1,0:T(8,128)(2,1)S(1)}, u32[]{:S(2)}, u32[]{:S(2)}) collective-permute-start(bf16[64,2048]{1,0:T(8,128)(2,1)S(1)} %pad_maximum_fusion.1.refs_0_), channel_id=1, source_target_pairs={{0,12},{4,0},{8,4},{12,8},{1,13},{5,1},{9,5},{13,9},{2,14},{6,2},{... | collective-permute-start | bytes 786440 | tf_op jit(solution)/shard_map/ppermute | solution.py:164
  109.3 1.3 collective-permute-done.11
  110.6 2.8 %collective-permute-start.9 = (f32[2,4096]{1,0:T(2,128)S(1)}, f32[2,4096]{1,0:T(2,128)S(1)}, u32[]{:S(2)}, u32[]{:S(2)}) collective-permute-start(f32[2,4096]{1,0:T(2,128)S(1)} %constant_dynamic-slice_fusion), channel_id=1, source_target_pairs={{0,2},{2,0},{1,3},{3,1},{4,6},{6,4},{5,7},{7,5},{8,10},{10,8},{9,1... | collective-permute-start | bytes 98312 | tf_op jit(solution)/shard_map/ppermute | solution.py:164
  113.4 2.9 %collective-permute-start.18 = (bf16[64,2048]{1,0:T(8,128)(2,1)S(1)}, bf16[64,2048]{1,0:T(8,128)(2,1)S(1)}, u32[]{:S(2)}, u32[]{:S(2)}) collective-permute-start(bf16[64,2048]{1,0:T(8,128)(2,1)S(1)} %pad_maximum_fusion.1.refs_0_), channel_id=1, source_target_pairs={{0,2},{2,0},{1,3},{3,1},{4,6},{6,4},{5,7},{7,5},{8,10},{10,8},{9,1... | collective-permute-start | bytes 786440 | tf_op jit(solution)/shard_map/ppermute | solution.py:164
  116.3 1.7 %collective-permute-start.13 = (bf16[128,2048]{1,0:T(8,128)(2,1)S(1)}, bf16[128,2048]{1,0:T(8,128)(2,1)S(1)}, u32[]{:S(2)}, u32[]{:S(2)}) collective-permute-start(bf16[128,2048]{1,0:T(8,128)(2,1)S(1)} %pad_maximum_fusion.refs_0_), channel_id=1, source_target_pairs={{0,128},{128,0},{1,129},{129,1},{2,130},{130,2},{3,131},{131,3},{4... | collective-permute-start | bytes 1572872 | tf_op jit(solution)/shard_map/ppermute | solution.py:164
  118.0 5.6 %collective-permute-start.19 = (bf16[64,2048]{1,0:T(8,128)(2,1)S(1)}, bf16[64,2048]{1,0:T(8,128)(2,1)S(1)}, u32[]{:S(2)}, u32[]{:S(2)}) collective-permute-start(bf16[64,2048]{1,0:T(8,128)(2,1)S(1)} %collective-permute-done.15.refs_1_), channel_id=1, source_target_pairs={{0,2},{2,0},{1,3},{3,1},{4,6},{6,4},{5,7},{7,5},{8,10},{10,8},{9,1... | collective-permute-start | bytes 786440 | tf_op jit(solution)/shard_map/ppermute | solution.py:164
  123.6 0.5 collective-permute-start.21
  124.3 0.4 collective-permute-done.19.refs_5_
  124.7 0.4 collective-permute-done.20.refs_6_
  125.1 0.4 collective-permute-done.21.refs_7_
  125.5 2.6 %from_blocks.2.refs_4_ = bf16[256,8192]{1,0:T(8,128)(2,1)} custom-call(s32[1]{0:T(128)} %bitcast.2.core, bf16[256,256]{1,0:T(8,128)(2,1)S(1)} %fusion.1.one, bf16[64,2048]{1,0:T(8,128)(2,1)S(1)} %pad_maximum_fusion.1.refs_0_, bf16[64,2048]{1,0:T(8,128)(2,1)S(1)} %collective-permute-done.15.refs_1_, bf16[64,2048]{1,0:T(8,128)(2,1)S(1)} %collective-permute-done.16.refs_2_, ...), custom_call_target="tpu_custom_call" | custom-call | tf_op jit(solution)/shard_map/from_blocks/pallas_call | solution.py:135
  128.1 3.3 %collective-permute-done.13.refs_1_ = bf16[128,2048]{1,0:T(8,128)(2,1)S(1)} collective-permute-done((bf16[128,2048]{1,0:T(8,128)(2,1)S(1)}, bf16[128,2048]{1,0:T(8,128)(2,1)S(1)}, u32[]{:S(2)}, u32[]{:S(2)}) %collective-permute-start.13) | collective-permute-done | bytes 524320 | tf_op jit(solution)/shard_map/ppermute | solution.py:164
  131.4 0.9 collective-permute-start.23
  132.2 0.8 multiply_subtract_fusion
  133.0 0.8 collective-permute-done.23.refs_3_
  133.8 2.6 %from_blocks.3 = bf16[256,8192]{1,0:T(8,128)(2,1)} custom-call(s32[1]{0:T(128)} %bitcast.2.core, bf16[256,256]{1,0:T(8,128)(2,1)S(1)} %fusion.one, bf16[128,2048]{1,0:T(8,128)(2,1)S(1)} %pad_maximum_fusion.refs_0_, bf16[128,2048]{1,0:T(8,128)(2,1)S(1)} %collective-permute-done.13.refs_1_, ...), custom_call_target="tpu_custom_call", output_to_operand_aliasing={{}: (6, {})} | custom-call | tf_op jit(solution)/shard_map/from_blocks/pallas_call | solution.py:135
  (45 shorter events, 1.7 us)
Async XLA Ops:
  3.7 7.3 %collective-permute-start = (bf16[256,4096]{1,0:T(8,128)(2,1)}, bf16[256,4096]{1,0:T(8,128)(2,1)S(1)}, u32[]{:S(2)}, u32[]{:S(2)}) collective-permute-start(bf16[256,4096]{1,0:T(8,128)(2,1)} %pick.1), channel_id=1, source_target_pairs={{0,2},{2,0},{1,3},{3,1},{4,6},{6,4},{5,7},{7,5},{8,10},{10,8},{9,1... | collective-permute-start | bytes 6291464 | tf_op jit(solution)/shard_map/ppermute | solution.py:164
  11.7 0.8 copy-start
  11.7 0.9 copy-start.1
  12.7 9.4 %collective-permute-start.1 = (f32[2,4096]{1,0:T(2,128)S(1)}, f32[2,4096]{1,0:T(2,128)S(1)}, u32[]{:S(2)}, u32[]{:S(2)}) collective-permute-start(f32[2,4096]{1,0:T(2,128)S(1)} %dynamic-slice_bitcast_fusion), channel_id=1, source_target_pairs={{0,2},{2,0},{1,3},{3,1},{4,6},{6,4},{5,7},{7,5},{8,10},{10,8},{9,1... | collective-permute-start | bytes 98312 | tf_op jit(solution)/shard_map/ppermute | solution.py:164
  13.2 11.8 %collective-permute-start.2 = (f16[32,4096]{1,0:T(8,128)(2,1)S(1)}, f16[32,4096]{1,0:T(8,128)(2,1)S(1)}, u32[]{:S(2)}, u32[]{:S(2)}) collective-permute-start(f16[32,4096]{1,0:T(8,128)(2,1)S(1)} %convert_element_type.61), channel_id=1, source_target_pairs={{0,136},{4,140},{8,128},{12,132},{128,8},{132,12},{136,0},{140,4},... | collective-permute-start | bytes 786440 | tf_op jit(solution)/shard_map/ppermute | solution.py:168
  16.9 13.5 %collective-permute-start.3 = (f16[32,4096]{1,0:T(8,128)(2,1)S(1)}, f16[32,4096]{1,0:T(8,128)(2,1)S(1)}, u32[]{:S(2)}, u32[]{:S(2)}) collective-permute-start(f16[32,4096]{1,0:T(8,128)(2,1)S(1)} %convert_element_type.62), channel_id=1, source_target_pairs={{0,132},{4,136},{8,140},{12,128},{128,4},{132,8},{136,12},{140,0},... | collective-permute-start | bytes 786440 | tf_op jit(solution)/shard_map/ppermute | solution.py:168
  17.2 18.3 %collective-permute-start.4 = (f16[32,4096]{1,0:T(8,128)(2,1)S(1)}, f16[32,4096]{1,0:T(8,128)(2,1)S(1)}, u32[]{:S(2)}, u32[]{:S(2)}) collective-permute-start(f16[32,4096]{1,0:T(8,128)(2,1)S(1)} %convert_element_type.63), channel_id=1, source_target_pairs={{0,140},{4,128},{8,132},{12,136},{128,12},{132,0},{136,4},{140,8},... | collective-permute-start | bytes 786440 | tf_op jit(solution)/shard_map/ppermute | solution.py:168
  21.9 18.6 %collective-permute-start.5 = (f16[32,4096]{1,0:T(8,128)(2,1)S(1)}, f16[32,4096]{1,0:T(8,128)(2,1)S(1)}, u32[]{:S(2)}, u32[]{:S(2)}) collective-permute-start(f16[32,4096]{1,0:T(8,128)(2,1)S(1)} %convert_element_type.64), channel_id=1, source_target_pairs={{0,128},{4,132},{8,136},{12,140},{128,0},{132,4},{136,8},{140,12},... | collective-permute-start | bytes 786440 | tf_op jit(solution)/shard_map/ppermute | solution.py:168
  22.2 18.4 %collective-permute-start.6 = (f16[32,4096]{1,0:T(8,128)(2,1)S(1)}, f16[32,4096]{1,0:T(8,128)(2,1)S(1)}, u32[]{:S(2)}, u32[]{:S(2)}) collective-permute-start(f16[32,4096]{1,0:T(8,128)(2,1)S(1)} %convert_element_type.65), channel_id=1, source_target_pairs={{0,8},{4,12},{8,0},{12,4},{128,136},{132,140},{136,128},{140,132},... | collective-permute-start | bytes 786440 | tf_op jit(solution)/shard_map/ppermute | solution.py:168
  25.0 17.2 %collective-permute-start.7 = (f16[32,4096]{1,0:T(8,128)(2,1)S(1)}, f16[32,4096]{1,0:T(8,128)(2,1)S(1)}, u32[]{:S(2)}, u32[]{:S(2)}) collective-permute-start(f16[32,4096]{1,0:T(8,128)(2,1)S(1)} %convert_element_type.66), channel_id=1, source_target_pairs={{0,4},{4,8},{8,12},{12,0},{128,132},{132,136},{136,140},{140,128},... | collective-permute-start | bytes 786440 | tf_op jit(solution)/shard_map/ppermute | solution.py:168
  30.4 11.8 %collective-permute-start.8 = (f16[32,4096]{1,0:T(8,128)(2,1)S(1)}, f16[32,4096]{1,0:T(8,128)(2,1)S(1)}, u32[]{:S(2)}, u32[]{:S(2)}) collective-permute-start(f16[32,4096]{1,0:T(8,128)(2,1)S(1)} %convert_element_type.67), channel_id=1, source_target_pairs={{0,12},{4,0},{8,4},{12,8},{128,140},{132,128},{136,132},{140,136},... | collective-permute-start | bytes 786440 | tf_op jit(solution)/shard_map/ppermute | solution.py:168
  85.8 15.2 %all-to-all-start.2 = ((bf16[8,4,4096]{2,1,0:T(4,128)(2,1)}), bf16[8,4,4096]{2,1,0:T(4,128)(2,1)S(1)}, u32[]{:S(2)}, u32[]{:S(2)}) async-start(bf16[8,4,4096]{2,1,0:T(4,128)(2,1)} %broadcast_in_dim.34), calls=%async_computation.2 | async-start | bytes 524288 | tf_op jit(solution)/shard_map/all_to_all | solution.py:212
  101.0 5.4 %collective-permute-start.14 = (bf16[32,2048]{1,0:T(8,128)(2,1)S(1)}, bf16[32,2048]{1,0:T(8,128)(2,1)S(1)}, u32[]{:S(2)}, u32[]{:S(2)}) collective-permute-start(bf16[32,2048]{1,0:T(8,128)(2,1)S(1)} %get-tuple-element.49), channel_id=1, source_target_pairs={{0,128},{128,0},{1,129},{129,1},{2,130},{130,2},{3,131},{131,3},{4... | collective-permute-start | bytes 393224 | tf_op jit(solution)/shard_map/ppermute | solution.py:164
  101.2 6.4 %collective-permute-start.10 = (bf16[32,2048]{1,0:T(8,128)(2,1)S(1)}, bf16[32,2048]{1,0:T(8,128)(2,1)S(1)}, u32[]{:S(2)}, u32[]{:S(2)}) collective-permute-start(bf16[32,2048]{1,0:T(8,128)(2,1)S(1)} %get-tuple-element.50), channel_id=1, source_target_pairs={{0,4},{4,8},{8,12},{12,0},{1,5},{5,9},{9,13},{13,1},{2,6},{6,10},{... | collective-permute-start | bytes 393224 | tf_op jit(solution)/shard_map/ppermute | solution.py:164
  101.7 8.9 %collective-permute-start.11 = (bf16[32,2048]{1,0:T(8,128)(2,1)S(1)}, bf16[32,2048]{1,0:T(8,128)(2,1)S(1)}, u32[]{:S(2)}, u32[]{:S(2)}) collective-permute-start(bf16[32,2048]{1,0:T(8,128)(2,1)S(1)} %get-tuple-element.50), channel_id=1, source_target_pairs={{0,8},{4,12},{8,0},{12,4},{1,9},{5,13},{9,1},{13,5},{2,10},{6,14},... | collective-permute-start | bytes 393224 | tf_op jit(solution)/shard_map/ppermute | solution.py:164
  104.9 8.5 %collective-permute-start.12 = (bf16[32,2048]{1,0:T(8,128)(2,1)S(1)}, bf16[32,2048]{1,0:T(8,128)(2,1)S(1)}, u32[]{:S(2)}, u32[]{:S(2)}) collective-permute-start(bf16[32,2048]{1,0:T(8,128)(2,1)S(1)} %get-tuple-element.50), channel_id=1, source_target_pairs={{0,12},{4,0},{8,4},{12,8},{1,13},{5,1},{9,5},{13,9},{2,14},{6,2},{... | collective-permute-start | bytes 393224 | tf_op jit(solution)/shard_map/ppermute | solution.py:164
  106.5 11.5 %collective-permute-start.15 = (bf16[64,2048]{1,0:T(8,128)(2,1)S(1)}, bf16[64,2048]{1,0:T(8,128)(2,1)S(1)}, u32[]{:S(2)}, u32[]{:S(2)}) collective-permute-start(bf16[64,2048]{1,0:T(8,128)(2,1)S(1)} %pad_maximum_fusion.1.refs_0_), channel_id=1, source_target_pairs={{0,4},{4,8},{8,12},{12,0},{1,5},{5,9},{9,13},{13,1},{2,6},{6,10},{... | collective-permute-start | bytes 786440 | tf_op jit(solution)/shard_map/ppermute | solution.py:164
  106.8 16.8 %collective-permute-start.16 = (bf16[64,2048]{1,0:T(8,128)(2,1)S(1)}, bf16[64,2048]{1,0:T(8,128)(2,1)S(1)}, u32[]{:S(2)}, u32[]{:S(2)}) collective-permute-start(bf16[64,2048]{1,0:T(8,128)(2,1)S(1)} %pad_maximum_fusion.1.refs_0_), channel_id=1, source_target_pairs={{0,8},{4,12},{8,0},{12,4},{1,9},{5,13},{9,1},{13,5},{2,10},{6,14},... | collective-permute-start | bytes 786440 | tf_op jit(solution)/shard_map/ppermute | solution.py:164
  107.6 16.0 %collective-permute-start.17 = (bf16[64,2048]{1,0:T(8,128)(2,1)S(1)}, bf16[64,2048]{1,0:T(8,128)(2,1)S(1)}, u32[]{:S(2)}, u32[]{:S(2)}) collective-permute-start(bf16[64,2048]{1,0:T(8,128)(2,1)S(1)} %pad_maximum_fusion.1.refs_0_), channel_id=1, source_target_pairs={{0,12},{4,0},{8,4},{12,8},{1,13},{5,1},{9,5},{13,9},{2,14},{6,2},{... | collective-permute-start | bytes 786440 | tf_op jit(solution)/shard_map/ppermute | solution.py:164
  110.6 5.7 %collective-permute-start.9 = (f32[2,4096]{1,0:T(2,128)S(1)}, f32[2,4096]{1,0:T(2,128)S(1)}, u32[]{:S(2)}, u32[]{:S(2)}) collective-permute-start(f32[2,4096]{1,0:T(2,128)S(1)} %constant_dynamic-slice_fusion), channel_id=1, source_target_pairs={{0,2},{2,0},{1,3},{3,1},{4,6},{6,4},{5,7},{7,5},{8,10},{10,8},{9,1... | collective-permute-start | bytes 98312 | tf_op jit(solution)/shard_map/ppermute | solution.py:164
  113.4 10.7 %collective-permute-start.18 = (bf16[64,2048]{1,0:T(8,128)(2,1)S(1)}, bf16[64,2048]{1,0:T(8,128)(2,1)S(1)}, u32[]{:S(2)}, u32[]{:S(2)}) collective-permute-start(bf16[64,2048]{1,0:T(8,128)(2,1)S(1)} %pad_maximum_fusion.1.refs_0_), channel_id=1, source_target_pairs={{0,2},{2,0},{1,3},{3,1},{4,6},{6,4},{5,7},{7,5},{8,10},{10,8},{9,1... | collective-permute-start | bytes 786440 | tf_op jit(solution)/shard_map/ppermute | solution.py:164
  116.3 15.1 %collective-permute-start.13 = (bf16[128,2048]{1,0:T(8,128)(2,1)S(1)}, bf16[128,2048]{1,0:T(8,128)(2,1)S(1)}, u32[]{:S(2)}, u32[]{:S(2)}) collective-permute-start(bf16[128,2048]{1,0:T(8,128)(2,1)S(1)} %pad_maximum_fusion.refs_0_), channel_id=1, source_target_pairs={{0,128},{128,0},{1,129},{129,1},{2,130},{130,2},{3,131},{131,3},{4... | collective-permute-start | bytes 1572872 | tf_op jit(solution)/shard_map/ppermute | solution.py:164
  118.0 6.7 %collective-permute-start.19 = (bf16[64,2048]{1,0:T(8,128)(2,1)S(1)}, bf16[64,2048]{1,0:T(8,128)(2,1)S(1)}, u32[]{:S(2)}, u32[]{:S(2)}) collective-permute-start(bf16[64,2048]{1,0:T(8,128)(2,1)S(1)} %collective-permute-done.15.refs_1_), channel_id=1, source_target_pairs={{0,2},{2,0},{1,3},{3,1},{4,6},{6,4},{5,7},{7,5},{8,10},{10,8},{9,1... | collective-permute-start | bytes 786440 | tf_op jit(solution)/shard_map/ppermute | solution.py:164
  123.6 1.5 %collective-permute-start.20 = (bf16[64,2048]{1,0:T(8,128)(2,1)S(1)}, bf16[64,2048]{1,0:T(8,128)(2,1)S(1)}, u32[]{:S(2)}, u32[]{:S(2)}) collective-permute-start(bf16[64,2048]{1,0:T(8,128)(2,1)S(1)} %collective-permute-done.16.refs_2_), channel_id=1, source_target_pairs={{0,2},{2,0},{1,3},{3,1},{4,6},{6,4},{5,7},{7,5},{8,10},{10,8},{9,1... | collective-permute-start | bytes 786440 | tf_op jit(solution)/shard_map/ppermute | solution.py:164
  123.6 1.9 %collective-permute-start.21 = (bf16[64,2048]{1,0:T(8,128)(2,1)S(1)}, bf16[64,2048]{1,0:T(8,128)(2,1)S(1)}, u32[]{:S(2)}, u32[]{:S(2)}) collective-permute-start(bf16[64,2048]{1,0:T(8,128)(2,1)S(1)} %collective-permute-done.17.refs_3_), channel_id=1, source_target_pairs={{0,2},{2,0},{1,3},{3,1},{4,6},{6,4},{5,7},{7,5},{8,10},{10,8},{9,1... | collective-permute-start | bytes 786440 | tf_op jit(solution)/shard_map/ppermute | solution.py:164
  124.1 8.9 %collective-permute-start.22 = (bf16[128,2048]{1,0:T(8,128)(2,1)S(1)}, bf16[128,2048]{1,0:T(8,128)(2,1)S(1)}, u32[]{:S(2)}, u32[]{:S(2)}) collective-permute-start(bf16[128,2048]{1,0:T(8,128)(2,1)S(1)} %pad_maximum_fusion.refs_0_), channel_id=1, source_target_pairs={{0,2},{2,0},{1,3},{3,1},{4,6},{6,4},{5,7},{7,5},{8,10},{10,8},{9,1... | collective-permute-start | bytes 1572872 | tf_op jit(solution)/shard_map/ppermute | solution.py:164
  131.4 2.4 %collective-permute-start.23 = (bf16[128,2048]{1,0:T(8,128)(2,1)S(1)}, bf16[128,2048]{1,0:T(8,128)(2,1)S(1)}, u32[]{:S(2)}, u32[]{:S(2)}) collective-permute-start(bf16[128,2048]{1,0:T(8,128)(2,1)S(1)} %collective-permute-done.13.refs_1_), channel_id=1, source_target_pairs={{0,2},{2,0},{1,3},{3,1},{4,6},{6,4},{5,7},{7,5},{8,10},{10,8},{9,1... | collective-permute-start | bytes 1572872 | tf_op jit(solution)/shard_map/ppermute | solution.py:164

commit v4 on v2

--- a/solution.py
+++ b/solution.py
@@ -180,7 +180,7 @@
 
     o = jnp.arange(rows)
     q, z, h, j = o % 4, o // 4 % nz, o // (4 * nz) % nx, o // (4 * nz * nx)
-    to = row_of(j, h, (lax.axis_index("z") + z) % nz, q, 1)[:, None] == o[None]
+    to = row_of(j, h, z, q, 1)[:, None] == o[None]
     z = (lax.axis_index("z") - z) % nz
     back_y = o[:, None] == row_of(j, h, z, q, -1)[None]
     j, h = o // (4 * nz) % ny, o // (4 * nz * ny)
@@ -214,13 +214,11 @@
     first = first[:per] + wide(far)
 
     far_z = (4, 3, 5, 2, 6, 1, 7)
-    total = jnp.concatenate([first, second], axis=1).reshape(nz, 4, half)
-    pieces = [total[k] for k in range(nz)]
-    total = pieces[0]
-    for k in far_z:
-        total = total + wide(send(pieces[k].astype(wire), "z", k))
+    total = jnp.concatenate([first, second], axis=1).astype(wire).reshape(nz, 4, half)
+    base, total = lax.optimization_barrier((base, total))
+    total = wide(lax.all_to_all(total, "z", 0, 0, tiled=True)).sum(axis=0)
     grad = total * (1.0 / (SCALE * replicas))
-    grad, base = lax.optimization_barrier((grad, base))
+    grad = lax.optimization_barrier(grad)
     grads = {k: send(grad, "z", k) for k in far_z}
     grads[0] = grad
 

time: 147 us -> 133 us (0.905)
  starting transfers between devices: 85.5 us -> 69.4 us
  other arithmetic: 3.57 us -> 7.61 us
  waiting for transfers between devices: 41.2 us -> 39.2 us
    ppermute x39 -> x32, starting transfers between devices: 64.2 us -> 48.3 us  [send(): return lax.ppermute(x, axis, shift(axis, by))]
    ppermute x39 -> x32, waiting for transfers between devices: 41.2 us -> 26 us  [send(): return lax.ppermute(x, axis, shift(axis, by))]
    all_to_all x0 -> x1, waiting for transfers between devices: none -> 9.21 us  [step(): total = wide(lax.all_to_all(total, 'z', 0, 0, tiled=True)).sum(axis=0)]
    all_to_all x1, starting transfers between devices: 15.1 us -> 8.78 us  [step(): lax.all_to_all(jnp.full((members, 1, 128), jnp.sum(grad * grad)), ALL, 0,...]
    all_to_all x0 -> x1, starting transfers between devices: none -> 4.18 us  [step(): total = wide(lax.all_to_all(total, 'z', 0, 0, tiled=True)).sum(axis=0)]
    all_to_all x1, waiting for transfers between devices: 0.01 us -> 4.01 us  [step(): lax.all_to_all(jnp.broadcast_to(base[None], (nz, 4, half)), 'z', 0, 0, ti...]
    convert_element_type x3, other arithmetic: 0.09 us -> 2.17 us  [step(): by_y = [x.astype(wire) for x in by_y]]
    all_to_all x1, starting transfers between devices: 6.11 us -> 8.19 us  [step(): lax.all_to_all(jnp.broadcast_to(base[None], (nz, 4, half)), 'z', 0, 0, ti...]
  transfers between devices with their start and end apart: 41 -> 35, of which waited for: 16 -> 13; matrix products, arithmetic and copies ran while one was open for 2% -> 4% of each run, Pallas kernels for 4% -> 4%
where the time goes in v4:
time: 133 us
  starting transfers between devices  69.4 us (52%)
  waiting for transfers between devices  39.2 us (29%)
  Pallas kernels  11.9 us (9%)
  other arithmetic  7.61 us (6%)
  local copies, waits for them, and re-layouts  2.76 us (2%)
  between operations  1.64 us (1%)
    ppermute x32, starting transfers between devices, send(): return lax.ppermute(x, axis, shift(axis, by))  48.3 us
    ppermute x32, waiting for transfers between devices, send(): return lax.ppermute(x, axis, shift(axis, by))  26 us
    all_to_all x1, waiting for transfers between devices, step(): total = wide(lax.all_to_all(total, 'z', 0, 0, tiled=True)).sum(axis=0)  9.21 us
    all_to_all x1, starting transfers between devices, step(): lax.all_to_all(jnp.full((members, 1, 128), jnp.sum(grad * grad)), ALL, 0,...  8.78 us
    all_to_all x1, starting transfers between devices, step(): lax.all_to_all(jnp.broadcast_to(base[None], (nz, 4, half)), 'z', 0, 0, ti...  8.19 us
    pallas_call x2, Pallas kernels, from_blocks(): pl.pallas_call(from_blocks_kernel, grid_spec=pltpu.PrefetchScalarGridSpec...  5.25 us
    all_to_all x1, starting transfers between devices, step(): total = wide(lax.all_to_all(total, 'z', 0, 0, tiled=True)).sum(axis=0)  4.18 us
    all_to_all x1, waiting for transfers between devices, step(): lax.all_to_all(jnp.broadcast_to(base[None], (nz, 4, half)), 'z', 0, 0, ti...  4.01 us
  transfers between devices with their start and end apart: 35, of which 13 were waited for; matrix products, arithmetic and copies ran while one was open for 4% of the time, Pallas kernels for 4%

profile of v4, /device:TPU:1, one launch (start us, length us, event | category | flops | bytes accessed | tf_op | source)
XLA Modules:
  0.0 132.6 jit_solution(17278187368076864015)
XLA Ops:
  0.8 2.9 %pick.1 = bf16[256,4096]{1,0:T(8,128)(2,1)} custom-call(s32[1]{0:T(128)} %bitcast.2.core, bf16[256,8192]{1,0:T(8,128)(2,1)} %bitcast.45), custom_call_target="tpu_custom_call" | custom-call | tf_op jit(solution)/shard_map/pick/pallas_call | solution.py:48
  3.7 3.3 %collective-permute-start = (bf16[256,4096]{1,0:T(8,128)(2,1)}, bf16[256,4096]{1,0:T(8,128)(2,1)S(1)}, u32[]{:S(2)}, u32[]{:S(2)}) collective-permute-start(bf16[256,4096]{1,0:T(8,128)(2,1)} %pick.1), channel_id=1, source_target_pairs={{0,2},{2,0},{1,3},{3,1},{4,6},{6,4},{5,7},{7,5},{8,10},{10,8},{9,1... | collective-permute-start | bytes 6291464 | tf_op jit(solution)/shard_map/ppermute | solution.py:173
  7.0 3.0 %change.1.own = f32[256,4096]{1,0:T(8,128)S(1)} custom-call(s32[1]{0:T(128)} %bitcast.2.core, bf16[256,256]{1,0:T(8,128)(2,1)S(1)} %select_convert_fusion.one, bf16[256,8192]{1,0:T(8,128)(2,1)} %bitcast.46, bf16[256,8192]{1,0:T(8,128)(2,1)} %bitcast.48), custom_call_target="tpu_custom_call" | custom-call | tf_op jit(solution)/shard_map/change/pallas_call | solution.py:80
  10.1 0.9 collective-permute-done.other
  14.6 1.2 collective-permute-start.2
  16.2 2.3 %collective-permute-start.4 = (f16[64,2048]{1,0:T(8,128)(2,1)}, f16[64,2048]{1,0:T(8,128)(2,1)}, u32[]{:S(2)}, u32[]{:S(2)}) collective-permute-start(f16[64,2048]{1,0:T(8,128)(2,1)} %convert_element_type.94), channel_id=1, source_target_pairs={{0,12},{4,0},{8,4},{12,8},{1,13},{5,1},{9,5},{13,9},{2,14},{6,2},{... | collective-permute-start | bytes 786440 | tf_op jit(solution)/shard_map/ppermute | solution.py:173
  18.5 2.7 %collective-permute-start.6 = (f16[128,2048]{1,0:T(8,128)(2,1)S(1)}, f16[128,2048]{1,0:T(8,128)(2,1)S(1)}, u32[]{:S(2)}, u32[]{:S(2)}) collective-permute-start(f16[128,2048]{1,0:T(8,128)(2,1)S(1)} %convert_element_type.91), channel_id=1, source_target_pairs={{0,128},{128,0},{1,129},{129,1},{2,130},{130,2},{3,131},{131,3},{4... | collective-permute-start | bytes 1572872 | tf_op jit(solution)/shard_map/ppermute | solution.py:173
  21.4 0.9 broadcast_in_dim.33
  22.2 8.2 %all-to-all-start = ((f32[8,4,4096]{2,1,0:T(4,128)}), f32[8,4,4096]{2,1,0:T(4,128)S(1)}, u32[]{:S(2)}, u32[]{:S(2)}) async-start(f32[8,4,4096]{2,1,0:T(4,128)} %broadcast_in_dim.33), calls=%async_computation | async-start | bytes 1048576 | tf_op jit(solution)/shard_map/all_to_all | solution.py:206
  30.4 1.1 convert_add_fusion.1
  31.6 0.9 collective-permute-start.5
  32.8 1.7 %collective-permute-start.7 = (f16[32,2048]{1,0:T(8,128)(2,1)S(1)}, f16[32,2048]{1,0:T(8,128)(2,1)S(1)}, u32[]{:S(2)}, u32[]{:S(2)}) collective-permute-start(f16[32,2048]{1,0:T(8,128)(2,1)S(1)} %get-tuple-element.51), channel_id=1, source_target_pairs={{0,8},{4,12},{8,0},{12,4},{1,9},{5,13},{9,1},{13,5},{2,10},{6,14},... | collective-permute-start | bytes 393224 | tf_op jit(solution)/shard_map/ppermute | solution.py:173
  34.5 1.7 %collective-permute-start.8 = (f16[32,2048]{1,0:T(8,128)(2,1)S(1)}, f16[32,2048]{1,0:T(8,128)(2,1)S(1)}, u32[]{:S(2)}, u32[]{:S(2)}) collective-permute-start(f16[32,2048]{1,0:T(8,128)(2,1)S(1)} %get-tuple-element.53), channel_id=1, source_target_pairs={{0,4},{4,8},{8,12},{12,0},{1,5},{5,9},{9,13},{13,1},{2,6},{6,10},{... | collective-permute-start | bytes 393224 | tf_op jit(solution)/shard_map/ppermute | solution.py:173
  36.2 1.0 collective-permute-start.9
  37.3 1.2 collective-permute-done.7
  38.5 2.1 %collective-permute-done.8 = f16[32,2048]{1,0:T(8,128)(2,1)S(1)} collective-permute-done((f16[32,2048]{1,0:T(8,128)(2,1)S(1)}, f16[32,2048]{1,0:T(8,128)(2,1)S(1)}, u32[]{:S(2)}, u32[]{:S(2)}) %collective-permute-start.8) | collective-permute-done | bytes 131104 | tf_op jit(solution)/shard_map/ppermute | solution.py:173
  40.6 1.2 collective-permute-done.9
  42.0 0.9 pad_maximum_fusion.1
  42.9 4.0 %all-to-all-done = f32[8,4,4096]{2,1,0:T(4,128)S(1)} async-done(((f32[8,4,4096]{2,1,0:T(4,128)}), f32[8,4,4096]{2,1,0:T(4,128)S(1)}, u32[]{:S(2)}, u32[]{:S(2)}) %all-to-all-start) | async-done | bytes 524320 | tf_op jit(solution)/shard_map/all_to_all | solution.py:206
  46.9 4.2 %all-to-all-start.1 = ((f16[8,4,4096]{2,1,0:T(4,128)(2,1)}), f16[8,4,4096]{2,1,0:T(4,128)(2,1)S(1)}, u32[]{:S(2)}, u32[]{:S(2)}) async-start(f16[8,4,4096]{2,1,0:T(4,128)(2,1)} %pad_maximum_fusion.1), calls=%async_computation.1 | async-start | bytes 524288 | tf_op jit(solution)/shard_map/all_to_all | solution.py:219
  51.1 9.2 %all-to-all-done.1 = f16[8,4,4096]{2,1,0:T(4,128)(2,1)S(1)} async-done(((f16[8,4,4096]{2,1,0:T(4,128)(2,1)}), f16[8,4,4096]{2,1,0:T(4,128)(2,1)S(1)}, u32[]{:S(2)}, u32[]{:S(2)}) %all-to-all-start.1) | async-done | bytes 262176 | tf_op jit(solution)/shard_map/all_to_all | solution.py:219
  61.1 1.4 %broadcast_in_dim.34 = f32[256,1,128]{2,1,0:T(1,128)} broadcast(f32[]{:T(128)} %multiply_reduce_fusion), dimensions={} | broadcast | bytes 131076 | tf_op jit(solution)/shard_map/broadcast_in_dim | solution.py:226
  62.5 8.8 %all-to-all-start.2 = ((f32[256,1,128]{2,1,0:T(1,128)}), f32[256,1,128]{2,1,0:T(1,128)S(1)}, u32[]{:S(2)}, u32[]{:S(2)}) async-start(f32[256,1,128]{2,1,0:T(1,128)} %broadcast_in_dim.34), calls=%async_computation.2 | async-start | bytes 262144 | tf_op jit(solution)/shard_map/all_to_all | solution.py:226
  71.3 1.7 %collective-permute-start.11 = (f32[4,4096]{1,0:T(4,128)S(1)}, f32[4,4096]{1,0:T(4,128)S(1)}, u32[]{:S(2)}, u32[]{:S(2)}) collective-permute-start(f32[4,4096]{1,0:T(4,128)S(1)} %broadcast_multiply_fusion), channel_id=1, source_target_pairs={{0,16},{16,32},{32,48},{48,64},{64,80},{80,96},{96,112},{112,0},{1... | collective-permute-start | bytes 196616 | tf_op jit(solution)/shard_map/ppermute | solution.py:173
  73.0 2.6 %collective-permute-start.12 = (f32[4,4096]{1,0:T(4,128)S(1)}, f32[4,4096]{1,0:T(4,128)S(1)}, u32[]{:S(2)}, u32[]{:S(2)}) collective-permute-start(f32[4,4096]{1,0:T(4,128)S(1)} %broadcast_multiply_fusion), channel_id=1, source_target_pairs={{0,32},{16,48},{32,64},{48,80},{64,96},{80,112},{96,0},{112,16},{1... | collective-permute-start | bytes 196616 | tf_op jit(solution)/shard_map/ppermute | solution.py:173
  75.7 3.3 %collective-permute-start.13 = (f32[4,4096]{1,0:T(4,128)S(1)}, f32[4,4096]{1,0:T(4,128)S(1)}, u32[]{:S(2)}, u32[]{:S(2)}) collective-permute-start(f32[4,4096]{1,0:T(4,128)S(1)} %broadcast_multiply_fusion), channel_id=1, source_target_pairs={{0,48},{16,64},{32,80},{48,96},{64,112},{80,0},{96,16},{112,32},{1... | collective-permute-start | bytes 196616 | tf_op jit(solution)/shard_map/ppermute | solution.py:173
  78.9 1.0 collective-permute-start.14
  80.0 3.7 %collective-permute-start.15 = (f32[4,4096]{1,0:T(4,128)S(1)}, f32[4,4096]{1,0:T(4,128)S(1)}, u32[]{:S(2)}, u32[]{:S(2)}) collective-permute-start(f32[4,4096]{1,0:T(4,128)S(1)} %broadcast_multiply_fusion), channel_id=1, source_target_pairs={{0,80},{16,96},{32,112},{48,0},{64,16},{80,32},{96,48},{112,64},{1... | collective-permute-start | bytes 196616 | tf_op jit(solution)/shard_map/ppermute | solution.py:173
  83.7 2.8 %collective-permute-start.16 = (f32[4,4096]{1,0:T(4,128)S(1)}, f32[4,4096]{1,0:T(4,128)S(1)}, u32[]{:S(2)}, u32[]{:S(2)}) collective-permute-start(f32[4,4096]{1,0:T(4,128)S(1)} %broadcast_multiply_fusion), channel_id=1, source_target_pairs={{0,96},{16,112},{32,0},{48,16},{64,32},{80,48},{96,64},{112,80},{1... | collective-permute-start | bytes 196616 | tf_op jit(solution)/shard_map/ppermute | solution.py:173
  86.5 0.9 collective-permute-start.17
  87.4 0.9 slice_reduce_fusion
  89.0 0.9 collective-permute-done.15
  89.8 3.9 %collective-permute-done.16 = f32[4,4096]{1,0:T(4,128)S(1)} collective-permute-done((f32[4,4096]{1,0:T(4,128)S(1)}, f32[4,4096]{1,0:T(4,128)S(1)}, u32[]{:S(2)}, u32[]{:S(2)}) %collective-permute-start.16) | collective-permute-done | bytes 65568 | tf_op jit(solution)/shard_map/ppermute | solution.py:173
  94.1 2.8 %collective-permute-start.24 = (bf16[32,2048]{1,0:T(8,128)(2,1)S(1)}, bf16[32,2048]{1,0:T(8,128)(2,1)S(1)}, u32[]{:S(2)}, u32[]{:S(2)}) collective-permute-start(bf16[32,2048]{1,0:T(8,128)(2,1)S(1)} %get-tuple-element.54), channel_id=1, source_target_pairs={{0,128},{128,0},{1,129},{129,1},{2,130},{130,2},{3,131},{131,3},{4... | collective-permute-start | bytes 393224 | tf_op jit(solution)/shard_map/ppermute | solution.py:173
  97.0 1.9 %collective-permute-start.10 = (f32[2,4096]{1,0:T(2,128)S(1)}, f32[2,4096]{1,0:T(2,128)S(1)}, u32[]{:S(2)}, u32[]{:S(2)}) collective-permute-start(f32[2,4096]{1,0:T(2,128)S(1)} %constant_dynamic-slice_fusion), channel_id=1, source_target_pairs={{0,2},{2,0},{1,3},{3,1},{4,6},{6,4},{5,7},{7,5},{8,10},{10,8},{9,1... | collective-permute-start | bytes 98312 | tf_op jit(solution)/shard_map/ppermute | solution.py:173
  98.9 1.2 collective-permute-start.18
  100.1 2.5 %collective-permute-start.19 = (bf16[32,2048]{1,0:T(8,128)(2,1)S(1)}, bf16[32,2048]{1,0:T(8,128)(2,1)S(1)}, u32[]{:S(2)}, u32[]{:S(2)}) collective-permute-start(bf16[32,2048]{1,0:T(8,128)(2,1)S(1)} %get-tuple-element.55), channel_id=1, source_target_pairs={{0,8},{4,12},{8,0},{12,4},{1,9},{5,13},{9,1},{13,5},{2,10},{6,14},... | collective-permute-start | bytes 393224 | tf_op jit(solution)/shard_map/ppermute | solution.py:173
  102.7 1.1 collective-permute-start.20
  105.1 1.6 %collective-permute-start.26 = (bf16[64,2048]{1,0:T(8,128)(2,1)S(1)}, bf16[64,2048]{1,0:T(8,128)(2,1)S(1)}, u32[]{:S(2)}, u32[]{:S(2)}) collective-permute-start(bf16[64,2048]{1,0:T(8,128)(2,1)S(1)} %pad_maximum_fusion.2.refs_0_), channel_id=1, source_target_pairs={{0,8},{4,12},{8,0},{12,4},{1,9},{5,13},{9,1},{13,5},{2,10},{6,14},... | collective-permute-start | bytes 786440 | tf_op jit(solution)/shard_map/ppermute | solution.py:173
  106.7 2.3 %collective-permute-done.19 = bf16[32,2048]{1,0:T(8,128)(2,1)S(1)} collective-permute-done((bf16[32,2048]{1,0:T(8,128)(2,1)S(1)}, bf16[32,2048]{1,0:T(8,128)(2,1)S(1)}, u32[]{:S(2)}, u32[]{:S(2)}) %collective-permute-start.19) | collective-permute-done | bytes 131104 | tf_op jit(solution)/shard_map/ppermute | solution.py:173
  109.0 1.6 %collective-permute-start.28 = (bf16[64,2048]{1,0:T(8,128)(2,1)S(1)}, bf16[64,2048]{1,0:T(8,128)(2,1)S(1)}, u32[]{:S(2)}, u32[]{:S(2)}) collective-permute-start(bf16[64,2048]{1,0:T(8,128)(2,1)S(1)} %pad_maximum_fusion.2.refs_0_), channel_id=1, source_target_pairs={{0,2},{2,0},{1,3},{3,1},{4,6},{6,4},{5,7},{7,5},{8,10},{10,8},{9,1... | collective-permute-start | bytes 786440 | tf_op jit(solution)/shard_map/ppermute | solution.py:173
  111.0 4.5 %collective-permute-done.25.refs_1_ = bf16[64,2048]{1,0:T(8,128)(2,1)S(1)} collective-permute-done((bf16[64,2048]{1,0:T(8,128)(2,1)S(1)}, bf16[64,2048]{1,0:T(8,128)(2,1)S(1)}, u32[]{:S(2)}, u32[]{:S(2)}) %collective-permute-start.25) | collective-permute-done | bytes 262176 | tf_op jit(solution)/shard_map/ppermute | solution.py:173
  116.1 4.1 %collective-permute-done.26.refs_2_ = bf16[64,2048]{1,0:T(8,128)(2,1)S(1)} collective-permute-done((bf16[64,2048]{1,0:T(8,128)(2,1)S(1)}, bf16[64,2048]{1,0:T(8,128)(2,1)S(1)}, u32[]{:S(2)}, u32[]{:S(2)}) %collective-permute-start.26) | collective-permute-done | bytes 262176 | tf_op jit(solution)/shard_map/ppermute | solution.py:173
  120.2 0.9 collective-permute-start.29
  121.7 4.0 %collective-permute-done.21.refs_1_ = bf16[128,2048]{1,0:T(8,128)(2,1)S(1)} collective-permute-done((bf16[128,2048]{1,0:T(8,128)(2,1)S(1)}, bf16[128,2048]{1,0:T(8,128)(2,1)S(1)}, u32[]{:S(2)}, u32[]{:S(2)}) %collective-permute-start.21) | collective-permute-done | bytes 524320 | tf_op jit(solution)/shard_map/ppermute | solution.py:173
  125.7 0.9 collective-permute-start.23
  127.3 2.6 %from_blocks.2.refs_4_ = bf16[256,8192]{1,0:T(8,128)(2,1)} custom-call(s32[1]{0:T(128)} %bitcast.2.core, bf16[256,256]{1,0:T(8,128)(2,1)S(1)} %fusion.5.one, bf16[64,2048]{1,0:T(8,128)(2,1)S(1)} %pad_maximum_fusion.2.refs_0_, bf16[64,2048]{1,0:T(8,128)(2,1)S(1)} %collective-permute-done.25.refs_1_, bf16[64,2048]{1,0:T(8,128)(2,1)S(1)} %collective-permute-done.26.refs_2_, ...), custom_call_target="tpu_custom_call" | custom-call | tf_op jit(solution)/shard_map/from_blocks/pallas_call | solution.py:144
  129.9 2.6 %from_blocks.3 = bf16[256,8192]{1,0:T(8,128)(2,1)} custom-call(s32[1]{0:T(128)} %bitcast.2.core, bf16[256,256]{1,0:T(8,128)(2,1)S(1)} %fusion.4.one, bf16[128,2048]{1,0:T(8,128)(2,1)S(1)} %pad_maximum_fusion.refs_0_, bf16[128,2048]{1,0:T(8,128)(2,1)S(1)} %collective-permute-done.21.refs_1_, ...), custom_call_target="tpu_custom_call", output_to_operand_aliasing={{}: (6, {})} | custom-call | tf_op jit(solution)/shard_map/from_blocks/pallas_call | solution.py:144
  (68 shorter events, 9.6 us)
Async XLA Ops:
  3.7 7.3 %collective-permute-start = (bf16[256,4096]{1,0:T(8,128)(2,1)}, bf16[256,4096]{1,0:T(8,128)(2,1)S(1)}, u32[]{:S(2)}, u32[]{:S(2)}) collective-permute-start(bf16[256,4096]{1,0:T(8,128)(2,1)} %pick.1), channel_id=1, source_target_pairs={{0,2},{2,0},{1,3},{3,1},{4,6},{6,4},{5,7},{7,5},{8,10},{10,8},{9,1... | collective-permute-start | bytes 6291464 | tf_op jit(solution)/shard_map/ppermute | solution.py:173
  10.0 3.9 %copy-start = (f32[1,2,8192]{2,1,0:T(2,128)S(1)}, f32[1,2,8192]{2,1,0:T(2,128)}, u32[]{:S(2)}) copy-start(f32[1,2,8192]{2,1,0:T(2,128)} %param.6) | copy-start | bytes 196612
  10.1 3.9 %copy-start.1 = (f32[1,2,8192]{2,1,0:T(2,128)S(1)}, f32[1,2,8192]{2,1,0:T(2,128)}, u32[]{:S(2)}) copy-start(f32[1,2,8192]{2,1,0:T(2,128)} %param.7) | copy-start | bytes 196612
  14.1 7.1 %collective-permute-start.1 = (f32[2,4096]{1,0:T(2,128)S(1)}, f32[2,4096]{1,0:T(2,128)S(1)}, u32[]{:S(2)}, u32[]{:S(2)}) collective-permute-start(f32[2,4096]{1,0:T(2,128)S(1)} %dynamic-slice_bitcast_fusion), channel_id=1, source_target_pairs={{0,2},{2,0},{1,3},{3,1},{4,6},{6,4},{5,7},{7,5},{8,10},{10,8},{9,1... | collective-permute-start | bytes 98312 | tf_op jit(solution)/shard_map/ppermute | solution.py:173
  14.6 15.8 %collective-permute-start.2 = (f16[64,2048]{1,0:T(8,128)(2,1)}, f16[64,2048]{1,0:T(8,128)(2,1)S(1)}, u32[]{:S(2)}, u32[]{:S(2)}) collective-permute-start(f16[64,2048]{1,0:T(8,128)(2,1)} %convert_element_type.93), channel_id=1, source_target_pairs={{0,8},{4,12},{8,0},{12,4},{1,9},{5,13},{9,1},{13,5},{2,10},{6,14},... | collective-permute-start | bytes 786440 | tf_op jit(solution)/shard_map/ppermute | solution.py:173
  15.8 14.6 %collective-permute-start.3 = (f16[64,2048]{1,0:T(8,128)(2,1)}, f16[64,2048]{1,0:T(8,128)(2,1)}, u32[]{:S(2)}, u32[]{:S(2)}) collective-permute-start(f16[64,2048]{1,0:T(8,128)(2,1)} %convert_element_type.92), channel_id=1, source_target_pairs={{0,4},{4,8},{8,12},{12,0},{1,5},{5,9},{9,13},{13,1},{2,6},{6,10},{... | collective-permute-start | bytes 786440 | tf_op jit(solution)/shard_map/ppermute | solution.py:173
  16.2 14.2 %collective-permute-start.4 = (f16[64,2048]{1,0:T(8,128)(2,1)}, f16[64,2048]{1,0:T(8,128)(2,1)}, u32[]{:S(2)}, u32[]{:S(2)}) collective-permute-start(f16[64,2048]{1,0:T(8,128)(2,1)} %convert_element_type.94), channel_id=1, source_target_pairs={{0,12},{4,0},{8,4},{12,8},{1,13},{5,1},{9,5},{13,9},{2,14},{6,2},{... | collective-permute-start | bytes 786440 | tf_op jit(solution)/shard_map/ppermute | solution.py:173
  18.5 14.1 %collective-permute-start.6 = (f16[128,2048]{1,0:T(8,128)(2,1)S(1)}, f16[128,2048]{1,0:T(8,128)(2,1)S(1)}, u32[]{:S(2)}, u32[]{:S(2)}) collective-permute-start(f16[128,2048]{1,0:T(8,128)(2,1)S(1)} %convert_element_type.91), channel_id=1, source_target_pairs={{0,128},{128,0},{1,129},{129,1},{2,130},{130,2},{3,131},{131,3},{4... | collective-permute-start | bytes 1572872 | tf_op jit(solution)/shard_map/ppermute | solution.py:173
  22.2 24.6 %all-to-all-start = ((f32[8,4,4096]{2,1,0:T(4,128)}), f32[8,4,4096]{2,1,0:T(4,128)S(1)}, u32[]{:S(2)}, u32[]{:S(2)}) async-start(f32[8,4,4096]{2,1,0:T(4,128)} %broadcast_in_dim.33), calls=%async_computation | async-start | bytes 1048576 | tf_op jit(solution)/shard_map/all_to_all | solution.py:206
  31.6 5.6 %collective-permute-start.5 = (f16[32,2048]{1,0:T(8,128)(2,1)S(1)}, f16[32,2048]{1,0:T(8,128)(2,1)S(1)}, u32[]{:S(2)}, u32[]{:S(2)}) collective-permute-start(f16[32,2048]{1,0:T(8,128)(2,1)S(1)} %slice_convert_fusion), channel_id=1, source_target_pairs={{0,128},{128,0},{1,129},{129,1},{2,130},{130,2},{3,131},{131,3},{4... | collective-permute-start | bytes 393224 | tf_op jit(solution)/shard_map/ppermute | solution.py:173
  32.8 5.7 %collective-permute-start.7 = (f16[32,2048]{1,0:T(8,128)(2,1)S(1)}, f16[32,2048]{1,0:T(8,128)(2,1)S(1)}, u32[]{:S(2)}, u32[]{:S(2)}) collective-permute-start(f16[32,2048]{1,0:T(8,128)(2,1)S(1)} %get-tuple-element.51), channel_id=1, source_target_pairs={{0,8},{4,12},{8,0},{12,4},{1,9},{5,13},{9,1},{13,5},{2,10},{6,14},... | collective-permute-start | bytes 393224 | tf_op jit(solution)/shard_map/ppermute | solution.py:173
  34.5 6.1 %collective-permute-start.8 = (f16[32,2048]{1,0:T(8,128)(2,1)S(1)}, f16[32,2048]{1,0:T(8,128)(2,1)S(1)}, u32[]{:S(2)}, u32[]{:S(2)}) collective-permute-start(f16[32,2048]{1,0:T(8,128)(2,1)S(1)} %get-tuple-element.53), channel_id=1, source_target_pairs={{0,4},{4,8},{8,12},{12,0},{1,5},{5,9},{9,13},{13,1},{2,6},{6,10},{... | collective-permute-start | bytes 393224 | tf_op jit(solution)/shard_map/ppermute | solution.py:173
  36.2 5.6 %collective-permute-start.9 = (f16[32,2048]{1,0:T(8,128)(2,1)S(1)}, f16[32,2048]{1,0:T(8,128)(2,1)S(1)}, u32[]{:S(2)}, u32[]{:S(2)}) collective-permute-start(f16[32,2048]{1,0:T(8,128)(2,1)S(1)} %get-tuple-element.52), channel_id=1, source_target_pairs={{0,12},{4,0},{8,4},{12,8},{1,13},{5,1},{9,5},{13,9},{2,14},{6,2},{... | collective-permute-start | bytes 393224 | tf_op jit(solution)/shard_map/ppermute | solution.py:173
  46.9 13.4 %all-to-all-start.1 = ((f16[8,4,4096]{2,1,0:T(4,128)(2,1)}), f16[8,4,4096]{2,1,0:T(4,128)(2,1)S(1)}, u32[]{:S(2)}, u32[]{:S(2)}) async-start(f16[8,4,4096]{2,1,0:T(4,128)(2,1)} %pad_maximum_fusion.1), calls=%async_computation.1 | async-start | bytes 524288 | tf_op jit(solution)/shard_map/all_to_all | solution.py:219
  62.5 24.9 %all-to-all-start.2 = ((f32[256,1,128]{2,1,0:T(1,128)}), f32[256,1,128]{2,1,0:T(1,128)S(1)}, u32[]{:S(2)}, u32[]{:S(2)}) async-start(f32[256,1,128]{2,1,0:T(1,128)} %broadcast_in_dim.34), calls=%async_computation.2 | async-start | bytes 262144 | tf_op jit(solution)/shard_map/all_to_all | solution.py:226
  71.3 12.4 %collective-permute-start.11 = (f32[4,4096]{1,0:T(4,128)S(1)}, f32[4,4096]{1,0:T(4,128)S(1)}, u32[]{:S(2)}, u32[]{:S(2)}) collective-permute-start(f32[4,4096]{1,0:T(4,128)S(1)} %broadcast_multiply_fusion), channel_id=1, source_target_pairs={{0,16},{16,32},{32,48},{48,64},{64,80},{80,96},{96,112},{112,0},{1... | collective-permute-start | bytes 196616 | tf_op jit(solution)/shard_map/ppermute | solution.py:173
  73.0 13.5 %collective-permute-start.12 = (f32[4,4096]{1,0:T(4,128)S(1)}, f32[4,4096]{1,0:T(4,128)S(1)}, u32[]{:S(2)}, u32[]{:S(2)}) collective-permute-start(f32[4,4096]{1,0:T(4,128)S(1)} %broadcast_multiply_fusion), channel_id=1, source_target_pairs={{0,32},{16,48},{32,64},{48,80},{64,96},{80,112},{96,0},{112,16},{1... | collective-permute-start | bytes 196616 | tf_op jit(solution)/shard_map/ppermute | solution.py:173
  75.7 13.3 %collective-permute-start.13 = (f32[4,4096]{1,0:T(4,128)S(1)}, f32[4,4096]{1,0:T(4,128)S(1)}, u32[]{:S(2)}, u32[]{:S(2)}) collective-permute-start(f32[4,4096]{1,0:T(4,128)S(1)} %broadcast_multiply_fusion), channel_id=1, source_target_pairs={{0,48},{16,64},{32,80},{48,96},{64,112},{80,0},{96,16},{112,32},{1... | collective-permute-start | bytes 196616 | tf_op jit(solution)/shard_map/ppermute | solution.py:173
  78.9 10.0 %collective-permute-start.14 = (f32[4,4096]{1,0:T(4,128)S(1)}, f32[4,4096]{1,0:T(4,128)S(1)}, u32[]{:S(2)}, u32[]{:S(2)}) collective-permute-start(f32[4,4096]{1,0:T(4,128)S(1)} %broadcast_multiply_fusion), channel_id=1, source_target_pairs={{0,64},{16,80},{32,96},{48,112},{64,0},{80,16},{96,32},{112,48},{1... | collective-permute-start | bytes 196616 | tf_op jit(solution)/shard_map/ppermute | solution.py:173
  80.0 9.9 %collective-permute-start.15 = (f32[4,4096]{1,0:T(4,128)S(1)}, f32[4,4096]{1,0:T(4,128)S(1)}, u32[]{:S(2)}, u32[]{:S(2)}) collective-permute-start(f32[4,4096]{1,0:T(4,128)S(1)} %broadcast_multiply_fusion), channel_id=1, source_target_pairs={{0,80},{16,96},{32,112},{48,0},{64,16},{80,32},{96,48},{112,64},{1... | collective-permute-start | bytes 196616 | tf_op jit(solution)/shard_map/ppermute | solution.py:173
  83.7 10.0 %collective-permute-start.16 = (f32[4,4096]{1,0:T(4,128)S(1)}, f32[4,4096]{1,0:T(4,128)S(1)}, u32[]{:S(2)}, u32[]{:S(2)}) collective-permute-start(f32[4,4096]{1,0:T(4,128)S(1)} %broadcast_multiply_fusion), channel_id=1, source_target_pairs={{0,96},{16,112},{32,0},{48,16},{64,32},{80,48},{96,64},{112,80},{1... | collective-permute-start | bytes 196616 | tf_op jit(solution)/shard_map/ppermute | solution.py:173
  86.5 7.3 %collective-permute-start.17 = (f32[4,4096]{1,0:T(4,128)S(1)}, f32[4,4096]{1,0:T(4,128)S(1)}, u32[]{:S(2)}, u32[]{:S(2)}) collective-permute-start(f32[4,4096]{1,0:T(4,128)S(1)} %broadcast_multiply_fusion), channel_id=1, source_target_pairs={{0,112},{16,0},{32,16},{48,32},{64,48},{80,64},{96,80},{112,96},{1... | collective-permute-start | bytes 196616 | tf_op jit(solution)/shard_map/ppermute | solution.py:173
  94.1 9.6 %collective-permute-start.24 = (bf16[32,2048]{1,0:T(8,128)(2,1)S(1)}, bf16[32,2048]{1,0:T(8,128)(2,1)S(1)}, u32[]{:S(2)}, u32[]{:S(2)}) collective-permute-start(bf16[32,2048]{1,0:T(8,128)(2,1)S(1)} %get-tuple-element.54), channel_id=1, source_target_pairs={{0,128},{128,0},{1,129},{129,1},{2,130},{130,2},{3,131},{131,3},{4... | collective-permute-start | bytes 393224 | tf_op jit(solution)/shard_map/ppermute | solution.py:173
  97.0 13.6 %collective-permute-start.10 = (f32[2,4096]{1,0:T(2,128)S(1)}, f32[2,4096]{1,0:T(2,128)S(1)}, u32[]{:S(2)}, u32[]{:S(2)}) collective-permute-start(f32[2,4096]{1,0:T(2,128)S(1)} %constant_dynamic-slice_fusion), channel_id=1, source_target_pairs={{0,2},{2,0},{1,3},{3,1},{4,6},{6,4},{5,7},{7,5},{8,10},{10,8},{9,1... | collective-permute-start | bytes 98312 | tf_op jit(solution)/shard_map/ppermute | solution.py:173
  98.9 6.2 %collective-permute-start.18 = (bf16[32,2048]{1,0:T(8,128)(2,1)S(1)}, bf16[32,2048]{1,0:T(8,128)(2,1)S(1)}, u32[]{:S(2)}, u32[]{:S(2)}) collective-permute-start(bf16[32,2048]{1,0:T(8,128)(2,1)S(1)} %get-tuple-element.55), channel_id=1, source_target_pairs={{0,4},{4,8},{8,12},{12,0},{1,5},{5,9},{9,13},{13,1},{2,6},{6,10},{... | collective-permute-start | bytes 393224 | tf_op jit(solution)/shard_map/ppermute | solution.py:173
  100.1 8.8 %collective-permute-start.19 = (bf16[32,2048]{1,0:T(8,128)(2,1)S(1)}, bf16[32,2048]{1,0:T(8,128)(2,1)S(1)}, u32[]{:S(2)}, u32[]{:S(2)}) collective-permute-start(bf16[32,2048]{1,0:T(8,128)(2,1)S(1)} %get-tuple-element.55), channel_id=1, source_target_pairs={{0,8},{4,12},{8,0},{12,4},{1,9},{5,13},{9,1},{13,5},{2,10},{6,14},... | collective-permute-start | bytes 393224 | tf_op jit(solution)/shard_map/ppermute | solution.py:173
  102.7 6.3 %collective-permute-start.20 = (bf16[32,2048]{1,0:T(8,128)(2,1)S(1)}, bf16[32,2048]{1,0:T(8,128)(2,1)S(1)}, u32[]{:S(2)}, u32[]{:S(2)}) collective-permute-start(bf16[32,2048]{1,0:T(8,128)(2,1)S(1)} %get-tuple-element.55), channel_id=1, source_target_pairs={{0,12},{4,0},{8,4},{12,8},{1,13},{5,1},{9,5},{13,9},{2,14},{6,2},{... | collective-permute-start | bytes 393224 | tf_op jit(solution)/shard_map/ppermute | solution.py:173
  103.8 11.7 %collective-permute-start.25 = (bf16[64,2048]{1,0:T(8,128)(2,1)S(1)}, bf16[64,2048]{1,0:T(8,128)(2,1)S(1)}, u32[]{:S(2)}, u32[]{:S(2)}) collective-permute-start(bf16[64,2048]{1,0:T(8,128)(2,1)S(1)} %pad_maximum_fusion.2.refs_0_), channel_id=1, source_target_pairs={{0,4},{4,8},{8,12},{12,0},{1,5},{5,9},{9,13},{13,1},{2,6},{6,10},{... | collective-permute-start | bytes 786440 | tf_op jit(solution)/shard_map/ppermute | solution.py:173
  105.1 15.1 %collective-permute-start.26 = (bf16[64,2048]{1,0:T(8,128)(2,1)S(1)}, bf16[64,2048]{1,0:T(8,128)(2,1)S(1)}, u32[]{:S(2)}, u32[]{:S(2)}) collective-permute-start(bf16[64,2048]{1,0:T(8,128)(2,1)S(1)} %pad_maximum_fusion.2.refs_0_), channel_id=1, source_target_pairs={{0,8},{4,12},{8,0},{12,4},{1,9},{5,13},{9,1},{13,5},{2,10},{6,14},... | collective-permute-start | bytes 786440 | tf_op jit(solution)/shard_map/ppermute | solution.py:173
  109.0 12.2 %collective-permute-start.27 = (bf16[64,2048]{1,0:T(8,128)(2,1)S(1)}, bf16[64,2048]{1,0:T(8,128)(2,1)S(1)}, u32[]{:S(2)}, u32[]{:S(2)}) collective-permute-start(bf16[64,2048]{1,0:T(8,128)(2,1)S(1)} %pad_maximum_fusion.2.refs_0_), channel_id=1, source_target_pairs={{0,12},{4,0},{8,4},{12,8},{1,13},{5,1},{9,5},{13,9},{2,14},{6,2},{... | collective-permute-start | bytes 786440 | tf_op jit(solution)/shard_map/ppermute | solution.py:173
  109.0 12.2 %collective-permute-start.28 = (bf16[64,2048]{1,0:T(8,128)(2,1)S(1)}, bf16[64,2048]{1,0:T(8,128)(2,1)S(1)}, u32[]{:S(2)}, u32[]{:S(2)}) collective-permute-start(bf16[64,2048]{1,0:T(8,128)(2,1)S(1)} %pad_maximum_fusion.2.refs_0_), channel_id=1, source_target_pairs={{0,2},{2,0},{1,3},{3,1},{4,6},{6,4},{5,7},{7,5},{8,10},{10,8},{9,1... | collective-permute-start | bytes 786440 | tf_op jit(solution)/shard_map/ppermute | solution.py:173
  110.6 15.1 %collective-permute-start.21 = (bf16[128,2048]{1,0:T(8,128)(2,1)S(1)}, bf16[128,2048]{1,0:T(8,128)(2,1)S(1)}, u32[]{:S(2)}, u32[]{:S(2)}) collective-permute-start(bf16[128,2048]{1,0:T(8,128)(2,1)S(1)} %pad_maximum_fusion.refs_0_), channel_id=1, source_target_pairs={{0,128},{128,0},{1,129},{129,1},{2,130},{130,2},{3,131},{131,3},{4... | collective-permute-start | bytes 1572872 | tf_op jit(solution)/shard_map/ppermute | solution.py:173
  115.5 14.5 %collective-permute-start.22 = (bf16[128,2048]{1,0:T(8,128)(2,1)S(1)}, bf16[128,2048]{1,0:T(8,128)(2,1)S(1)}, u32[]{:S(2)}, u32[]{:S(2)}) collective-permute-start(bf16[128,2048]{1,0:T(8,128)(2,1)S(1)} %pad_maximum_fusion.refs_0_), channel_id=1, source_target_pairs={{0,2},{2,0},{1,3},{3,1},{4,6},{6,4},{5,7},{7,5},{8,10},{10,8},{9,1... | collective-permute-start | bytes 1572872 | tf_op jit(solution)/shard_map/ppermute | solution.py:173
  120.2 7.1 %collective-permute-start.29 = (bf16[64,2048]{1,0:T(8,128)(2,1)S(1)}, bf16[64,2048]{1,0:T(8,128)(2,1)S(1)}, u32[]{:S(2)}, u32[]{:S(2)}) collective-permute-start(bf16[64,2048]{1,0:T(8,128)(2,1)S(1)} %collective-permute-done.25.refs_1_), channel_id=1, source_target_pairs={{0,2},{2,0},{1,3},{3,1},{4,6},{6,4},{5,7},{7,5},{8,10},{10,8},{9,1... | collective-permute-start | bytes 786440 | tf_op jit(solution)/shard_map/ppermute | solution.py:173
  121.2 6.2 %collective-permute-start.30 = (bf16[64,2048]{1,0:T(8,128)(2,1)S(1)}, bf16[64,2048]{1,0:T(8,128)(2,1)S(1)}, u32[]{:S(2)}, u32[]{:S(2)}) collective-permute-start(bf16[64,2048]{1,0:T(8,128)(2,1)S(1)} %collective-permute-done.26.refs_2_), channel_id=1, source_target_pairs={{0,2},{2,0},{1,3},{3,1},{4,6},{6,4},{5,7},{7,5},{8,10},{10,8},{9,1... | collective-permute-start | bytes 786440 | tf_op jit(solution)/shard_map/ppermute | solution.py:173
  121.2 6.1 %collective-permute-start.31 = (bf16[64,2048]{1,0:T(8,128)(2,1)S(1)}, bf16[64,2048]{1,0:T(8,128)(2,1)S(1)}, u32[]{:S(2)}, u32[]{:S(2)}) collective-permute-start(bf16[64,2048]{1,0:T(8,128)(2,1)S(1)} %collective-permute-done.27.refs_3_), channel_id=1, source_target_pairs={{0,2},{2,0},{1,3},{3,1},{4,6},{6,4},{5,7},{7,5},{8,10},{10,8},{9,1... | collective-permute-start | bytes 786440 | tf_op jit(solution)/shard_map/ppermute | solution.py:173
  125.7 4.3 %collective-permute-start.23 = (bf16[128,2048]{1,0:T(8,128)(2,1)S(1)}, bf16[128,2048]{1,0:T(8,128)(2,1)S(1)}, u32[]{:S(2)}, u32[]{:S(2)}) collective-permute-start(bf16[128,2048]{1,0:T(8,128)(2,1)S(1)} %collective-permute-done.21.refs_1_), channel_id=1, source_target_pairs={{0,2},{2,0},{1,3},{3,1},{4,6},{6,4},{5,7},{7,5},{8,10},{10,8},{9,1... | collective-permute-start | bytes 1572872 | tf_op jit(solution)/shard_map/ppermute | solution.py:173

commit v5 on v4

--- a/solution.py
+++ b/solution.py
@@ -51,7 +51,7 @@
         out_specs=VMEM,
         out_shape=jax.ShapeDtypeStruct((rows, cols // 2), local.dtype),
         scratch_shapes=[pltpu.SemaphoreType.DMA],
-        compiler_params=pltpu.CompilerParams(vmem_limit_bytes=59 * MIB),
+        compiler_params=pltpu.CompilerParams(vmem_limit_bytes=50 * MIB),
         name="pick",
     )(core, local)
 
@@ -239,13 +239,14 @@
     arrived = {j: send(second, "y", j) for j in far_y}
     second = jnp.concatenate([second] + [arrived[j] for j in range(1, ny)], axis=0)
     first = jnp.concatenate([first, send(first, "xh", 1)], axis=0)
+    mine = [second, send(second, "xh", 1)]
+    theirs = [send(x, "c", 1) for x in mine]
+    new_params = from_blocks(core1, back_x.astype(jnp.bfloat16), mine, theirs, 1)
     arrived = {j: send(first, "y", j) for j in far_y}
+    arrived, new_params = lax.optimization_barrier((arrived, new_params))
     mine = [first] + [arrived[j] for j in range(1, ny)]
     theirs = [send(x, "c", 1) for x in mine]
-    new_params = from_blocks(core1, back_y.astype(jnp.bfloat16), mine, theirs, 0)
-    mine = [second, send(second, "xh", 1)]
-    theirs = [send(x, "c", 1) for x in mine]
-    new_params = from_blocks(core1, back_x.astype(jnp.bfloat16), mine, theirs, 1, new_params)
+    new_params = from_blocks(core1, back_y.astype(jnp.bfloat16), mine, theirs, 0, new_params)
 
     other = send(part(grad, at[3], 0), "c", 1)
     own = part(grad, at[2], 0)

time: 133 us -> 128 us (0.962)
  waiting for transfers between devices: 39.2 us -> 30.1 us
  starting transfers between devices: 69.4 us -> 75.6 us
  Pallas kernels: 11.9 us -> 10.5 us
    ppermute x32, waiting for transfers between devices: 26 us -> 16.9 us  [send(): return lax.ppermute(x, axis, shift(axis, by))]
    ppermute x32, starting transfers between devices: 48.3 us -> 54.3 us  [send(): return lax.ppermute(x, axis, shift(axis, by))]
  transfers between devices with their start and end apart: 35 -> 35, of which waited for: 13 -> 15; matrix products, arithmetic and copies ran while one was open for 4% -> 4% of each run, Pallas kernels for 4% -> 4%
where the time goes in v5:
time: 128 us
  starting transfers between devices  75.6 us (59%)
  waiting for transfers between devices  30.1 us (24%)
  Pallas kernels  10.5 us (8%)
  other arithmetic  6.98 us (5%)
  local copies, waits for them, and re-layouts  2.76 us (2%)
  between operations  1.63 us (1%)
    ppermute x32, starting transfers between devices, send(): return lax.ppermute(x, axis, shift(axis, by))  54.3 us
    ppermute x32, waiting for transfers between devices, send(): return lax.ppermute(x, axis, shift(axis, by))  16.9 us
    all_to_all x1, waiting for transfers between devices, step(): total = wide(lax.all_to_all(total, 'z', 0, 0, tiled=True)).sum(axis=0)  9.25 us
    all_to_all x1, starting transfers between devices, step(): lax.all_to_all(jnp.full((members, 1, 128), jnp.sum(grad * grad)), ALL, 0,...  8.82 us
    all_to_all x1, starting transfers between devices, step(): lax.all_to_all(jnp.broadcast_to(base[None], (nz, 4, half)), 'z', 0, 0, ti...  8.19 us
    pallas_call x2, Pallas kernels, from_blocks(): pl.pallas_call(from_blocks_kernel, grid_spec=pltpu.PrefetchScalarGridSpec...  5.16 us
    all_to_all x1, starting transfers between devices, step(): total = wide(lax.all_to_all(total, 'z', 0, 0, tiled=True)).sum(axis=0)  4.25 us
    all_to_all x1, waiting for transfers between devices, step(): lax.all_to_all(jnp.broadcast_to(base[None], (nz, 4, half)), 'z', 0, 0, ti...  3.94 us
  transfers between devices with their start and end apart: 35, of which 15 were waited for; matrix products, arithmetic and copies ran while one was open for 4% of the time, Pallas kernels for 4%

profile of v5, /device:TPU:1, one launch (start us, length us, event | category | flops | bytes accessed | tf_op | source)
XLA Modules:
  0.0 127.6 jit_solution(7154057664411838149)
XLA Ops:
  0.8 1.6 %pick.1 = bf16[256,4096]{1,0:T(8,128)(2,1)S(1)} custom-call(s32[1]{0:T(128)} %bitcast.2.core, bf16[256,8192]{1,0:T(8,128)(2,1)} %bitcast.45), custom_call_target="tpu_custom_call" | custom-call | tf_op jit(solution)/shard_map/pick/pallas_call | solution.py:48
  2.4 3.3 %collective-permute-start = (bf16[256,4096]{1,0:T(8,128)(2,1)S(1)}, bf16[256,4096]{1,0:T(8,128)(2,1)S(1)}, u32[]{:S(2)}, u32[]{:S(2)}) collective-permute-start(bf16[256,4096]{1,0:T(8,128)(2,1)S(1)} %pick.1), channel_id=1, source_target_pairs={{0,2},{2,0},{1,3},{3,1},{4,6},{6,4},{5,7},{7,5},{8,10},{10,8},{9,1... | collective-permute-start | bytes 6291464 | tf_op jit(solution)/shard_map/ppermute | solution.py:173
  5.7 3.0 %change.1.own = f32[256,4096]{1,0:T(8,128)S(1)} custom-call(s32[1]{0:T(128)} %bitcast.2.core, bf16[256,256]{1,0:T(8,128)(2,1)S(1)} %select_convert_fusion.one, bf16[256,8192]{1,0:T(8,128)(2,1)} %bitcast.46, bf16[256,8192]{1,0:T(8,128)(2,1)} %bitcast.48), custom_call_target="tpu_custom_call" | custom-call | tf_op jit(solution)/shard_map/change/pallas_call | solution.py:80
  12.4 1.2 collective-permute-start.2
  14.0 2.3 %collective-permute-start.4 = (f16[64,2048]{1,0:T(8,128)(2,1)S(1)}, f16[64,2048]{1,0:T(8,128)(2,1)}, u32[]{:S(2)}, u32[]{:S(2)}) collective-permute-start(f16[64,2048]{1,0:T(8,128)(2,1)S(1)} %convert_element_type.94), channel_id=1, source_target_pairs={{0,12},{4,0},{8,4},{12,8},{1,13},{5,1},{9,5},{13,9},{2,14},{6,2},{... | collective-permute-start | bytes 786440 | tf_op jit(solution)/shard_map/ppermute | solution.py:173
  16.3 2.7 %collective-permute-start.6 = (f16[128,2048]{1,0:T(8,128)(2,1)S(1)}, f16[128,2048]{1,0:T(8,128)(2,1)S(1)}, u32[]{:S(2)}, u32[]{:S(2)}) collective-permute-start(f16[128,2048]{1,0:T(8,128)(2,1)S(1)} %convert_element_type.91), channel_id=1, source_target_pairs={{0,128},{128,0},{1,129},{129,1},{2,130},{130,2},{3,131},{131,3},{4... | collective-permute-start | bytes 1572872 | tf_op jit(solution)/shard_map/ppermute | solution.py:173
  19.2 0.9 broadcast_in_dim.33
  20.0 8.2 %all-to-all-start = ((f32[8,4,4096]{2,1,0:T(4,128)}), f32[8,4,4096]{2,1,0:T(4,128)S(1)}, u32[]{:S(2)}, u32[]{:S(2)}) async-start(f32[8,4,4096]{2,1,0:T(4,128)} %broadcast_in_dim.33), calls=%async_computation | async-start | bytes 1048576 | tf_op jit(solution)/shard_map/all_to_all | solution.py:206
  28.2 1.2 convert_add_fusion.1
  29.5 0.9 collective-permute-start.5
  30.7 1.7 %collective-permute-start.7 = (f16[32,2048]{1,0:T(8,128)(2,1)S(1)}, f16[32,2048]{1,0:T(8,128)(2,1)S(1)}, u32[]{:S(2)}, u32[]{:S(2)}) collective-permute-start(f16[32,2048]{1,0:T(8,128)(2,1)S(1)} %get-tuple-element.59), channel_id=1, source_target_pairs={{0,8},{4,12},{8,0},{12,4},{1,9},{5,13},{9,1},{13,5},{2,10},{6,14},... | collective-permute-start | bytes 393224 | tf_op jit(solution)/shard_map/ppermute | solution.py:173
  32.4 1.7 %collective-permute-start.8 = (f16[32,2048]{1,0:T(8,128)(2,1)S(1)}, f16[32,2048]{1,0:T(8,128)(2,1)S(1)}, u32[]{:S(2)}, u32[]{:S(2)}) collective-permute-start(f16[32,2048]{1,0:T(8,128)(2,1)S(1)} %get-tuple-element.61), channel_id=1, source_target_pairs={{0,4},{4,8},{8,12},{12,0},{1,5},{5,9},{9,13},{13,1},{2,6},{6,10},{... | collective-permute-start | bytes 393224 | tf_op jit(solution)/shard_map/ppermute | solution.py:173
  34.1 1.0 collective-permute-start.9
  35.2 1.2 collective-permute-done.7
  36.4 2.2 %collective-permute-done.8 = f16[32,2048]{1,0:T(8,128)(2,1)S(1)} collective-permute-done((f16[32,2048]{1,0:T(8,128)(2,1)S(1)}, f16[32,2048]{1,0:T(8,128)(2,1)S(1)}, u32[]{:S(2)}, u32[]{:S(2)}) %collective-permute-start.8) | collective-permute-done | bytes 131104 | tf_op jit(solution)/shard_map/ppermute | solution.py:173
  38.6 1.1 collective-permute-done.9
  39.8 0.9 pad_maximum_fusion.1
  40.7 3.9 %all-to-all-done = f32[8,4,4096]{2,1,0:T(4,128)S(1)} async-done(((f32[8,4,4096]{2,1,0:T(4,128)}), f32[8,4,4096]{2,1,0:T(4,128)S(1)}, u32[]{:S(2)}, u32[]{:S(2)}) %all-to-all-start) | async-done | bytes 524320 | tf_op jit(solution)/shard_map/all_to_all | solution.py:206
  44.6 4.3 %all-to-all-start.1 = ((f16[8,4,4096]{2,1,0:T(4,128)(2,1)}), f16[8,4,4096]{2,1,0:T(4,128)(2,1)S(1)}, u32[]{:S(2)}, u32[]{:S(2)}) async-start(f16[8,4,4096]{2,1,0:T(4,128)(2,1)} %pad_maximum_fusion.1), calls=%async_computation.1 | async-start | bytes 524288 | tf_op jit(solution)/shard_map/all_to_all | solution.py:219
  48.9 9.2 %all-to-all-done.1 = f16[8,4,4096]{2,1,0:T(4,128)(2,1)S(1)} async-done(((f16[8,4,4096]{2,1,0:T(4,128)(2,1)}), f16[8,4,4096]{2,1,0:T(4,128)(2,1)S(1)}, u32[]{:S(2)}, u32[]{:S(2)}) %all-to-all-start.1) | async-done | bytes 262176 | tf_op jit(solution)/shard_map/all_to_all | solution.py:219
  58.9 1.4 %broadcast_in_dim.34 = f32[256,1,128]{2,1,0:T(1,128)} broadcast(f32[]{:T(128)} %multiply_reduce_fusion), dimensions={} | broadcast | bytes 131076 | tf_op jit(solution)/shard_map/broadcast_in_dim | solution.py:226
  60.3 8.8 %all-to-all-start.2 = ((f32[256,1,128]{2,1,0:T(1,128)}), f32[256,1,128]{2,1,0:T(1,128)S(1)}, u32[]{:S(2)}, u32[]{:S(2)}) async-start(f32[256,1,128]{2,1,0:T(1,128)} %broadcast_in_dim.34), calls=%async_computation.2 | async-start | bytes 262144 | tf_op jit(solution)/shard_map/all_to_all | solution.py:226
  69.2 1.7 %collective-permute-start.11 = (f32[4,4096]{1,0:T(4,128)S(1)}, f32[4,4096]{1,0:T(4,128)S(1)}, u32[]{:S(2)}, u32[]{:S(2)}) collective-permute-start(f32[4,4096]{1,0:T(4,128)S(1)} %broadcast_multiply_fusion), channel_id=1, source_target_pairs={{0,16},{16,32},{32,48},{48,64},{64,80},{80,96},{96,112},{112,0},{1... | collective-permute-start | bytes 196616 | tf_op jit(solution)/shard_map/ppermute | solution.py:173
  70.9 2.6 %collective-permute-start.12 = (f32[4,4096]{1,0:T(4,128)S(1)}, f32[4,4096]{1,0:T(4,128)S(1)}, u32[]{:S(2)}, u32[]{:S(2)}) collective-permute-start(f32[4,4096]{1,0:T(4,128)S(1)} %broadcast_multiply_fusion), channel_id=1, source_target_pairs={{0,32},{16,48},{32,64},{48,80},{64,96},{80,112},{96,0},{112,16},{1... | collective-permute-start | bytes 196616 | tf_op jit(solution)/shard_map/ppermute | solution.py:173
  73.6 3.3 %collective-permute-start.13 = (f32[4,4096]{1,0:T(4,128)S(1)}, f32[4,4096]{1,0:T(4,128)S(1)}, u32[]{:S(2)}, u32[]{:S(2)}) collective-permute-start(f32[4,4096]{1,0:T(4,128)S(1)} %broadcast_multiply_fusion), channel_id=1, source_target_pairs={{0,48},{16,64},{32,80},{48,96},{64,112},{80,0},{96,16},{112,32},{1... | collective-permute-start | bytes 196616 | tf_op jit(solution)/shard_map/ppermute | solution.py:173
  76.8 1.0 collective-permute-start.14
  77.8 3.7 %collective-permute-start.15 = (f32[4,4096]{1,0:T(4,128)S(1)}, f32[4,4096]{1,0:T(4,128)S(1)}, u32[]{:S(2)}, u32[]{:S(2)}) collective-permute-start(f32[4,4096]{1,0:T(4,128)S(1)} %broadcast_multiply_fusion), channel_id=1, source_target_pairs={{0,80},{16,96},{32,112},{48,0},{64,16},{80,32},{96,48},{112,64},{1... | collective-permute-start | bytes 196616 | tf_op jit(solution)/shard_map/ppermute | solution.py:173
  81.6 2.8 %collective-permute-start.16 = (f32[4,4096]{1,0:T(4,128)S(1)}, f32[4,4096]{1,0:T(4,128)S(1)}, u32[]{:S(2)}, u32[]{:S(2)}) collective-permute-start(f32[4,4096]{1,0:T(4,128)S(1)} %broadcast_multiply_fusion), channel_id=1, source_target_pairs={{0,96},{16,112},{32,0},{48,16},{64,32},{80,48},{96,64},{112,80},{1... | collective-permute-start | bytes 196616 | tf_op jit(solution)/shard_map/ppermute | solution.py:173
  84.3 0.9 collective-permute-start.17
  85.3 0.9 slice_reduce_fusion
  86.8 0.9 collective-permute-done.15
  87.7 3.9 %collective-permute-done.16 = f32[4,4096]{1,0:T(4,128)S(1)} collective-permute-done((f32[4,4096]{1,0:T(4,128)S(1)}, f32[4,4096]{1,0:T(4,128)S(1)}, u32[]{:S(2)}, u32[]{:S(2)}) %collective-permute-start.16) | collective-permute-done | bytes 65568 | tf_op jit(solution)/shard_map/ppermute | solution.py:173
  92.0 1.3 %collective-permute-start.22 = (bf16[32,2048]{1,0:T(8,128)(2,1)S(1)}, bf16[32,2048]{1,0:T(8,128)(2,1)S(1)}, u32[]{:S(2)}, u32[]{:S(2)}) collective-permute-start(bf16[32,2048]{1,0:T(8,128)(2,1)S(1)} %get-tuple-element.62), channel_id=1, source_target_pairs={{0,4},{4,8},{8,12},{12,0},{1,5},{5,9},{9,13},{13,1},{2,6},{6,10},{... | collective-permute-start | bytes 393224 | tf_op jit(solution)/shard_map/ppermute | solution.py:173
  93.4 2.5 %collective-permute-start.23 = (bf16[32,2048]{1,0:T(8,128)(2,1)S(1)}, bf16[32,2048]{1,0:T(8,128)(2,1)S(1)}, u32[]{:S(2)}, u32[]{:S(2)}) collective-permute-start(bf16[32,2048]{1,0:T(8,128)(2,1)S(1)} %get-tuple-element.62), channel_id=1, source_target_pairs={{0,8},{4,12},{8,0},{12,4},{1,9},{5,13},{9,1},{13,5},{2,10},{6,14},... | collective-permute-start | bytes 393224 | tf_op jit(solution)/shard_map/ppermute | solution.py:173
  95.9 1.1 collective-permute-start.24
  97.0 2.8 %collective-permute-start.18 = (bf16[32,2048]{1,0:T(8,128)(2,1)S(1)}, bf16[32,2048]{1,0:T(8,128)(2,1)S(1)}, u32[]{:S(2)}, u32[]{:S(2)}) collective-permute-start(bf16[32,2048]{1,0:T(8,128)(2,1)S(1)} %get-tuple-element.63), channel_id=1, source_target_pairs={{0,128},{128,0},{1,129},{129,1},{2,130},{130,2},{3,131},{131,3},{4... | collective-permute-start | bytes 393224 | tf_op jit(solution)/shard_map/ppermute | solution.py:173
  100.9 2.8 %collective-permute-start.25 = (bf16[128,2048]{1,0:T(8,128)(2,1)S(1)}, bf16[128,2048]{1,0:T(8,128)(2,1)S(1)}, u32[]{:S(2)}, u32[]{:S(2)}) collective-permute-start(bf16[128,2048]{1,0:T(8,128)(2,1)S(1)} %pad_maximum_fusion.refs_0_), channel_id=1, source_target_pairs={{0,128},{128,0},{1,129},{129,1},{2,130},{130,2},{3,131},{131,3},{4... | collective-permute-start | bytes 1572872 | tf_op jit(solution)/shard_map/ppermute | solution.py:173
  103.7 2.7 %collective-permute-start.10 = (f32[2,4096]{1,0:T(2,128)S(1)}, f32[2,4096]{1,0:T(2,128)S(1)}, u32[]{:S(2)}, u32[]{:S(2)}) collective-permute-start(f32[2,4096]{1,0:T(2,128)S(1)} %constant_dynamic-slice_fusion), channel_id=1, source_target_pairs={{0,2},{2,0},{1,3},{3,1},{4,6},{6,4},{5,7},{7,5},{8,10},{10,8},{9,1... | collective-permute-start | bytes 98312 | tf_op jit(solution)/shard_map/ppermute | solution.py:173
  106.6 1.0 collective-permute-start.19
  107.5 2.7 %collective-permute-start.20 = (bf16[64,2048]{1,0:T(8,128)(2,1)S(1)}, bf16[64,2048]{1,0:T(8,128)(2,1)S(1)}, u32[]{:S(2)}, u32[]{:S(2)}) collective-permute-start(bf16[64,2048]{1,0:T(8,128)(2,1)S(1)} %pad_maximum_fusion.2.refs_0_), channel_id=1, source_target_pairs={{0,8},{4,12},{8,0},{12,4},{1,9},{5,13},{9,1},{13,5},{2,10},{6,14},... | collective-permute-start | bytes 786440 | tf_op jit(solution)/shard_map/ppermute | solution.py:173
  110.2 0.8 collective-permute-start.21
  111.0 3.4 %collective-permute-done.25.refs_1_ = bf16[128,2048]{1,0:T(8,128)(2,1)S(1)} collective-permute-done((bf16[128,2048]{1,0:T(8,128)(2,1)S(1)}, bf16[128,2048]{1,0:T(8,128)(2,1)S(1)}, u32[]{:S(2)}, u32[]{:S(2)}) %collective-permute-start.25) | collective-permute-done | bytes 524320 | tf_op jit(solution)/shard_map/ppermute | solution.py:173
  114.4 2.8 %collective-permute-start.27 = (bf16[128,2048]{1,0:T(8,128)(2,1)S(1)}, bf16[128,2048]{1,0:T(8,128)(2,1)S(1)}, u32[]{:S(2)}, u32[]{:S(2)}) collective-permute-start(bf16[128,2048]{1,0:T(8,128)(2,1)S(1)} %collective-permute-done.25.refs_1_), channel_id=1, source_target_pairs={{0,2},{2,0},{1,3},{3,1},{4,6},{6,4},{5,7},{7,5},{8,10},{10,8},{9,1... | collective-permute-start | bytes 1572872 | tf_op jit(solution)/shard_map/ppermute | solution.py:173
  117.3 1.4 %collective-permute-done.27.refs_3_ = bf16[128,2048]{1,0:T(8,128)(2,1)S(1)} collective-permute-done((bf16[128,2048]{1,0:T(8,128)(2,1)S(1)}, bf16[128,2048]{1,0:T(8,128)(2,1)S(1)}, u32[]{:S(2)}, u32[]{:S(2)}) %collective-permute-start.27) | collective-permute-done | bytes 524320 | tf_op jit(solution)/shard_map/ppermute | solution.py:173
  118.7 2.6 %from_blocks.2.refs_8_ = bf16[256,8192]{1,0:T(8,128)(2,1)} custom-call(s32[1]{0:T(128)} %bitcast.2.core, bf16[256,256]{1,0:T(8,128)(2,1)S(1)} %fusion.5.one, bf16[128,2048]{1,0:T(8,128)(2,1)S(1)} %pad_maximum_fusion.refs_0_, bf16[128,2048]{1,0:T(8,128)(2,1)S(1)} %collective-permute-done.25.refs_1_, bf16[128,2048]{1,0:T(8,128)(2,1)S(1)} %collective-permute-done.26.refs_2_, ...), custom_call_target="tpu_custom_call" | custom-call | tf_op jit(solution)/shard_map/from_blocks/pallas_call | solution.py:144
  121.8 1.3 collective-permute-start.29
  123.6 0.8 multiply_subtract_fusion
  125.0 2.6 %from_blocks.3 = bf16[256,8192]{1,0:T(8,128)(2,1)} custom-call(s32[1]{0:T(128)} %bitcast.2.core, bf16[256,256]{1,0:T(8,128)(2,1)S(1)} %fusion.4.one, bf16[64,2048]{1,0:T(8,128)(2,1)S(1)} %pad_maximum_fusion.2.refs_0_, bf16[64,2048]{1,0:T(8,128)(2,1)S(1)} %collective-permute-done.19.refs_1_, ...), custom_call_target="tpu_custom_call", output_to_operand_aliasing={{}: (10, {})} | custom-call | tf_op jit(solution)/shard_map/from_blocks/pallas_call | solution.py:144
  (68 shorter events, 8.9 us)
Async XLA Ops:
  2.4 7.1 %collective-permute-start = (bf16[256,4096]{1,0:T(8,128)(2,1)S(1)}, bf16[256,4096]{1,0:T(8,128)(2,1)S(1)}, u32[]{:S(2)}, u32[]{:S(2)}) collective-permute-start(bf16[256,4096]{1,0:T(8,128)(2,1)S(1)} %pick.1), channel_id=1, source_target_pairs={{0,2},{2,0},{1,3},{3,1},{4,6},{6,4},{5,7},{7,5},{8,10},{10,8},{9,1... | collective-permute-start | bytes 6291464 | tf_op jit(solution)/shard_map/ppermute | solution.py:173
  8.7 3.0 %copy-start = (f32[1,2,8192]{2,1,0:T(2,128)S(1)}, f32[1,2,8192]{2,1,0:T(2,128)}, u32[]{:S(2)}) copy-start(f32[1,2,8192]{2,1,0:T(2,128)} %param.6) | copy-start | bytes 196612
  8.7 3.0 %copy-start.1 = (f32[1,2,8192]{2,1,0:T(2,128)S(1)}, f32[1,2,8192]{2,1,0:T(2,128)}, u32[]{:S(2)}) copy-start(f32[1,2,8192]{2,1,0:T(2,128)} %param.7) | copy-start | bytes 196612
  11.9 7.1 %collective-permute-start.1 = (f32[2,4096]{1,0:T(2,128)S(1)}, f32[2,4096]{1,0:T(2,128)S(1)}, u32[]{:S(2)}, u32[]{:S(2)}) collective-permute-start(f32[2,4096]{1,0:T(2,128)S(1)} %dynamic-slice_bitcast_fusion), channel_id=1, source_target_pairs={{0,2},{2,0},{1,3},{3,1},{4,6},{6,4},{5,7},{7,5},{8,10},{10,8},{9,1... | collective-permute-start | bytes 98312 | tf_op jit(solution)/shard_map/ppermute | solution.py:173
  12.4 15.8 %collective-permute-start.2 = (f16[64,2048]{1,0:T(8,128)(2,1)}, f16[64,2048]{1,0:T(8,128)(2,1)}, u32[]{:S(2)}, u32[]{:S(2)}) collective-permute-start(f16[64,2048]{1,0:T(8,128)(2,1)} %convert_element_type.93), channel_id=1, source_target_pairs={{0,8},{4,12},{8,0},{12,4},{1,9},{5,13},{9,1},{13,5},{2,10},{6,14},... | collective-permute-start | bytes 786440 | tf_op jit(solution)/shard_map/ppermute | solution.py:173
  13.6 14.6 %collective-permute-start.3 = (f16[64,2048]{1,0:T(8,128)(2,1)}, f16[64,2048]{1,0:T(8,128)(2,1)}, u32[]{:S(2)}, u32[]{:S(2)}) collective-permute-start(f16[64,2048]{1,0:T(8,128)(2,1)} %convert_element_type.92), channel_id=1, source_target_pairs={{0,4},{4,8},{8,12},{12,0},{1,5},{5,9},{9,13},{13,1},{2,6},{6,10},{... | collective-permute-start | bytes 786440 | tf_op jit(solution)/shard_map/ppermute | solution.py:173
  14.0 14.2 %collective-permute-start.4 = (f16[64,2048]{1,0:T(8,128)(2,1)S(1)}, f16[64,2048]{1,0:T(8,128)(2,1)}, u32[]{:S(2)}, u32[]{:S(2)}) collective-permute-start(f16[64,2048]{1,0:T(8,128)(2,1)S(1)} %convert_element_type.94), channel_id=1, source_target_pairs={{0,12},{4,0},{8,4},{12,8},{1,13},{5,1},{9,5},{13,9},{2,14},{6,2},{... | collective-permute-start | bytes 786440 | tf_op jit(solution)/shard_map/ppermute | solution.py:173
  16.3 14.2 %collective-permute-start.6 = (f16[128,2048]{1,0:T(8,128)(2,1)S(1)}, f16[128,2048]{1,0:T(8,128)(2,1)S(1)}, u32[]{:S(2)}, u32[]{:S(2)}) collective-permute-start(f16[128,2048]{1,0:T(8,128)(2,1)S(1)} %convert_element_type.91), channel_id=1, source_target_pairs={{0,128},{128,0},{1,129},{129,1},{2,130},{130,2},{3,131},{131,3},{4... | collective-permute-start | bytes 1572872 | tf_op jit(solution)/shard_map/ppermute | solution.py:173
  20.0 24.6 %all-to-all-start = ((f32[8,4,4096]{2,1,0:T(4,128)}), f32[8,4,4096]{2,1,0:T(4,128)S(1)}, u32[]{:S(2)}, u32[]{:S(2)}) async-start(f32[8,4,4096]{2,1,0:T(4,128)} %broadcast_in_dim.33), calls=%async_computation | async-start | bytes 1048576 | tf_op jit(solution)/shard_map/all_to_all | solution.py:206
  29.5 5.6 %collective-permute-start.5 = (f16[32,2048]{1,0:T(8,128)(2,1)S(1)}, f16[32,2048]{1,0:T(8,128)(2,1)S(1)}, u32[]{:S(2)}, u32[]{:S(2)}) collective-permute-start(f16[32,2048]{1,0:T(8,128)(2,1)S(1)} %slice_convert_fusion), channel_id=1, source_target_pairs={{0,128},{128,0},{1,129},{129,1},{2,130},{130,2},{3,131},{131,3},{4... | collective-permute-start | bytes 393224 | tf_op jit(solution)/shard_map/ppermute | solution.py:173
  30.7 5.7 %collective-permute-start.7 = (f16[32,2048]{1,0:T(8,128)(2,1)S(1)}, f16[32,2048]{1,0:T(8,128)(2,1)S(1)}, u32[]{:S(2)}, u32[]{:S(2)}) collective-permute-start(f16[32,2048]{1,0:T(8,128)(2,1)S(1)} %get-tuple-element.59), channel_id=1, source_target_pairs={{0,8},{4,12},{8,0},{12,4},{1,9},{5,13},{9,1},{13,5},{2,10},{6,14},... | collective-permute-start | bytes 393224 | tf_op jit(solution)/shard_map/ppermute | solution.py:173
  32.4 6.2 %collective-permute-start.8 = (f16[32,2048]{1,0:T(8,128)(2,1)S(1)}, f16[32,2048]{1,0:T(8,128)(2,1)S(1)}, u32[]{:S(2)}, u32[]{:S(2)}) collective-permute-start(f16[32,2048]{1,0:T(8,128)(2,1)S(1)} %get-tuple-element.61), channel_id=1, source_target_pairs={{0,4},{4,8},{8,12},{12,0},{1,5},{5,9},{9,13},{13,1},{2,6},{6,10},{... | collective-permute-start | bytes 393224 | tf_op jit(solution)/shard_map/ppermute | solution.py:173
  34.1 5.6 %collective-permute-start.9 = (f16[32,2048]{1,0:T(8,128)(2,1)S(1)}, f16[32,2048]{1,0:T(8,128)(2,1)S(1)}, u32[]{:S(2)}, u32[]{:S(2)}) collective-permute-start(f16[32,2048]{1,0:T(8,128)(2,1)S(1)} %get-tuple-element.60), channel_id=1, source_target_pairs={{0,12},{4,0},{8,4},{12,8},{1,13},{5,1},{9,5},{13,9},{2,14},{6,2},{... | collective-permute-start | bytes 393224 | tf_op jit(solution)/shard_map/ppermute | solution.py:173
  44.6 13.5 %all-to-all-start.1 = ((f16[8,4,4096]{2,1,0:T(4,128)(2,1)}), f16[8,4,4096]{2,1,0:T(4,128)(2,1)S(1)}, u32[]{:S(2)}, u32[]{:S(2)}) async-start(f16[8,4,4096]{2,1,0:T(4,128)(2,1)} %pad_maximum_fusion.1), calls=%async_computation.1 | async-start | bytes 524288 | tf_op jit(solution)/shard_map/all_to_all | solution.py:219
  60.3 24.9 %all-to-all-start.2 = ((f32[256,1,128]{2,1,0:T(1,128)}), f32[256,1,128]{2,1,0:T(1,128)S(1)}, u32[]{:S(2)}, u32[]{:S(2)}) async-start(f32[256,1,128]{2,1,0:T(1,128)} %broadcast_in_dim.34), calls=%async_computation.2 | async-start | bytes 262144 | tf_op jit(solution)/shard_map/all_to_all | solution.py:226
  69.2 12.4 %collective-permute-start.11 = (f32[4,4096]{1,0:T(4,128)S(1)}, f32[4,4096]{1,0:T(4,128)S(1)}, u32[]{:S(2)}, u32[]{:S(2)}) collective-permute-start(f32[4,4096]{1,0:T(4,128)S(1)} %broadcast_multiply_fusion), channel_id=1, source_target_pairs={{0,16},{16,32},{32,48},{48,64},{64,80},{80,96},{96,112},{112,0},{1... | collective-permute-start | bytes 196616 | tf_op jit(solution)/shard_map/ppermute | solution.py:173
  70.9 13.4 %collective-permute-start.12 = (f32[4,4096]{1,0:T(4,128)S(1)}, f32[4,4096]{1,0:T(4,128)S(1)}, u32[]{:S(2)}, u32[]{:S(2)}) collective-permute-start(f32[4,4096]{1,0:T(4,128)S(1)} %broadcast_multiply_fusion), channel_id=1, source_target_pairs={{0,32},{16,48},{32,64},{48,80},{64,96},{80,112},{96,0},{112,16},{1... | collective-permute-start | bytes 196616 | tf_op jit(solution)/shard_map/ppermute | solution.py:173
  73.6 13.3 %collective-permute-start.13 = (f32[4,4096]{1,0:T(4,128)S(1)}, f32[4,4096]{1,0:T(4,128)S(1)}, u32[]{:S(2)}, u32[]{:S(2)}) collective-permute-start(f32[4,4096]{1,0:T(4,128)S(1)} %broadcast_multiply_fusion), channel_id=1, source_target_pairs={{0,48},{16,64},{32,80},{48,96},{64,112},{80,0},{96,16},{112,32},{1... | collective-permute-start | bytes 196616 | tf_op jit(solution)/shard_map/ppermute | solution.py:173
  76.8 10.0 %collective-permute-start.14 = (f32[4,4096]{1,0:T(4,128)S(1)}, f32[4,4096]{1,0:T(4,128)S(1)}, u32[]{:S(2)}, u32[]{:S(2)}) collective-permute-start(f32[4,4096]{1,0:T(4,128)S(1)} %broadcast_multiply_fusion), channel_id=1, source_target_pairs={{0,64},{16,80},{32,96},{48,112},{64,0},{80,16},{96,32},{112,48},{1... | collective-permute-start | bytes 196616 | tf_op jit(solution)/shard_map/ppermute | solution.py:173
  77.8 9.9 %collective-permute-start.15 = (f32[4,4096]{1,0:T(4,128)S(1)}, f32[4,4096]{1,0:T(4,128)S(1)}, u32[]{:S(2)}, u32[]{:S(2)}) collective-permute-start(f32[4,4096]{1,0:T(4,128)S(1)} %broadcast_multiply_fusion), channel_id=1, source_target_pairs={{0,80},{16,96},{32,112},{48,0},{64,16},{80,32},{96,48},{112,64},{1... | collective-permute-start | bytes 196616 | tf_op jit(solution)/shard_map/ppermute | solution.py:173
  81.6 10.0 %collective-permute-start.16 = (f32[4,4096]{1,0:T(4,128)S(1)}, f32[4,4096]{1,0:T(4,128)S(1)}, u32[]{:S(2)}, u32[]{:S(2)}) collective-permute-start(f32[4,4096]{1,0:T(4,128)S(1)} %broadcast_multiply_fusion), channel_id=1, source_target_pairs={{0,96},{16,112},{32,0},{48,16},{64,32},{80,48},{96,64},{112,80},{1... | collective-permute-start | bytes 196616 | tf_op jit(solution)/shard_map/ppermute | solution.py:173
  84.3 7.3 %collective-permute-start.17 = (f32[4,4096]{1,0:T(4,128)S(1)}, f32[4,4096]{1,0:T(4,128)S(1)}, u32[]{:S(2)}, u32[]{:S(2)}) collective-permute-start(f32[4,4096]{1,0:T(4,128)S(1)} %broadcast_multiply_fusion), channel_id=1, source_target_pairs={{0,112},{16,0},{32,16},{48,32},{64,48},{80,64},{96,80},{112,96},{1... | collective-permute-start | bytes 196616 | tf_op jit(solution)/shard_map/ppermute | solution.py:173
  92.0 7.8 %collective-permute-start.22 = (bf16[32,2048]{1,0:T(8,128)(2,1)S(1)}, bf16[32,2048]{1,0:T(8,128)(2,1)S(1)}, u32[]{:S(2)}, u32[]{:S(2)}) collective-permute-start(bf16[32,2048]{1,0:T(8,128)(2,1)S(1)} %get-tuple-element.62), channel_id=1, source_target_pairs={{0,4},{4,8},{8,12},{12,0},{1,5},{5,9},{9,13},{13,1},{2,6},{6,10},{... | collective-permute-start | bytes 393224 | tf_op jit(solution)/shard_map/ppermute | solution.py:173
  93.4 7.1 %collective-permute-start.23 = (bf16[32,2048]{1,0:T(8,128)(2,1)S(1)}, bf16[32,2048]{1,0:T(8,128)(2,1)S(1)}, u32[]{:S(2)}, u32[]{:S(2)}) collective-permute-start(bf16[32,2048]{1,0:T(8,128)(2,1)S(1)} %get-tuple-element.62), channel_id=1, source_target_pairs={{0,8},{4,12},{8,0},{12,4},{1,9},{5,13},{9,1},{13,5},{2,10},{6,14},... | collective-permute-start | bytes 393224 | tf_op jit(solution)/shard_map/ppermute | solution.py:173
  95.9 4.9 %collective-permute-start.24 = (bf16[32,2048]{1,0:T(8,128)(2,1)S(1)}, bf16[32,2048]{1,0:T(8,128)(2,1)S(1)}, u32[]{:S(2)}, u32[]{:S(2)}) collective-permute-start(bf16[32,2048]{1,0:T(8,128)(2,1)S(1)} %get-tuple-element.62), channel_id=1, source_target_pairs={{0,12},{4,0},{8,4},{12,8},{1,13},{5,1},{9,5},{13,9},{2,14},{6,2},{... | collective-permute-start | bytes 393224 | tf_op jit(solution)/shard_map/ppermute | solution.py:173
  97.0 9.5 %collective-permute-start.18 = (bf16[32,2048]{1,0:T(8,128)(2,1)S(1)}, bf16[32,2048]{1,0:T(8,128)(2,1)S(1)}, u32[]{:S(2)}, u32[]{:S(2)}) collective-permute-start(bf16[32,2048]{1,0:T(8,128)(2,1)S(1)} %get-tuple-element.63), channel_id=1, source_target_pairs={{0,128},{128,0},{1,129},{129,1},{2,130},{130,2},{3,131},{131,3},{4... | collective-permute-start | bytes 393224 | tf_op jit(solution)/shard_map/ppermute | solution.py:173
  100.9 13.5 %collective-permute-start.25 = (bf16[128,2048]{1,0:T(8,128)(2,1)S(1)}, bf16[128,2048]{1,0:T(8,128)(2,1)S(1)}, u32[]{:S(2)}, u32[]{:S(2)}) collective-permute-start(bf16[128,2048]{1,0:T(8,128)(2,1)S(1)} %pad_maximum_fusion.refs_0_), channel_id=1, source_target_pairs={{0,128},{128,0},{1,129},{129,1},{2,130},{130,2},{3,131},{131,3},{4... | collective-permute-start | bytes 1572872 | tf_op jit(solution)/shard_map/ppermute | solution.py:173
  103.7 6.5 %collective-permute-start.10 = (f32[2,4096]{1,0:T(2,128)S(1)}, f32[2,4096]{1,0:T(2,128)S(1)}, u32[]{:S(2)}, u32[]{:S(2)}) collective-permute-start(f32[2,4096]{1,0:T(2,128)S(1)} %constant_dynamic-slice_fusion), channel_id=1, source_target_pairs={{0,2},{2,0},{1,3},{3,1},{4,6},{6,4},{5,7},{7,5},{8,10},{10,8},{9,1... | collective-permute-start | bytes 98312 | tf_op jit(solution)/shard_map/ppermute | solution.py:173
  106.4 10.8 %collective-permute-start.26 = (bf16[128,2048]{1,0:T(8,128)(2,1)S(1)}, bf16[128,2048]{1,0:T(8,128)(2,1)S(1)}, u32[]{:S(2)}, u32[]{:S(2)}) collective-permute-start(bf16[128,2048]{1,0:T(8,128)(2,1)S(1)} %pad_maximum_fusion.refs_0_), channel_id=1, source_target_pairs={{0,2},{2,0},{1,3},{3,1},{4,6},{6,4},{5,7},{7,5},{8,10},{10,8},{9,1... | collective-permute-start | bytes 1572872 | tf_op jit(solution)/shard_map/ppermute | solution.py:173
  106.6 14.8 %collective-permute-start.19 = (bf16[64,2048]{1,0:T(8,128)(2,1)S(1)}, bf16[64,2048]{1,0:T(8,128)(2,1)S(1)}, u32[]{:S(2)}, u32[]{:S(2)}) collective-permute-start(bf16[64,2048]{1,0:T(8,128)(2,1)S(1)} %pad_maximum_fusion.2.refs_0_), channel_id=1, source_target_pairs={{0,4},{4,8},{8,12},{12,0},{1,5},{5,9},{9,13},{13,1},{2,6},{6,10},{... | collective-permute-start | bytes 786440 | tf_op jit(solution)/shard_map/ppermute | solution.py:173
  107.5 14.3 %collective-permute-start.20 = (bf16[64,2048]{1,0:T(8,128)(2,1)S(1)}, bf16[64,2048]{1,0:T(8,128)(2,1)S(1)}, u32[]{:S(2)}, u32[]{:S(2)}) collective-permute-start(bf16[64,2048]{1,0:T(8,128)(2,1)S(1)} %pad_maximum_fusion.2.refs_0_), channel_id=1, source_target_pairs={{0,8},{4,12},{8,0},{12,4},{1,9},{5,13},{9,1},{13,5},{2,10},{6,14},... | collective-permute-start | bytes 786440 | tf_op jit(solution)/shard_map/ppermute | solution.py:173
  110.2 11.6 %collective-permute-start.21 = (bf16[64,2048]{1,0:T(8,128)(2,1)S(1)}, bf16[64,2048]{1,0:T(8,128)(2,1)S(1)}, u32[]{:S(2)}, u32[]{:S(2)}) collective-permute-start(bf16[64,2048]{1,0:T(8,128)(2,1)S(1)} %pad_maximum_fusion.2.refs_0_), channel_id=1, source_target_pairs={{0,12},{4,0},{8,4},{12,8},{1,13},{5,1},{9,5},{13,9},{2,14},{6,2},{... | collective-permute-start | bytes 786440 | tf_op jit(solution)/shard_map/ppermute | solution.py:173
  114.4 4.4 %collective-permute-start.27 = (bf16[128,2048]{1,0:T(8,128)(2,1)S(1)}, bf16[128,2048]{1,0:T(8,128)(2,1)S(1)}, u32[]{:S(2)}, u32[]{:S(2)}) collective-permute-start(bf16[128,2048]{1,0:T(8,128)(2,1)S(1)} %collective-permute-done.25.refs_1_), channel_id=1, source_target_pairs={{0,2},{2,0},{1,3},{3,1},{4,6},{6,4},{5,7},{7,5},{8,10},{10,8},{9,1... | collective-permute-start | bytes 1572872 | tf_op jit(solution)/shard_map/ppermute | solution.py:173
  117.2 7.1 %collective-permute-start.28 = (bf16[64,2048]{1,0:T(8,128)(2,1)S(1)}, bf16[64,2048]{1,0:T(8,128)(2,1)S(1)}, u32[]{:S(2)}, u32[]{:S(2)}) collective-permute-start(bf16[64,2048]{1,0:T(8,128)(2,1)S(1)} %pad_maximum_fusion.2.refs_0_), channel_id=1, source_target_pairs={{0,2},{2,0},{1,3},{3,1},{4,6},{6,4},{5,7},{7,5},{8,10},{10,8},{9,1... | collective-permute-start | bytes 786440 | tf_op jit(solution)/shard_map/ppermute | solution.py:173
  121.8 2.5 %collective-permute-start.29 = (bf16[64,2048]{1,0:T(8,128)(2,1)S(1)}, bf16[64,2048]{1,0:T(8,128)(2,1)S(1)}, u32[]{:S(2)}, u32[]{:S(2)}) collective-permute-start(bf16[64,2048]{1,0:T(8,128)(2,1)S(1)} %collective-permute-done.19.refs_1_), channel_id=1, source_target_pairs={{0,2},{2,0},{1,3},{3,1},{4,6},{6,4},{5,7},{7,5},{8,10},{10,8},{9,1... | collective-permute-start | bytes 786440 | tf_op jit(solution)/shard_map/ppermute | solution.py:173
  123.1 1.5 %collective-permute-start.30 = (bf16[64,2048]{1,0:T(8,128)(2,1)S(1)}, bf16[64,2048]{1,0:T(8,128)(2,1)S(1)}, u32[]{:S(2)}, u32[]{:S(2)}) collective-permute-start(bf16[64,2048]{1,0:T(8,128)(2,1)S(1)} %collective-permute-done.20.refs_2_), channel_id=1, source_target_pairs={{0,2},{2,0},{1,3},{3,1},{4,6},{6,4},{5,7},{7,5},{8,10},{10,8},{9,1... | collective-permute-start | bytes 786440 | tf_op jit(solution)/shard_map/ppermute | solution.py:173
  123.1 1.9 %collective-permute-start.31 = (bf16[64,2048]{1,0:T(8,128)(2,1)S(1)}, bf16[64,2048]{1,0:T(8,128)(2,1)S(1)}, u32[]{:S(2)}, u32[]{:S(2)}) collective-permute-start(bf16[64,2048]{1,0:T(8,128)(2,1)S(1)} %collective-permute-done.21.refs_3_), channel_id=1, source_target_pairs={{0,2},{2,0},{1,3},{3,1},{4,6},{6,4},{5,7},{7,5},{8,10},{10,8},{9,1... | collective-permute-start | bytes 786440 | tf_op jit(solution)/shard_map/ppermute | solution.py:173

commit v6 on v5

--- a/solution.py
+++ b/solution.py
@@ -17,6 +17,7 @@
 
 SCALE = 16.0
 WIDTH = 1024
+STEP = 512
 MIB = 1024 * 1024
 VMEM = pl.BlockSpec(memory_space=pltpu.VMEM)
 SMEM = pl.BlockSpec(memory_space=pltpu.SMEM)
@@ -127,18 +128,18 @@
     ins = refs[: 2 * n]
     side, k = pl.program_id(0), pl.program_id(1)
     for s in range(2):
-        for part in range(ins[0].shape[1] // WIDTH):
+        for part in range(ins[0].shape[1] // STEP):
 
             @pl.when((side == s) & (k == part))
             def _():
-                blocks = [b[:, part * WIDTH : (part + 1) * WIDTH] for b in ins[s * n : (s + 1) * n]]
+                blocks = [b[:, part * STEP : (part + 1) * STEP] for b in ins[s * n : (s + 1) * n]]
                 x = jnp.concatenate(blocks, axis=0)
                 out[...] = jnp.dot(one[...], x, preferred_element_type=jnp.float32).astype(out.dtype)
 
 
-def from_blocks(core, one, mine, theirs, quarter, out=None):
-    rows, width = one.shape[0], 4 * mine[0].shape[1]
-    steps = mine[0].shape[1] // WIDTH
+def from_blocks(core, one, mine, theirs, begin, half, out=None):
+    rows, width = one.shape[0], 2 * half
+    steps = mine[0].shape[1] // STEP
     blocks = [*mine, *theirs]
     rest = [] if out is None else [out]
     return pl.pallas_call(
@@ -148,7 +149,7 @@
             grid=(2, steps),
             in_specs=[VMEM] * (1 + len(blocks)) + [HBM] * len(rest),
             out_specs=pl.BlockSpec(
-                (rows, WIDTH), lambda s, k, core: (0, ((core[0] + s) % 2 * 2 + quarter) * steps + k)
+                (rows, STEP), lambda s, k, core: (0, ((core[0] + s) % 2 * half + begin) // STEP + k)
             ),
         ),
         out_shape=jax.ShapeDtypeStruct((rows, width), mine[0].dtype),
@@ -235,18 +236,19 @@
         there = lax.dynamic_index_in_dim(base, there, 0, keepdims=False, allow_negative_indices=False)
         mine.append((there - outer_rate * (1.0 + nesterov_mu) * (clip * grads[k])).astype(jnp.bfloat16))
     mine = jnp.concatenate(mine, axis=0)
+    edge = half * 3 // 8
     first, second = mine[:, :edge], mine[:, edge:]
     arrived = {j: send(second, "y", j) for j in far_y}
     second = jnp.concatenate([second] + [arrived[j] for j in range(1, ny)], axis=0)
     first = jnp.concatenate([first, send(first, "xh", 1)], axis=0)
     mine = [second, send(second, "xh", 1)]
     theirs = [send(x, "c", 1) for x in mine]
-    new_params = from_blocks(core1, back_x.astype(jnp.bfloat16), mine, theirs, 1)
+    new_params = from_blocks(core1, back_x.astype(jnp.bfloat16), mine, theirs, edge, half)
     arrived = {j: send(first, "y", j) for j in far_y}
     arrived, new_params = lax.optimization_barrier((arrived, new_params))
     mine = [first] + [arrived[j] for j in range(1, ny)]
     theirs = [send(x, "c", 1) for x in mine]
-    new_params = from_blocks(core1, back_y.astype(jnp.bfloat16), mine, theirs, 0, new_params)
+    new_params = from_blocks(core1, back_y.astype(jnp.bfloat16), mine, theirs, 0, half, new_params)
 
     other = send(part(grad, at[3], 0), "c", 1)
     own = part(grad, at[2], 0)

time: 128 us -> 134 us (1.047)
  Pallas kernels: 10.5 us -> 13.7 us
    pallas_call x2, Pallas kernels: 5.16 us -> 8.29 us  [from_blocks(): pl.pallas_call(from_blocks_kernel, grid_spec=pltpu.PrefetchScalarGridSpec...]
  transfers between devices with their start and end apart: 35 -> 35, of which waited for: 15 -> 13; matrix products, arithmetic and copies ran while one was open for 4% -> 4% of each run, Pallas kernels for 4% -> 6%
where the time goes in v6:
time: 134 us; the launch traced here: 133 us
  starting transfers between devices  76.6 us (57%)
  waiting for transfers between devices  31.2 us (23%)
  Pallas kernels  13.7 us (10%)
  other arithmetic  7 us (5%)
  local copies, waits for them, and re-layouts  2.76 us (2%)
  between operations  1.64 us (1%)
    ppermute x32, starting transfers between devices, send(): return lax.ppermute(x, axis, shift(axis, by))  55.4 us
    ppermute x32, waiting for transfers between devices, send(): return lax.ppermute(x, axis, shift(axis, by))  18 us
    all_to_all x1, waiting for transfers between devices, step(): total = wide(lax.all_to_all(total, 'z', 0, 0, tiled=True)).sum(axis=0)  9.25 us
    all_to_all x1, starting transfers between devices, step(): lax.all_to_all(jnp.full((members, 1, 128), jnp.sum(grad * grad)), ALL, 0,...  8.82 us
    pallas_call x2, Pallas kernels, from_blocks(): pl.pallas_call(from_blocks_kernel, grid_spec=pltpu.PrefetchScalarGridSpec...  8.29 us
    all_to_all x1, starting transfers between devices, step(): lax.all_to_all(jnp.broadcast_to(base[None], (nz, 4, half)), 'z', 0, 0, ti...  8.19 us
    all_to_all x1, starting transfers between devices, step(): total = wide(lax.all_to_all(total, 'z', 0, 0, tiled=True)).sum(axis=0)  4.26 us
    all_to_all x1, waiting for transfers between devices, step(): lax.all_to_all(jnp.broadcast_to(base[None], (nz, 4, half)), 'z', 0, 0, ti...  3.93 us
  transfers between devices with their start and end apart: 35, of which 13 were waited for; matrix products, arithmetic and copies ran while one was open for 4% of the time, Pallas kernels for 6%

profile of v6, /device:TPU:1, one launch (start us, length us, event | category | flops | bytes accessed | tf_op | source)
XLA Modules:
  0.0 132.9 jit_solution(8134693394887340096)
XLA Ops:
  0.8 1.6 %pick.1 = bf16[256,4096]{1,0:T(8,128)(2,1)S(1)} custom-call(s32[1]{0:T(128)} %bitcast.2.core, bf16[256,8192]{1,0:T(8,128)(2,1)} %bitcast.46), custom_call_target="tpu_custom_call" | custom-call | tf_op jit(solution)/shard_map/pick/pallas_call | solution.py:49
  2.4 3.3 %collective-permute-start = (bf16[256,4096]{1,0:T(8,128)(2,1)S(1)}, bf16[256,4096]{1,0:T(8,128)(2,1)S(1)}, u32[]{:S(2)}, u32[]{:S(2)}) collective-permute-start(bf16[256,4096]{1,0:T(8,128)(2,1)S(1)} %pick.1), channel_id=1, source_target_pairs={{0,2},{2,0},{1,3},{3,1},{4,6},{6,4},{5,7},{7,5},{8,10},{10,8},{9,1... | collective-permute-start | bytes 6291464 | tf_op jit(solution)/shard_map/ppermute | solution.py:174
  5.7 3.0 %change.1.own = f32[256,4096]{1,0:T(8,128)S(1)} custom-call(s32[1]{0:T(128)} %bitcast.2.core, bf16[256,256]{1,0:T(8,128)(2,1)S(1)} %select_convert_fusion.one, bf16[256,8192]{1,0:T(8,128)(2,1)} %bitcast.47, bf16[256,8192]{1,0:T(8,128)(2,1)} %bitcast.48), custom_call_target="tpu_custom_call" | custom-call | tf_op jit(solution)/shard_map/change/pallas_call | solution.py:81
  12.4 1.2 collective-permute-start.2
  14.0 2.3 %collective-permute-start.4 = (f16[64,2048]{1,0:T(8,128)(2,1)S(1)}, f16[64,2048]{1,0:T(8,128)(2,1)}, u32[]{:S(2)}, u32[]{:S(2)}) collective-permute-start(f16[64,2048]{1,0:T(8,128)(2,1)S(1)} %convert_element_type.94), channel_id=1, source_target_pairs={{0,12},{4,0},{8,4},{12,8},{1,13},{5,1},{9,5},{13,9},{2,14},{6,2},{... | collective-permute-start | bytes 786440 | tf_op jit(solution)/shard_map/ppermute | solution.py:174
  16.3 2.7 %collective-permute-start.6 = (f16[128,2048]{1,0:T(8,128)(2,1)S(1)}, f16[128,2048]{1,0:T(8,128)(2,1)S(1)}, u32[]{:S(2)}, u32[]{:S(2)}) collective-permute-start(f16[128,2048]{1,0:T(8,128)(2,1)S(1)} %convert_element_type.91), channel_id=1, source_target_pairs={{0,128},{128,0},{1,129},{129,1},{2,130},{130,2},{3,131},{131,3},{4... | collective-permute-start | bytes 1572872 | tf_op jit(solution)/shard_map/ppermute | solution.py:174
  19.2 0.9 broadcast_in_dim.33
  20.1 8.2 %all-to-all-start = ((f32[8,4,4096]{2,1,0:T(4,128)}), f32[8,4,4096]{2,1,0:T(4,128)S(1)}, u32[]{:S(2)}, u32[]{:S(2)}) async-start(f32[8,4,4096]{2,1,0:T(4,128)} %broadcast_in_dim.33), calls=%async_computation | async-start | bytes 1048576 | tf_op jit(solution)/shard_map/all_to_all | solution.py:207
  28.3 1.2 convert_add_fusion.1
  29.5 0.9 collective-permute-start.5
  30.7 1.7 %collective-permute-start.7 = (f16[32,2048]{1,0:T(8,128)(2,1)S(1)}, f16[32,2048]{1,0:T(8,128)(2,1)S(1)}, u32[]{:S(2)}, u32[]{:S(2)}) collective-permute-start(f16[32,2048]{1,0:T(8,128)(2,1)S(1)} %get-tuple-element.59), channel_id=1, source_target_pairs={{0,8},{4,12},{8,0},{12,4},{1,9},{5,13},{9,1},{13,5},{2,10},{6,14},... | collective-permute-start | bytes 393224 | tf_op jit(solution)/shard_map/ppermute | solution.py:174
  32.4 1.7 %collective-permute-start.8 = (f16[32,2048]{1,0:T(8,128)(2,1)S(1)}, f16[32,2048]{1,0:T(8,128)(2,1)S(1)}, u32[]{:S(2)}, u32[]{:S(2)}) collective-permute-start(f16[32,2048]{1,0:T(8,128)(2,1)S(1)} %get-tuple-element.61), channel_id=1, source_target_pairs={{0,4},{4,8},{8,12},{12,0},{1,5},{5,9},{9,13},{13,1},{2,6},{6,10},{... | collective-permute-start | bytes 393224 | tf_op jit(solution)/shard_map/ppermute | solution.py:174
  34.1 1.0 collective-permute-start.9
  35.2 1.2 collective-permute-done.7
  36.4 2.2 %collective-permute-done.8 = f16[32,2048]{1,0:T(8,128)(2,1)S(1)} collective-permute-done((f16[32,2048]{1,0:T(8,128)(2,1)S(1)}, f16[32,2048]{1,0:T(8,128)(2,1)S(1)}, u32[]{:S(2)}, u32[]{:S(2)}) %collective-permute-start.8) | collective-permute-done | bytes 131104 | tf_op jit(solution)/shard_map/ppermute | solution.py:174
  38.7 1.1 collective-permute-done.9
  39.9 0.9 pad_maximum_fusion.1
  40.8 3.9 %all-to-all-done = f32[8,4,4096]{2,1,0:T(4,128)S(1)} async-done(((f32[8,4,4096]{2,1,0:T(4,128)}), f32[8,4,4096]{2,1,0:T(4,128)S(1)}, u32[]{:S(2)}, u32[]{:S(2)}) %all-to-all-start) | async-done | bytes 524320 | tf_op jit(solution)/shard_map/all_to_all | solution.py:207
  44.7 4.3 %all-to-all-start.1 = ((f16[8,4,4096]{2,1,0:T(4,128)(2,1)}), f16[8,4,4096]{2,1,0:T(4,128)(2,1)S(1)}, u32[]{:S(2)}, u32[]{:S(2)}) async-start(f16[8,4,4096]{2,1,0:T(4,128)(2,1)} %pad_maximum_fusion.1), calls=%async_computation.1 | async-start | bytes 524288 | tf_op jit(solution)/shard_map/all_to_all | solution.py:220
  49.0 9.2 %all-to-all-done.1 = f16[8,4,4096]{2,1,0:T(4,128)(2,1)S(1)} async-done(((f16[8,4,4096]{2,1,0:T(4,128)(2,1)}), f16[8,4,4096]{2,1,0:T(4,128)(2,1)S(1)}, u32[]{:S(2)}, u32[]{:S(2)}) %all-to-all-start.1) | async-done | bytes 262176 | tf_op jit(solution)/shard_map/all_to_all | solution.py:220
  59.0 1.4 %broadcast_in_dim.34 = f32[256,1,128]{2,1,0:T(1,128)} broadcast(f32[]{:T(128)} %multiply_reduce_fusion), dimensions={} | broadcast | bytes 131076 | tf_op jit(solution)/shard_map/broadcast_in_dim | solution.py:227
  60.3 8.8 %all-to-all-start.2 = ((f32[256,1,128]{2,1,0:T(1,128)}), f32[256,1,128]{2,1,0:T(1,128)S(1)}, u32[]{:S(2)}, u32[]{:S(2)}) async-start(f32[256,1,128]{2,1,0:T(1,128)} %broadcast_in_dim.34), calls=%async_computation.2 | async-start | bytes 262144 | tf_op jit(solution)/shard_map/all_to_all | solution.py:227
  69.2 1.7 %collective-permute-start.11 = (f32[4,4096]{1,0:T(4,128)S(1)}, f32[4,4096]{1,0:T(4,128)S(1)}, u32[]{:S(2)}, u32[]{:S(2)}) collective-permute-start(f32[4,4096]{1,0:T(4,128)S(1)} %broadcast_multiply_fusion), channel_id=1, source_target_pairs={{0,16},{16,32},{32,48},{48,64},{64,80},{80,96},{96,112},{112,0},{1... | collective-permute-start | bytes 196616 | tf_op jit(solution)/shard_map/ppermute | solution.py:174
  71.0 2.6 %collective-permute-start.12 = (f32[4,4096]{1,0:T(4,128)S(1)}, f32[4,4096]{1,0:T(4,128)S(1)}, u32[]{:S(2)}, u32[]{:S(2)}) collective-permute-start(f32[4,4096]{1,0:T(4,128)S(1)} %broadcast_multiply_fusion), channel_id=1, source_target_pairs={{0,32},{16,48},{32,64},{48,80},{64,96},{80,112},{96,0},{112,16},{1... | collective-permute-start | bytes 196616 | tf_op jit(solution)/shard_map/ppermute | solution.py:174
  73.6 3.3 %collective-permute-start.13 = (f32[4,4096]{1,0:T(4,128)S(1)}, f32[4,4096]{1,0:T(4,128)S(1)}, u32[]{:S(2)}, u32[]{:S(2)}) collective-permute-start(f32[4,4096]{1,0:T(4,128)S(1)} %broadcast_multiply_fusion), channel_id=1, source_target_pairs={{0,48},{16,64},{32,80},{48,96},{64,112},{80,0},{96,16},{112,32},{1... | collective-permute-start | bytes 196616 | tf_op jit(solution)/shard_map/ppermute | solution.py:174
  76.9 1.0 collective-permute-start.14
  77.9 3.7 %collective-permute-start.15 = (f32[4,4096]{1,0:T(4,128)S(1)}, f32[4,4096]{1,0:T(4,128)S(1)}, u32[]{:S(2)}, u32[]{:S(2)}) collective-permute-start(f32[4,4096]{1,0:T(4,128)S(1)} %broadcast_multiply_fusion), channel_id=1, source_target_pairs={{0,80},{16,96},{32,112},{48,0},{64,16},{80,32},{96,48},{112,64},{1... | collective-permute-start | bytes 196616 | tf_op jit(solution)/shard_map/ppermute | solution.py:174
  81.6 2.8 %collective-permute-start.16 = (f32[4,4096]{1,0:T(4,128)S(1)}, f32[4,4096]{1,0:T(4,128)S(1)}, u32[]{:S(2)}, u32[]{:S(2)}) collective-permute-start(f32[4,4096]{1,0:T(4,128)S(1)} %broadcast_multiply_fusion), channel_id=1, source_target_pairs={{0,96},{16,112},{32,0},{48,16},{64,32},{80,48},{96,64},{112,80},{1... | collective-permute-start | bytes 196616 | tf_op jit(solution)/shard_map/ppermute | solution.py:174
  84.4 0.9 collective-permute-start.17
  85.3 0.9 slice_reduce_fusion
  86.9 0.9 collective-permute-done.15
  87.8 3.9 %collective-permute-done.16 = f32[4,4096]{1,0:T(4,128)S(1)} collective-permute-done((f32[4,4096]{1,0:T(4,128)S(1)}, f32[4,4096]{1,0:T(4,128)S(1)}, u32[]{:S(2)}, u32[]{:S(2)}) %collective-permute-start.16) | collective-permute-done | bytes 65568 | tf_op jit(solution)/shard_map/ppermute | solution.py:174
  92.0 1.3 %collective-permute-start.22 = (bf16[32,2560]{1,0:T(8,128)(2,1)S(1)}, bf16[32,2560]{1,0:T(8,128)(2,1)S(1)}, u32[]{:S(2)}, u32[]{:S(2)}) collective-permute-start(bf16[32,2560]{1,0:T(8,128)(2,1)S(1)} %slice.48), channel_id=1, source_target_pairs={{0,4},{4,8},{8,12},{12,0},{1,5},{5,9},{9,13},{13,1},{2,6},{6,10},{... | collective-permute-start | bytes 491528 | tf_op jit(solution)/shard_map/ppermute | solution.py:174
  93.4 2.5 %collective-permute-start.23 = (bf16[32,2560]{1,0:T(8,128)(2,1)S(1)}, bf16[32,2560]{1,0:T(8,128)(2,1)S(1)}, u32[]{:S(2)}, u32[]{:S(2)}) collective-permute-start(bf16[32,2560]{1,0:T(8,128)(2,1)S(1)} %slice.48), channel_id=1, source_target_pairs={{0,8},{4,12},{8,0},{12,4},{1,9},{5,13},{9,1},{13,5},{2,10},{6,14},... | collective-permute-start | bytes 491528 | tf_op jit(solution)/shard_map/ppermute | solution.py:174
  95.9 1.1 collective-permute-start.24
  97.1 2.8 %collective-permute-start.18 = (bf16[32,1536]{1,0:T(8,128)(2,1)S(1)}, bf16[32,1536]{1,0:T(8,128)(2,1)S(1)}, u32[]{:S(2)}, u32[]{:S(2)}) collective-permute-start(bf16[32,1536]{1,0:T(8,128)(2,1)S(1)} %slice.47), channel_id=1, source_target_pairs={{0,128},{128,0},{1,129},{129,1},{2,130},{130,2},{3,131},{131,3},{4... | collective-permute-start | bytes 294920 | tf_op jit(solution)/shard_map/ppermute | solution.py:174
  99.9 2.0 %collective-permute-done.23 = bf16[32,2560]{1,0:T(8,128)(2,1)S(1)} collective-permute-done((bf16[32,2560]{1,0:T(8,128)(2,1)S(1)}, bf16[32,2560]{1,0:T(8,128)(2,1)S(1)}, u32[]{:S(2)}, u32[]{:S(2)}) %collective-permute-start.23) | collective-permute-done | bytes 163872 | tf_op jit(solution)/shard_map/ppermute | solution.py:174
  101.9 2.8 %collective-permute-start.25 = (bf16[128,2560]{1,0:T(8,128)(2,1)S(1)}, bf16[128,2560]{1,0:T(8,128)(2,1)S(1)}, u32[]{:S(2)}, u32[]{:S(2)}) collective-permute-start(bf16[128,2560]{1,0:T(8,128)(2,1)S(1)} %pad_maximum_fusion.refs_0_), channel_id=1, source_target_pairs={{0,128},{128,0},{1,129},{129,1},{2,130},{130,2},{3,131},{131,3},{4... | collective-permute-start | bytes 1966088 | tf_op jit(solution)/shard_map/ppermute | solution.py:174
  104.8 3.1 %collective-permute-start.10 = (f32[2,4096]{1,0:T(2,128)S(1)}, f32[2,4096]{1,0:T(2,128)S(1)}, u32[]{:S(2)}, u32[]{:S(2)}) collective-permute-start(f32[2,4096]{1,0:T(2,128)S(1)} %constant_dynamic-slice_fusion), channel_id=1, source_target_pairs={{0,2},{2,0},{1,3},{3,1},{4,6},{6,4},{5,7},{7,5},{8,10},{10,8},{9,1... | collective-permute-start | bytes 98312 | tf_op jit(solution)/shard_map/ppermute | solution.py:174
  107.8 1.0 collective-permute-start.19
  108.9 2.3 %collective-permute-start.20 = (bf16[64,1536]{1,0:T(8,128)(2,1)S(1)}, bf16[64,1536]{1,0:T(8,128)(2,1)S(1)}, u32[]{:S(2)}, u32[]{:S(2)}) collective-permute-start(bf16[64,1536]{1,0:T(8,128)(2,1)S(1)} %pad_maximum_fusion.2.refs_0_), channel_id=1, source_target_pairs={{0,8},{4,12},{8,0},{12,4},{1,9},{5,13},{9,1},{13,5},{2,10},{6,14},... | collective-permute-start | bytes 589832 | tf_op jit(solution)/shard_map/ppermute | solution.py:174
  111.1 1.2 collective-permute-start.21
  112.3 0.9 collective-permute-start.26
  113.2 3.9 %collective-permute-done.25.refs_1_ = bf16[128,2560]{1,0:T(8,128)(2,1)S(1)} collective-permute-done((bf16[128,2560]{1,0:T(8,128)(2,1)S(1)}, bf16[128,2560]{1,0:T(8,128)(2,1)S(1)}, u32[]{:S(2)}, u32[]{:S(2)}) %collective-permute-start.25) | collective-permute-done | bytes 655392 | tf_op jit(solution)/shard_map/ppermute | solution.py:174
  117.1 3.5 %collective-permute-start.27 = (bf16[128,2560]{1,0:T(8,128)(2,1)S(1)}, bf16[128,2560]{1,0:T(8,128)(2,1)S(1)}, u32[]{:S(2)}, u32[]{:S(2)}) collective-permute-start(bf16[128,2560]{1,0:T(8,128)(2,1)S(1)} %collective-permute-done.25.refs_1_), channel_id=1, source_target_pairs={{0,2},{2,0},{1,3},{3,1},{4,6},{6,4},{5,7},{7,5},{8,10},{10,8},{9,1... | collective-permute-start | bytes 1966088 | tf_op jit(solution)/shard_map/ppermute | solution.py:174
  120.8 1.6 %collective-permute-done.27.refs_3_ = bf16[128,2560]{1,0:T(8,128)(2,1)S(1)} collective-permute-done((bf16[128,2560]{1,0:T(8,128)(2,1)S(1)}, bf16[128,2560]{1,0:T(8,128)(2,1)S(1)}, u32[]{:S(2)}, u32[]{:S(2)}) %collective-permute-start.27) | collective-permute-done | bytes 655392 | tf_op jit(solution)/shard_map/ppermute | solution.py:174
  122.4 5.1 %from_blocks.2.refs_8_ = bf16[256,8192]{1,0:T(8,128)(2,1)} custom-call(s32[1]{0:T(128)} %bitcast.2.core, bf16[256,256]{1,0:T(8,128)(2,1)S(1)} %fusion.5.one, bf16[128,2560]{1,0:T(8,128)(2,1)S(1)} %pad_maximum_fusion.refs_0_, bf16[128,2560]{1,0:T(8,128)(2,1)S(1)} %collective-permute-done.25.refs_1_, bf16[128,2560]{1,0:T(8,128)(2,1)S(1)} %collective-permute-done.26.refs_2_, ...), custom_call_target="tpu_custom_call" | custom-call | tf_op jit(solution)/shard_map/from_blocks/pallas_call | solution.py:145
  129.7 3.2 %from_blocks.3 = bf16[256,8192]{1,0:T(8,128)(2,1)} custom-call(s32[1]{0:T(128)} %bitcast.2.core, bf16[256,256]{1,0:T(8,128)(2,1)S(1)} %fusion.4.one, bf16[64,1536]{1,0:T(8,128)(2,1)S(1)} %pad_maximum_fusion.2.refs_0_, bf16[64,1536]{1,0:T(8,128)(2,1)S(1)} %collective-permute-done.19.refs_1_, ...), custom_call_target="tpu_custom_call", output_to_operand_aliasing={{}: (10, {})} | custom-call | tf_op jit(solution)/shard_map/from_blocks/pallas_call | solution.py:145
  (69 shorter events, 8.4 us)
Async XLA Ops:
  2.4 7.1 %collective-permute-start = (bf16[256,4096]{1,0:T(8,128)(2,1)S(1)}, bf16[256,4096]{1,0:T(8,128)(2,1)S(1)}, u32[]{:S(2)}, u32[]{:S(2)}) collective-permute-start(bf16[256,4096]{1,0:T(8,128)(2,1)S(1)} %pick.1), channel_id=1, source_target_pairs={{0,2},{2,0},{1,3},{3,1},{4,6},{6,4},{5,7},{7,5},{8,10},{10,8},{9,1... | collective-permute-start | bytes 6291464 | tf_op jit(solution)/shard_map/ppermute | solution.py:174
  10.2 1.6 %copy-start = (f32[1,2,8192]{2,1,0:T(2,128)S(1)}, f32[1,2,8192]{2,1,0:T(2,128)}, u32[]{:S(2)}) copy-start(f32[1,2,8192]{2,1,0:T(2,128)} %param.6) | copy-start | bytes 196612
  10.2 1.6 %copy-start.1 = (f32[1,2,8192]{2,1,0:T(2,128)S(1)}, f32[1,2,8192]{2,1,0:T(2,128)}, u32[]{:S(2)}) copy-start(f32[1,2,8192]{2,1,0:T(2,128)} %param.7) | copy-start | bytes 196612
  11.9 7.1 %collective-permute-start.1 = (f32[2,4096]{1,0:T(2,128)S(1)}, f32[2,4096]{1,0:T(2,128)S(1)}, u32[]{:S(2)}, u32[]{:S(2)}) collective-permute-start(f32[2,4096]{1,0:T(2,128)S(1)} %dynamic-slice_bitcast_fusion), channel_id=1, source_target_pairs={{0,2},{2,0},{1,3},{3,1},{4,6},{6,4},{5,7},{7,5},{8,10},{10,8},{9,1... | collective-permute-start | bytes 98312 | tf_op jit(solution)/shard_map/ppermute | solution.py:174
  12.4 15.8 %collective-permute-start.2 = (f16[64,2048]{1,0:T(8,128)(2,1)}, f16[64,2048]{1,0:T(8,128)(2,1)}, u32[]{:S(2)}, u32[]{:S(2)}) collective-permute-start(f16[64,2048]{1,0:T(8,128)(2,1)} %convert_element_type.93), channel_id=1, source_target_pairs={{0,8},{4,12},{8,0},{12,4},{1,9},{5,13},{9,1},{13,5},{2,10},{6,14},... | collective-permute-start | bytes 786440 | tf_op jit(solution)/shard_map/ppermute | solution.py:174
  13.6 14.6 %collective-permute-start.3 = (f16[64,2048]{1,0:T(8,128)(2,1)}, f16[64,2048]{1,0:T(8,128)(2,1)}, u32[]{:S(2)}, u32[]{:S(2)}) collective-permute-start(f16[64,2048]{1,0:T(8,128)(2,1)} %convert_element_type.92), channel_id=1, source_target_pairs={{0,4},{4,8},{8,12},{12,0},{1,5},{5,9},{9,13},{13,1},{2,6},{6,10},{... | collective-permute-start | bytes 786440 | tf_op jit(solution)/shard_map/ppermute | solution.py:174
  14.0 14.2 %collective-permute-start.4 = (f16[64,2048]{1,0:T(8,128)(2,1)S(1)}, f16[64,2048]{1,0:T(8,128)(2,1)}, u32[]{:S(2)}, u32[]{:S(2)}) collective-permute-start(f16[64,2048]{1,0:T(8,128)(2,1)S(1)} %convert_element_type.94), channel_id=1, source_target_pairs={{0,12},{4,0},{8,4},{12,8},{1,13},{5,1},{9,5},{13,9},{2,14},{6,2},{... | collective-permute-start | bytes 786440 | tf_op jit(solution)/shard_map/ppermute | solution.py:174
  16.3 14.2 %collective-permute-start.6 = (f16[128,2048]{1,0:T(8,128)(2,1)S(1)}, f16[128,2048]{1,0:T(8,128)(2,1)S(1)}, u32[]{:S(2)}, u32[]{:S(2)}) collective-permute-start(f16[128,2048]{1,0:T(8,128)(2,1)S(1)} %convert_element_type.91), channel_id=1, source_target_pairs={{0,128},{128,0},{1,129},{129,1},{2,130},{130,2},{3,131},{131,3},{4... | collective-permute-start | bytes 1572872 | tf_op jit(solution)/shard_map/ppermute | solution.py:174
  20.1 24.6 %all-to-all-start = ((f32[8,4,4096]{2,1,0:T(4,128)}), f32[8,4,4096]{2,1,0:T(4,128)S(1)}, u32[]{:S(2)}, u32[]{:S(2)}) async-start(f32[8,4,4096]{2,1,0:T(4,128)} %broadcast_in_dim.33), calls=%async_computation | async-start | bytes 1048576 | tf_op jit(solution)/shard_map/all_to_all | solution.py:207
  29.5 5.6 %collective-permute-start.5 = (f16[32,2048]{1,0:T(8,128)(2,1)S(1)}, f16[32,2048]{1,0:T(8,128)(2,1)S(1)}, u32[]{:S(2)}, u32[]{:S(2)}) collective-permute-start(f16[32,2048]{1,0:T(8,128)(2,1)S(1)} %slice_convert_fusion), channel_id=1, source_target_pairs={{0,128},{128,0},{1,129},{129,1},{2,130},{130,2},{3,131},{131,3},{4... | collective-permute-start | bytes 393224 | tf_op jit(solution)/shard_map/ppermute | solution.py:174
  30.7 5.7 %collective-permute-start.7 = (f16[32,2048]{1,0:T(8,128)(2,1)S(1)}, f16[32,2048]{1,0:T(8,128)(2,1)S(1)}, u32[]{:S(2)}, u32[]{:S(2)}) collective-permute-start(f16[32,2048]{1,0:T(8,128)(2,1)S(1)} %get-tuple-element.59), channel_id=1, source_target_pairs={{0,8},{4,12},{8,0},{12,4},{1,9},{5,13},{9,1},{13,5},{2,10},{6,14},... | collective-permute-start | bytes 393224 | tf_op jit(solution)/shard_map/ppermute | solution.py:174
  32.4 6.2 %collective-permute-start.8 = (f16[32,2048]{1,0:T(8,128)(2,1)S(1)}, f16[32,2048]{1,0:T(8,128)(2,1)S(1)}, u32[]{:S(2)}, u32[]{:S(2)}) collective-permute-start(f16[32,2048]{1,0:T(8,128)(2,1)S(1)} %get-tuple-element.61), channel_id=1, source_target_pairs={{0,4},{4,8},{8,12},{12,0},{1,5},{5,9},{9,13},{13,1},{2,6},{6,10},{... | collective-permute-start | bytes 393224 | tf_op jit(solution)/shard_map/ppermute | solution.py:174
  34.1 5.6 %collective-permute-start.9 = (f16[32,2048]{1,0:T(8,128)(2,1)S(1)}, f16[32,2048]{1,0:T(8,128)(2,1)S(1)}, u32[]{:S(2)}, u32[]{:S(2)}) collective-permute-start(f16[32,2048]{1,0:T(8,128)(2,1)S(1)} %get-tuple-element.60), channel_id=1, source_target_pairs={{0,12},{4,0},{8,4},{12,8},{1,13},{5,1},{9,5},{13,9},{2,14},{6,2},{... | collective-permute-start | bytes 393224 | tf_op jit(solution)/shard_map/ppermute | solution.py:174
  44.7 13.5 %all-to-all-start.1 = ((f16[8,4,4096]{2,1,0:T(4,128)(2,1)}), f16[8,4,4096]{2,1,0:T(4,128)(2,1)S(1)}, u32[]{:S(2)}, u32[]{:S(2)}) async-start(f16[8,4,4096]{2,1,0:T(4,128)(2,1)} %pad_maximum_fusion.1), calls=%async_computation.1 | async-start | bytes 524288 | tf_op jit(solution)/shard_map/all_to_all | solution.py:220
  60.3 24.9 %all-to-all-start.2 = ((f32[256,1,128]{2,1,0:T(1,128)}), f32[256,1,128]{2,1,0:T(1,128)S(1)}, u32[]{:S(2)}, u32[]{:S(2)}) async-start(f32[256,1,128]{2,1,0:T(1,128)} %broadcast_in_dim.34), calls=%async_computation.2 | async-start | bytes 262144 | tf_op jit(solution)/shard_map/all_to_all | solution.py:227
  69.2 12.4 %collective-permute-start.11 = (f32[4,4096]{1,0:T(4,128)S(1)}, f32[4,4096]{1,0:T(4,128)S(1)}, u32[]{:S(2)}, u32[]{:S(2)}) collective-permute-start(f32[4,4096]{1,0:T(4,128)S(1)} %broadcast_multiply_fusion), channel_id=1, source_target_pairs={{0,16},{16,32},{32,48},{48,64},{64,80},{80,96},{96,112},{112,0},{1... | collective-permute-start | bytes 196616 | tf_op jit(solution)/shard_map/ppermute | solution.py:174
  71.0 13.4 %collective-permute-start.12 = (f32[4,4096]{1,0:T(4,128)S(1)}, f32[4,4096]{1,0:T(4,128)S(1)}, u32[]{:S(2)}, u32[]{:S(2)}) collective-permute-start(f32[4,4096]{1,0:T(4,128)S(1)} %broadcast_multiply_fusion), channel_id=1, source_target_pairs={{0,32},{16,48},{32,64},{48,80},{64,96},{80,112},{96,0},{112,16},{1... | collective-permute-start | bytes 196616 | tf_op jit(solution)/shard_map/ppermute | solution.py:174
  73.6 13.3 %collective-permute-start.13 = (f32[4,4096]{1,0:T(4,128)S(1)}, f32[4,4096]{1,0:T(4,128)S(1)}, u32[]{:S(2)}, u32[]{:S(2)}) collective-permute-start(f32[4,4096]{1,0:T(4,128)S(1)} %broadcast_multiply_fusion), channel_id=1, source_target_pairs={{0,48},{16,64},{32,80},{48,96},{64,112},{80,0},{96,16},{112,32},{1... | collective-permute-start | bytes 196616 | tf_op jit(solution)/shard_map/ppermute | solution.py:174
  76.9 10.0 %collective-permute-start.14 = (f32[4,4096]{1,0:T(4,128)S(1)}, f32[4,4096]{1,0:T(4,128)S(1)}, u32[]{:S(2)}, u32[]{:S(2)}) collective-permute-start(f32[4,4096]{1,0:T(4,128)S(1)} %broadcast_multiply_fusion), channel_id=1, source_target_pairs={{0,64},{16,80},{32,96},{48,112},{64,0},{80,16},{96,32},{112,48},{1... | collective-permute-start | bytes 196616 | tf_op jit(solution)/shard_map/ppermute | solution.py:174
  77.9 9.9 %collective-permute-start.15 = (f32[4,4096]{1,0:T(4,128)S(1)}, f32[4,4096]{1,0:T(4,128)S(1)}, u32[]{:S(2)}, u32[]{:S(2)}) collective-permute-start(f32[4,4096]{1,0:T(4,128)S(1)} %broadcast_multiply_fusion), channel_id=1, source_target_pairs={{0,80},{16,96},{32,112},{48,0},{64,16},{80,32},{96,48},{112,64},{1... | collective-permute-start | bytes 196616 | tf_op jit(solution)/shard_map/ppermute | solution.py:174
  81.6 10.0 %collective-permute-start.16 = (f32[4,4096]{1,0:T(4,128)S(1)}, f32[4,4096]{1,0:T(4,128)S(1)}, u32[]{:S(2)}, u32[]{:S(2)}) collective-permute-start(f32[4,4096]{1,0:T(4,128)S(1)} %broadcast_multiply_fusion), channel_id=1, source_target_pairs={{0,96},{16,112},{32,0},{48,16},{64,32},{80,48},{96,64},{112,80},{1... | collective-permute-start | bytes 196616 | tf_op jit(solution)/shard_map/ppermute | solution.py:174
  84.4 7.3 %collective-permute-start.17 = (f32[4,4096]{1,0:T(4,128)S(1)}, f32[4,4096]{1,0:T(4,128)S(1)}, u32[]{:S(2)}, u32[]{:S(2)}) collective-permute-start(f32[4,4096]{1,0:T(4,128)S(1)} %broadcast_multiply_fusion), channel_id=1, source_target_pairs={{0,112},{16,0},{32,16},{48,32},{64,48},{80,64},{96,80},{112,96},{1... | collective-permute-start | bytes 196616 | tf_op jit(solution)/shard_map/ppermute | solution.py:174
  92.0 7.8 %collective-permute-start.22 = (bf16[32,2560]{1,0:T(8,128)(2,1)S(1)}, bf16[32,2560]{1,0:T(8,128)(2,1)S(1)}, u32[]{:S(2)}, u32[]{:S(2)}) collective-permute-start(bf16[32,2560]{1,0:T(8,128)(2,1)S(1)} %slice.48), channel_id=1, source_target_pairs={{0,4},{4,8},{8,12},{12,0},{1,5},{5,9},{9,13},{13,1},{2,6},{6,10},{... | collective-permute-start | bytes 491528 | tf_op jit(solution)/shard_map/ppermute | solution.py:174
  93.4 8.5 %collective-permute-start.23 = (bf16[32,2560]{1,0:T(8,128)(2,1)S(1)}, bf16[32,2560]{1,0:T(8,128)(2,1)S(1)}, u32[]{:S(2)}, u32[]{:S(2)}) collective-permute-start(bf16[32,2560]{1,0:T(8,128)(2,1)S(1)} %slice.48), channel_id=1, source_target_pairs={{0,8},{4,12},{8,0},{12,4},{1,9},{5,13},{9,1},{13,5},{2,10},{6,14},... | collective-permute-start | bytes 491528 | tf_op jit(solution)/shard_map/ppermute | solution.py:174
  95.9 6.0 %collective-permute-start.24 = (bf16[32,2560]{1,0:T(8,128)(2,1)S(1)}, bf16[32,2560]{1,0:T(8,128)(2,1)S(1)}, u32[]{:S(2)}, u32[]{:S(2)}) collective-permute-start(bf16[32,2560]{1,0:T(8,128)(2,1)S(1)} %slice.48), channel_id=1, source_target_pairs={{0,12},{4,0},{8,4},{12,8},{1,13},{5,1},{9,5},{13,9},{2,14},{6,2},{... | collective-permute-start | bytes 491528 | tf_op jit(solution)/shard_map/ppermute | solution.py:174
  97.1 10.7 %collective-permute-start.18 = (bf16[32,1536]{1,0:T(8,128)(2,1)S(1)}, bf16[32,1536]{1,0:T(8,128)(2,1)S(1)}, u32[]{:S(2)}, u32[]{:S(2)}) collective-permute-start(bf16[32,1536]{1,0:T(8,128)(2,1)S(1)} %slice.47), channel_id=1, source_target_pairs={{0,128},{128,0},{1,129},{129,1},{2,130},{130,2},{3,131},{131,3},{4... | collective-permute-start | bytes 294920 | tf_op jit(solution)/shard_map/ppermute | solution.py:174
  101.9 15.2 %collective-permute-start.25 = (bf16[128,2560]{1,0:T(8,128)(2,1)S(1)}, bf16[128,2560]{1,0:T(8,128)(2,1)S(1)}, u32[]{:S(2)}, u32[]{:S(2)}) collective-permute-start(bf16[128,2560]{1,0:T(8,128)(2,1)S(1)} %pad_maximum_fusion.refs_0_), channel_id=1, source_target_pairs={{0,128},{128,0},{1,129},{129,1},{2,130},{130,2},{3,131},{131,3},{4... | collective-permute-start | bytes 1966088 | tf_op jit(solution)/shard_map/ppermute | solution.py:174
  104.8 7.6 %collective-permute-start.10 = (f32[2,4096]{1,0:T(2,128)S(1)}, f32[2,4096]{1,0:T(2,128)S(1)}, u32[]{:S(2)}, u32[]{:S(2)}) collective-permute-start(f32[2,4096]{1,0:T(2,128)S(1)} %constant_dynamic-slice_fusion), channel_id=1, source_target_pairs={{0,2},{2,0},{1,3},{3,1},{4,6},{6,4},{5,7},{7,5},{8,10},{10,8},{9,1... | collective-permute-start | bytes 98312 | tf_op jit(solution)/shard_map/ppermute | solution.py:174
  107.8 19.7 %collective-permute-start.19 = (bf16[64,1536]{1,0:T(8,128)(2,1)S(1)}, bf16[64,1536]{1,0:T(8,128)(2,1)S(1)}, u32[]{:S(2)}, u32[]{:S(2)}) collective-permute-start(bf16[64,1536]{1,0:T(8,128)(2,1)S(1)} %pad_maximum_fusion.2.refs_0_), channel_id=1, source_target_pairs={{0,4},{4,8},{8,12},{12,0},{1,5},{5,9},{9,13},{13,1},{2,6},{6,10},{... | collective-permute-start | bytes 589832 | tf_op jit(solution)/shard_map/ppermute | solution.py:174
  108.9 18.7 %collective-permute-start.20 = (bf16[64,1536]{1,0:T(8,128)(2,1)S(1)}, bf16[64,1536]{1,0:T(8,128)(2,1)S(1)}, u32[]{:S(2)}, u32[]{:S(2)}) collective-permute-start(bf16[64,1536]{1,0:T(8,128)(2,1)S(1)} %pad_maximum_fusion.2.refs_0_), channel_id=1, source_target_pairs={{0,8},{4,12},{8,0},{12,4},{1,9},{5,13},{9,1},{13,5},{2,10},{6,14},... | collective-permute-start | bytes 589832 | tf_op jit(solution)/shard_map/ppermute | solution.py:174
  111.1 16.4 %collective-permute-start.21 = (bf16[64,1536]{1,0:T(8,128)(2,1)S(1)}, bf16[64,1536]{1,0:T(8,128)(2,1)S(1)}, u32[]{:S(2)}, u32[]{:S(2)}) collective-permute-start(bf16[64,1536]{1,0:T(8,128)(2,1)S(1)} %pad_maximum_fusion.2.refs_0_), channel_id=1, source_target_pairs={{0,12},{4,0},{8,4},{12,8},{1,13},{5,1},{9,5},{13,9},{2,14},{6,2},{... | collective-permute-start | bytes 589832 | tf_op jit(solution)/shard_map/ppermute | solution.py:174
  112.3 8.4 %collective-permute-start.26 = (bf16[128,2560]{1,0:T(8,128)(2,1)S(1)}, bf16[128,2560]{1,0:T(8,128)(2,1)S(1)}, u32[]{:S(2)}, u32[]{:S(2)}) collective-permute-start(bf16[128,2560]{1,0:T(8,128)(2,1)S(1)} %pad_maximum_fusion.refs_0_), channel_id=1, source_target_pairs={{0,2},{2,0},{1,3},{3,1},{4,6},{6,4},{5,7},{7,5},{8,10},{10,8},{9,1... | collective-permute-start | bytes 1966088 | tf_op jit(solution)/shard_map/ppermute | solution.py:174
  117.1 5.3 %collective-permute-start.27 = (bf16[128,2560]{1,0:T(8,128)(2,1)S(1)}, bf16[128,2560]{1,0:T(8,128)(2,1)S(1)}, u32[]{:S(2)}, u32[]{:S(2)}) collective-permute-start(bf16[128,2560]{1,0:T(8,128)(2,1)S(1)} %collective-permute-done.25.refs_1_), channel_id=1, source_target_pairs={{0,2},{2,0},{1,3},{3,1},{4,6},{6,4},{5,7},{7,5},{8,10},{10,8},{9,1... | collective-permute-start | bytes 1966088 | tf_op jit(solution)/shard_map/ppermute | solution.py:174
  120.7 8.6 %collective-permute-start.28 = (bf16[64,1536]{1,0:T(8,128)(2,1)S(1)}, bf16[64,1536]{1,0:T(8,128)(2,1)S(1)}, u32[]{:S(2)}, u32[]{:S(2)}) collective-permute-start(bf16[64,1536]{1,0:T(8,128)(2,1)S(1)} %pad_maximum_fusion.2.refs_0_), channel_id=1, source_target_pairs={{0,2},{2,0},{1,3},{3,1},{4,6},{6,4},{5,7},{7,5},{8,10},{10,8},{9,1... | collective-permute-start | bytes 589832 | tf_op jit(solution)/shard_map/ppermute | solution.py:174
  127.5 1.7 %collective-permute-start.29 = (bf16[64,1536]{1,0:T(8,128)(2,1)S(1)}, bf16[64,1536]{1,0:T(8,128)(2,1)S(1)}, u32[]{:S(2)}, u32[]{:S(2)}) collective-permute-start(bf16[64,1536]{1,0:T(8,128)(2,1)S(1)} %collective-permute-done.19.refs_1_), channel_id=1, source_target_pairs={{0,2},{2,0},{1,3},{3,1},{4,6},{6,4},{5,7},{7,5},{8,10},{10,8},{9,1... | collective-permute-start | bytes 589832 | tf_op jit(solution)/shard_map/ppermute | solution.py:174
  128.0 1.4 %collective-permute-start.30 = (bf16[64,1536]{1,0:T(8,128)(2,1)S(1)}, bf16[64,1536]{1,0:T(8,128)(2,1)S(1)}, u32[]{:S(2)}, u32[]{:S(2)}) collective-permute-start(bf16[64,1536]{1,0:T(8,128)(2,1)S(1)} %collective-permute-done.20.refs_2_), channel_id=1, source_target_pairs={{0,2},{2,0},{1,3},{3,1},{4,6},{6,4},{5,7},{7,5},{8,10},{10,8},{9,1... | collective-permute-start | bytes 589832 | tf_op jit(solution)/shard_map/ppermute | solution.py:174
  128.1 1.6 %collective-permute-start.31 = (bf16[64,1536]{1,0:T(8,128)(2,1)S(1)}, bf16[64,1536]{1,0:T(8,128)(2,1)S(1)}, u32[]{:S(2)}, u32[]{:S(2)}) collective-permute-start(bf16[64,1536]{1,0:T(8,128)(2,1)S(1)} %collective-permute-done.21.refs_3_), channel_id=1, source_target_pairs={{0,2},{2,0},{1,3},{3,1},{4,6},{6,4},{5,7},{7,5},{8,10},{10,8},{9,1... | collective-permute-start | bytes 589832 | tf_op jit(solution)/shard_map/ppermute | solution.py:174
